TPU v7x, 32 devices: a whole 2x2x4 slice. The times are simulated.
32 devices in a mesh: epoch: 4 (over y, x), blend: 8 (over z, core).
Axes of the slice: x: 2, y: 2, z: 4, core: 2. Of those that a mesh axis runs over, the one named last changes fastest.
Arguments:
- visit_flux: bfloat16 [16, 32, 6, 16384], P('epoch', None, None, 'blend'), may hold values from -6 to 6
- visit_precision: bfloat16 [16, 32, 6, 16384], P('epoch', None, None, 'blend'), may hold values from 0.25 to 4
- visit_live: int32 [16, 32], P('epoch'), may hold values 0 or 1
- footprint: int32 [32, 8, 16384], P('blend', None, 'epoch'), may hold values 0 or 1
- source_count: int32 [32], P('blend'), may hold values from 1 to 8
- spectra_init: float32 [32, 8, 6], P('blend'), may hold values from 0.2 to 1.2
- morphology_init: float32 [32, 8, 16384], P('blend', None, 'epoch'), may hold values from 0 to 0.25
Outputs:
- coadd_flux: float32 [32, 6, 16384], P('blend', None, 'epoch')
- spectra: float32 [32, 8, 6], P('blend')
- morphology: float32 [32, 8, 16384], P('blend', None, 'epoch')
All inputs are finite; a program needn't handle non-finite values. No bound on the sum of `visit_live` or of `footprint` on one device may be relied on, other than what follows from the above.
Results may differ from a plain program's by a relative error of at most 0.0003.
Values sent between devices are 32-bit elements; how exact they have to be, the bound alone decides.
No kernel may reach another device: no remote copies, remote signals or barrier semaphores. Data moves between devices by JAX's collectives and lax.ppermute only.
A program may use at most 64 MiB of HBM per device.

v0:
```python
import jax
import jax.numpy as jnp
from jax import lax
from jax.experimental import pallas as pl
from jax.experimental.pallas import tpu as pltpu
from jax.sharding import PartitionSpec as P


ITERS = 2
LANES = 128


def on_device_general(
    visit_flux, visit_precision, visit_live, footprint, source_count, spectra_init, morphology_init
):
    weights = visit_precision.astype(jnp.float32) * visit_live.astype(jnp.float32)[:, :, None, None]
    numerator = jnp.sum(weights * visit_flux.astype(jnp.float32), axis=0)
    weight_sum = jnp.sum(weights, axis=0)
    pix_part = morphology_init.shape[2]
    owned = morphology_init.shape[0]
    numerator, weight_sum = (
        lax.psum_scatter(numerator, "epoch", scatter_dimension=2, tiled=True),
        lax.psum_scatter(weight_sum, "epoch", scatter_dimension=2, tiled=True),
    )
    every_blend, band_count, piece = numerator.shape
    numerator = numerator.reshape(every_blend, band_count, 1, piece)
    weight_sum = weight_sum.reshape(every_blend, band_count, 1, piece)
    numerator, weight_sum = (
        lax.all_to_all(numerator, "blend", split_axis=0, concat_axis=2, tiled=True),
        lax.all_to_all(weight_sum, "blend", split_axis=0, concat_axis=2, tiled=True),
    )
    blocks = numerator.shape[2]
    numerator = numerator.reshape(owned, band_count, blocks, 1, piece)
    weight_sum = weight_sum.reshape(owned, band_count, blocks, 1, piece)
    numerator, weight_sum = (
        lax.all_to_all(numerator, "epoch", split_axis=2, concat_axis=3, tiled=True),
        lax.all_to_all(weight_sum, "epoch", split_axis=2, concat_axis=3, tiled=True),
    )
    numerator = numerator.reshape(owned, band_count, pix_part)
    weight_sum = weight_sum.reshape(owned, band_count, pix_part)
    coadd_flux = numerator / (1.0 + weight_sum)
    coverage = weight_sum / (1.0 + weight_sum)
    slots = footprint.shape[1]
    source_live = (jnp.arange(slots, dtype=jnp.int32)[None, :] < source_count[:, None]).astype(
        jnp.float32
    )
    footprint_mask = footprint.astype(jnp.float32) * source_live[:, :, None]
    live_count = source_count.astype(jnp.float32)
    morphology = morphology_init * footprint_mask
    spectra = spectra_init
    highest = lax.Precision.HIGHEST
    for _ in range(ITERS):
        blend_model = jnp.einsum("bkc,bkp->bcp", spectra, morphology, precision=highest)
        residual = coverage * (coadd_flux - blend_model)
        morph_grad = jnp.einsum("bkc,bcp->bkp", spectra, residual, precision=highest)
        morph_step = 1.0 / (1.0 + live_count[:, None] * jnp.sum(spectra * spectra, axis=2))
        morphology = (
            jnp.maximum(0.0, morphology + morph_grad * morph_step[:, :, None]) * footprint_mask
        )
        blend_model = jnp.einsum("bkc,bkp->bcp", spectra, morphology, precision=highest)
        residual = coverage * (coadd_flux - blend_model)
        spectra_grad = jnp.einsum("bkp,bcp->bkc", morphology, residual, precision=highest)
        morph_norm = jnp.sum(morphology * morphology, axis=2)
        spectra_grad, morph_norm = lax.psum((spectra_grad, morph_norm), "epoch")
        spectra = jnp.maximum(
            0.0, spectra + spectra_grad / (1.0 + live_count[:, None] * morph_norm)[:, :, None]
        )
    return (coadd_flux, spectra, morphology)


VMEM_LIMIT = 8 * 1024 * 1024


def hbm(x):
    return pltpu.with_memory_space_constraint(x, pltpu.HBM)


def whole():
    return pl.BlockSpec(memory_space=pltpu.VMEM)


def in_place():
    return pl.BlockSpec(memory_space=pltpu.HBM)


def cost(flops, nbytes):
    return pl.CostEstimate(flops=int(flops), bytes_accessed=int(nbytes), transcendentals=0)


def params(limit=VMEM_LIMIT):
    return pltpu.CompilerParams(vmem_limit_bytes=limit)


def visit_sums(flux, prec, live, ks, owned, n_e, cores):
    epochs, bands, blends, pix = flux.shape
    group = cores * owned
    rows = pix // LANES
    block_rows = 2 * bands * rows
    half = n_e // 2
    n_k = len(ks)
    order = {0: ((1, 3), (0, 2)), 1: ((2, 3), (0, 1))}

    def kernel(live_ref, flux_ref, prec_ref, s0, k0, s1, k1, scr, fbuf, pbuf, sems):
        e, b = lax.axis_index("epoch"), lax.axis_index("blend")
        chip, c = b // cores, b % cores

        def copies(i, band):
            at = pl.ds(pl.multiple_of((chip ^ ks[i]) * group, 8), group)
            return [
                pltpu.make_async_copy(ref.at[:, band, at, :], buf.at[i, band], sems.at[i, band, n])
                for n, (ref, buf) in enumerate(((flux_ref, fbuf), (prec_ref, pbuf)))
            ]

        for i in range(n_k):
            for band in range(bands):
                for copy in copies(i, band):
                    copy.start()
        sub = lax.broadcasted_iota(jnp.int32, (group, blends), 0)
        lane = lax.broadcasted_iota(jnp.int32, (group, blends), 1)
        for i in range(n_k):
            pick = lane == sub + (chip ^ ks[i]) * group
            lives = []
            for ep in range(epochs):
                row = live_ref[ep : ep + 1, :].astype(jnp.float32)
                col = jnp.where(pick, jnp.broadcast_to(row, pick.shape), 0.0)
                lives.append(jnp.broadcast_to(jnp.sum(col, axis=1, keepdims=True), (group, LANES)))
            for band in range(bands):
                for copy in copies(i, band):
                    copy.wait()
                for j in range(rows):
                    at = pl.ds(j * LANES, LANES)
                    num = wsum = None
                    for ep in range(epochs):
                        w = pbuf[i, band, ep, :, at].astype(jnp.float32) * lives[ep]
                        n = w * fbuf[i, band, ep, :, at].astype(jnp.float32)
                        num = n if num is None else num + n
                        wsum = w if wsum is None else wsum + w
                    scr[pl.ds(band * rows + j, group, stride=block_rows), :] = num
                    scr[pl.ds((bands + band) * rows + j, group, stride=block_rows), :] = wsum
            for d, refs in ((0, (s0, k0)), (1, (s1, k1))):
                for ref, slots in zip(refs, order[d]):
                    for slot, p in enumerate(slots):
                        r = jnp.bitwise_xor(c, d) * n_e + jnp.bitwise_xor(e, p)
                        start = pl.multiple_of(r * block_rows, 8)
                        ref[slot, i] = scr[pl.ds(start, block_rows), :].reshape(2 * bands, rows, LANES)

    out = pltpu.VMEM((half, n_k, 2 * bands, rows, LANES), jnp.float32)
    n_in = n_k * epochs * bands * group * pix
    return pl.pallas_call(
        kernel,
        in_specs=[whole(), in_place(), in_place()],
        out_specs=[whole()] * 4,
        out_shape=[out] * 4,
        scratch_shapes=[
            pltpu.VMEM((group * block_rows, LANES), jnp.float32),
            pltpu.VMEM((n_k, bands, epochs, group, pix), flux.dtype),
            pltpu.VMEM((n_k, bands, epochs, group, pix), prec.dtype),
            pltpu.SemaphoreType.DMA((n_k, bands, 2)),
        ],
        compiler_params=params(),
        cost_estimate=cost(n_in * 6, n_in * 4 + n_in * 2),
        name="visit_sums",
    )(live, flux, prec)


def pack_kernel(morph, footprint, n_e):
    _, slots, lanes = morph.shape

    def kernel(morph_ref, foot_ref, *refs):
        outs, buf, sems = refs[:n_e], refs[n_e], refs[n_e + 1]
        e = lax.axis_index("epoch")
        copies = []
        for p in range(n_e):
            q = jnp.bitwise_xor(e, p)
            copies.append(
                (
                    pltpu.make_async_copy(morph_ref.at[q], outs[p].at[0], sems.at[p, 0]),
                    pltpu.make_async_copy(foot_ref.at[q], buf.at[p], sems.at[p, 1]),
                )
            )
        for pair in copies:
            for copy in pair:
                copy.start()
        for p, pair in enumerate(copies):
            for copy in pair:
                copy.wait()
            outs[p][1] = buf[p].astype(jnp.float32)

    n = n_e * slots * lanes
    return pl.pallas_call(
        kernel,
        in_specs=[in_place()] * 2,
        out_specs=[whole()] * n_e,
        out_shape=[pltpu.VMEM((2, slots, lanes), jnp.float32)] * n_e,
        scratch_shapes=[
            pltpu.VMEM((n_e, slots, lanes), footprint.dtype),
            pltpu.SemaphoreType.DMA((n_e, 2)),
        ],
        compiler_params=params(),
        cost_estimate=cost(n * 2, n * 16),
        name="pack",
    )(morph, footprint)


def coadd_kernel(pieces, bands, n_e):
    n_b = len(pieces)
    rows = pieces[0].shape[1]
    total = n_b * rows
    per_e = total // n_e

    def kernel(*refs):
        ins, cov, outs, scr = refs[:n_b], refs[n_b], refs[n_b + 1 : n_b + 1 + n_e], refs[-1]
        e, b = lax.axis_index("epoch"), lax.axis_index("blend")
        for m in range(n_b):
            start = pl.multiple_of(jnp.bitwise_xor(b, m) * rows, 8)
            for band in range(bands):
                num, wsum = ins[m][band], ins[m][bands + band]
                inv = 1.0 / (1.0 + wsum)
                cov[band, pl.ds(start, rows), :] = wsum * inv
                scr[band, pl.ds(start, rows), :] = num * inv
        for p in range(n_e):
            start = pl.multiple_of(jnp.bitwise_xor(e, p) * per_e, 8)
            for band in range(bands):
                outs[p][band] = scr[band, pl.ds(start, per_e), :]

    return pl.pallas_call(
        kernel,
        in_specs=[whole()] * n_b,
        out_specs=[whole()] * (1 + n_e),
        out_shape=[jax.ShapeDtypeStruct((bands, total, LANES), jnp.float32)]
        + [jax.ShapeDtypeStruct((bands, per_e, LANES), jnp.float32)] * n_e,
        scratch_shapes=[pltpu.VMEM((bands, total, LANES), jnp.float32)],
        compiler_params=params(),
        cost_estimate=cost(bands * total * LANES * 8, bands * total * LANES * 16),
        name="coadd",
    )(*pieces)


def deblend_kernel(counts, cov, coadds, packed, spectra):
    n_e = len(coadds)
    bands, total, _ = cov.shape
    _, slots, lanes = packed[0].shape
    per_e = lanes // LANES
    groups = total // 8

    def kernel(count_ref, cov_ref, *refs):
        co_in, pk_in = refs[:n_e], refs[n_e : 2 * n_e]
        spec_ref = refs[2 * n_e]
        outs = refs[2 * n_e + 1 : 3 * n_e + 1]
        co, mo, ma, res, acc, spec, step = refs[3 * n_e + 1 :]
        e = lax.axis_index("epoch")
        count = count_ref[e]
        n_live = count.astype(jnp.float32)
        k_iota = lax.broadcasted_iota(jnp.int32, (slots, LANES), 0)
        live = (k_iota < count).astype(jnp.float32)
        for p in range(n_e):
            start = jnp.bitwise_xor(e, p) * per_e
            for band in range(bands):
                co[band, pl.ds(pl.multiple_of(start, 8), per_e), :] = co_in[p][band]
            for j in range(per_e):
                at = pl.ds(j * LANES, LANES)
                mask = pk_in[p][1, :, at] * live
                ma[pl.ds(start + j, slots, stride=total), :] = mask
                mo[pl.ds(start + j, slots, stride=total), :] = pk_in[p][0, :, at] * mask
        spec[...] = spec_ref[...]

        def bcast(ref, row):
            return jnp.broadcast_to(ref[pl.ds(row, 1), :], (8, LANES))

        for _ in range(ITERS):
            square = None
            for band in range(bands):
                s = spec[pl.ds(band * slots, slots), :]
                square = s * s if square is None else square + s * s
            step[...] = 1.0 / (1.0 + n_live * square)

            def group(g, carry):
                at = pl.multiple_of(g * 8, 8)
                m = [mo[pl.ds(pl.multiple_of(k * total + at, 8), 8), :] for k in range(slots)]
                cv = [cov_ref[c, pl.ds(at, 8), :] for c in range(bands)]
                cd = [co[c, pl.ds(at, 8), :] for c in range(bands)]
                r = []
                for c in range(bands):
                    model = None
                    for k in range(slots):
                        t = bcast(spec, c * slots + k) * m[k]
                        model = t if model is None else model + t
                    r.append(cv[c] * (cd[c] - model))
                for k in range(slots):
                    grad = None
                    for c in range(bands):
                        t = bcast(spec, c * slots + k) * r[c]
                        grad = t if grad is None else grad + t
                    mk = ma[pl.ds(pl.multiple_of(k * total + at, 8), 8), :]
                    m[k] = jnp.maximum(0.0, m[k] + grad * bcast(step, k)) * mk
                    mo[pl.ds(pl.multiple_of(k * total + at, 8), 8), :] = m[k]
                for c in range(bands):
                    model = None
                    for k in range(slots):
                        t = bcast(spec, c * slots + k) * m[k]
                        model = t if model is None else model + t
                    res[c, pl.ds(at, 8), :] = cv[c] * (cd[c] - model)
                return carry

            lax.fori_loop(0, groups, group, 0)
            for k in range(slots):
                sums = [None] * (bands + 1)
                for g in range(groups):
                    m = mo[pl.ds(k * total + g * 8, 8), :]
                    for c in range(bands):
                        t = m * res[c, pl.ds(g * 8, 8), :]
                        sums[c] = t if sums[c] is None else sums[c] + t
                    t = m * m
                    sums[bands] = t if sums[bands] is None else sums[bands] + t
                for c in range(bands + 1):
                    acc[pl.ds((c * slots + k) * 8, 8), :] = sums[c]

            def reduced(c):
                v = None
                for s in range(8):
                    t = acc[pl.ds(c * slots * 8 + s, slots, stride=8), :]
                    v = t if v is None else v + t
                return jnp.broadcast_to(jnp.sum(v, axis=1, keepdims=True), (slots, LANES))

            den = 1.0 + n_live * reduced(bands)
            for c in range(bands):
                s = spec[pl.ds(c * slots, slots), :]
                spec[pl.ds(c * slots, slots), :] = jnp.maximum(0.0, s + reduced(c) / den)

        lane = lax.broadcasted_iota(jnp.int32, (slots, LANES), 1)
        tile = jnp.zeros((slots, LANES), jnp.float32)
        for c in range(bands):
            on_diag = jnp.where(lane == k_iota, spec[pl.ds(c * slots, slots), :], 0.0)
            row = jnp.broadcast_to(jnp.sum(on_diag, axis=0, keepdims=True), (slots, LANES))
            tile = jnp.where(k_iota == c, row, tile)
        for p in range(n_e):
            start = jnp.bitwise_xor(e, p) * per_e
            for j in range(per_e):
                outs[p][:, pl.ds(j * LANES, LANES)] = mo[pl.ds(start + j, slots, stride=total), :]
            outs[p][:, pl.ds(lanes, LANES)] = tile

    f32 = jnp.float32
    return pl.pallas_call(
        kernel,
        in_specs=[pl.BlockSpec(memory_space=pltpu.SMEM)] + [whole()] * (2 * n_e + 2),
        out_specs=[whole()] * n_e,
        out_shape=[jax.ShapeDtypeStruct((slots, lanes + LANES), f32)] * n_e,
        scratch_shapes=[
            pltpu.VMEM((bands, total, LANES), f32),
            pltpu.VMEM((slots * total, LANES), f32),
            pltpu.VMEM((slots * total, LANES), f32),
            pltpu.VMEM((bands, total, LANES), f32),
            pltpu.VMEM(((bands + 1) * slots * 8, LANES), f32),
            pltpu.VMEM((bands * slots, LANES), f32),
            pltpu.VMEM((slots, LANES), f32),
        ],
        compiler_params=params(),
        cost_estimate=cost(total * LANES * slots * bands * 8 * ITERS, total * LANES * 4 * 30),
        name="deblend",
    )(counts, cov, *coadds, *packed, spectra)


def place_coadd(pieces):
    n_e = len(pieces)
    bands, rows, _ = pieces[0].shape

    def kernel(*refs):
        ins, out, scr = refs[:n_e], refs[n_e], refs[n_e + 1]
        e = lax.axis_index("epoch")
        for p in range(n_e):
            scr[jnp.bitwise_xor(e, p)] = ins[p][...].reshape(bands * rows, LANES)
        for band in range(bands):
            for j in range(rows):
                for q in range(n_e):
                    out[band, q : q + 1, pl.ds(j * LANES, LANES)] = scr[q, pl.ds(band * rows + j, 1), :]

    return pl.pallas_call(
        kernel,
        in_specs=[whole()] * n_e,
        out_specs=whole(),
        out_shape=jax.ShapeDtypeStruct((bands, n_e, rows * LANES), jnp.float32),
        scratch_shapes=[pltpu.VMEM((n_e, bands * rows, LANES), jnp.float32)],
        compiler_params=params(),
        cost_estimate=cost(bands * n_e * rows * LANES, bands * n_e * rows * LANES * 8),
        name="place_coadd",
    )(*pieces)


def place_morph(pieces, bands):
    n_e = len(pieces)
    slots, lanes = pieces[0].shape
    lanes -= LANES

    def kernel(*refs):
        ins, out, spec, scr = refs[:n_e], refs[n_e], refs[n_e + 1], refs[n_e + 2]
        e = lax.axis_index("epoch")
        for p in range(n_e):
            q = jnp.bitwise_xor(e, p)
            out[q] = ins[p][:, 0:lanes]
            scr[q] = ins[p][:, lanes : lanes + LANES]
        for c in range(bands):
            for q in range(n_e):
                spec[c, q : q + 1, :] = scr[q, pl.ds(c, 1), 0:slots]

    return pl.pallas_call(
        kernel,
        in_specs=[whole()] * n_e,
        out_specs=[whole()] * 2,
        out_shape=[
            jax.ShapeDtypeStruct((n_e, slots, lanes), jnp.float32),
            jax.ShapeDtypeStruct((bands, n_e, slots), jnp.float32),
        ],
        scratch_shapes=[pltpu.VMEM((n_e, slots, LANES), jnp.float32)],
        compiler_params=params(),
        cost_estimate=cost(n_e * slots * lanes, n_e * slots * lanes * 8),
        name="place_morph",
    )(*pieces)


def xor_permute(x, axis, size, mask):
    return lax.ppermute(x, axis, [(i, i ^ mask) for i in range(size)])


def on_device_blend(
    n_e, n_b, visit_flux, visit_precision, visit_live, footprint, source_count, spectra_init, morphology_init
):
    owned, slots, _ = morphology_init.shape
    bands = visit_flux.shape[2]
    cores = 2
    e = lax.axis_index("epoch")
    flux = hbm(jnp.transpose(visit_flux, (0, 2, 1, 3)))
    prec = hbm(jnp.transpose(visit_precision, (0, 2, 1, 3)))

    def swap(xs):
        out = [xs[0]]
        for p in range(1, n_e):
            out.append(xor_permute(xs[p], "epoch", n_e, p))
        return out

    spectra = lax.dynamic_index_in_dim(spectra_init, e, 0, keepdims=False)
    spectra = jnp.transpose(spectra).reshape(bands * slots, 1)
    spectra = jnp.broadcast_to(spectra, (bands * slots, LANES))

    chips = n_b // cores
    chunks = [[k] for k in range(chips - 1, 1, -1)] + [[1, 0] if chips > 1 else [0]]
    pieces = [None] * n_b
    for ks in chunks:
        s0, k0, s1, k1 = visit_sums(flux, prec, visit_live, ks, owned, n_e, cores)
        for d, (send, keep, first, second) in enumerate(((s0, k0, 1, 2), (s1, k1, 2, 1))):
            got = xor_permute(send, "epoch", n_e, first)
            onward = xor_permute(keep[1] + got[1], "epoch", n_e, second)
            full = keep[0] + got[0] + onward
            for i, k in enumerate(ks):
                m = k * cores + d
                pieces[m] = xor_permute(full[i], "blend", n_b, m) if m else full[i]
    packed = pack_kernel(hbm(morphology_init), hbm(footprint), n_e)
    packed = swap(packed)
    cov, *coadds = coadd_kernel(pieces, bands, n_e)
    blocks = deblend_kernel(source_count, cov, coadds, packed, spectra)
    out_coadd = place_coadd(swap(coadds))
    out_morph, out_spec = place_morph(swap(blocks), bands)
    return (jnp.transpose(out_coadd, (1, 0, 2)), jnp.transpose(out_spec, (1, 2, 0)), out_morph)


def solution(mesh):
    n_e, n_b = mesh.shape["epoch"], mesh.shape["blend"]
    in_specs = (
        P("epoch", None, None, "blend"),
        P("epoch", None, None, "blend"),
        P("epoch", None),
        P("blend", None, "epoch"),
        P("blend"),
        P("blend", None, None),
        P("blend", None, "epoch"),
    )
    out_specs = (P("blend", None, "epoch"), P("blend", None, None), P("blend", None, "epoch"))

    def on_device(*args):
        owned, slots, pix_part = args[6].shape
        pix = args[0].shape[3]
        by_blend = (
            n_e == 4
            and owned == n_e
            and slots == 8
            and n_b % 2 == 0
            and n_b & (n_b - 1) == 0
            and pix % (8 * LANES) == 0
            and pix_part % pix == 0
            and pix_part % (8 * LANES) == 0
        )
        if by_blend:
            return on_device_blend(n_e, n_b, *args)
        return on_device_general(*args)

    return jax.shard_map(
        on_device, mesh=mesh, in_specs=in_specs, out_specs=out_specs, check_vma=False
    )
```

profile of v0, /device:TPU:0, one launch (start us, length us, event | category | flops | bytes accessed | tf_op | source)
XLA Modules:
  0.0 105.9 jit_solution(16547767595093798294)
XLA Ops:
  0.6 0.0 copy-start
  0.7 0.7 copy-done.1
  1.3 1.8 %visit_sums.4 = (f32[2,1,12,16,128]{4,3,2,1,0:T(8,128)S(1)}, f32[2,1,12,16,128]{4,3,2,1,0:T(8,128)S(1)}, f32[2,1,12,16,128]{4,3,2,1,0:T(8,128)S(1)}, f32[2,1,12,16,128]{4,3,2,1,0:T(8,128)S(1)}) custom-call(s32[4,32]{1,0:T(4,128)S(1)} %copy-done.1, bf16[4,6,32,2048]{3,2,1,0:T(8,128)(2,1)} %bitcast.70, bf16[4,6,32,2048]{3,2,1,0:T(8,128)(2,1)} %bitcast.73), custom_call_target="tpu_custom_call" | custom-call | flops 2359296 | bytes 2359296 | tf_op jit(solution)/shard_map/visit_sums/pallas_call | solution.py:149
  3.2 3.1 %collective-permute-start.10 = (f32[2,1,12,16,128]{4,3,2,1,0:T(8,128)S(1)}, f32[2,1,12,16,128]{4,3,2,1,0:T(8,128)S(1)}, u32[]{:S(2)}, u32[]{:S(2)}) collective-permute-start(f32[2,1,12,16,128]{4,3,2,1,0:T(8,128)S(1)} %get-tuple-element.37), channel_id=1, source_target_pairs={{0,16},{8,24},{16,0},{24,8},{1,17},{9,25},{17,1},{25,9},{2,18},{10... | collective-permute-start | bytes 589832 | tf_op jit(solution)/shard_map/ppermute | solution.py:421
  6.2 2.7 %visit_sums.3 = (f32[2,2,12,16,128]{4,3,2,1,0:T(8,128)S(1)}, f32[2,2,12,16,128]{4,3,2,1,0:T(8,128)S(1)}, f32[2,2,12,16,128]{4,3,2,1,0:T(8,128)S(1)}, f32[2,2,12,16,128]{4,3,2,1,0:T(8,128)S(1)}) custom-call(s32[4,32]{1,0:T(4,128)S(1)} %copy-done.1, bf16[4,6,32,2048]{3,2,1,0:T(8,128)(2,1)} %bitcast.71, bf16[4,6,32,2048]{3,2,1,0:T(8,128)(2,1)} %bitcast.74), custom_call_target="tpu_custom_call" | custom-call | flops 4718592 | bytes 4718592 | tf_op jit(solution)/shard_map/visit_sums/pallas_call | solution.py:149
  9.0 0.1 collective-permute-start.2
  9.1 2.0 %collective-permute-start = (f32[2,2,12,16,128]{4,3,2,1,0:T(8,128)S(1)}, f32[2,2,12,16,128]{4,3,2,1,0:T(8,128)S(1)}, u32[]{:S(2)}, u32[]{:S(2)}) collective-permute-start(f32[2,2,12,16,128]{4,3,2,1,0:T(8,128)S(1)} %get-tuple-element.31), channel_id=1, source_target_pairs={{0,8},{8,0},{16,24},{24,16},{1,9},{9,1},{17,25},{25,17},{2,10},{10... | collective-permute-start | bytes 1179656 | tf_op jit(solution)/shard_map/ppermute | solution.py:421
  11.0 1.8 %visit_sums.5 = (f32[2,1,12,16,128]{4,3,2,1,0:T(8,128)S(1)}, f32[2,1,12,16,128]{4,3,2,1,0:T(8,128)S(1)}, f32[2,1,12,16,128]{4,3,2,1,0:T(8,128)S(1)}, f32[2,1,12,16,128]{4,3,2,1,0:T(8,128)S(1)}) custom-call(s32[4,32]{1,0:T(4,128)S(1)} %copy-done.1, bf16[4,6,32,2048]{3,2,1,0:T(8,128)(2,1)} %bitcast.72, bf16[4,6,32,2048]{3,2,1,0:T(8,128)(2,1)} %bitcast.75), custom_call_target="tpu_custom_call" | custom-call | flops 2359296 | bytes 2359296 | tf_op jit(solution)/shard_map/visit_sums/pallas_call | solution.py:149
  12.9 0.2 collective-permute-start.13
  13.1 1.9 %collective-permute-start.16 = (f32[2,1,12,16,128]{4,3,2,1,0:T(8,128)S(1)}, f32[2,1,12,16,128]{4,3,2,1,0:T(8,128)S(1)}, u32[]{:S(2)}, u32[]{:S(2)}) collective-permute-start(f32[2,1,12,16,128]{4,3,2,1,0:T(8,128)S(1)} %get-tuple-element.41), channel_id=1, source_target_pairs={{0,16},{8,24},{16,0},{24,8},{1,17},{9,25},{17,1},{25,9},{2,18},{10... | collective-permute-start | bytes 589832 | tf_op jit(solution)/shard_map/ppermute | solution.py:421
  15.0 1.4 %pack.1 = (f32[2,8,4096]{2,1,0:T(8,128)S(1)}, f32[2,8,4096]{2,1,0:T(8,128)S(1)}, f32[2,8,4096]{2,1,0:T(8,128)S(1)}, f32[2,8,4096]{2,1,0:T(8,128)S(1)}) custom-call(f32[4,8,4096]{2,1,0:T(8,128)} %morph_ref.1, s32[4,8,4096]{2,1,0:T(8,128)} %foot_ref.1), custom_call_target="tpu_custom_call" | custom-call | flops 262144 | bytes 2097152 | tf_op jit(solution)/shard_map/pack/pallas_call | solution.py:190
  16.4 0.0 collective-permute-done.10
  16.4 1.6 %collective-permute-start.7 = (f32[2,1,12,16,128]{4,3,2,1,0:T(8,128)S(1)}, f32[2,1,12,16,128]{4,3,2,1,0:T(8,128)S(1)}, u32[]{:S(2)}, u32[]{:S(2)}) collective-permute-start(f32[2,1,12,16,128]{4,3,2,1,0:T(8,128)S(1)} %get-tuple-element.35), channel_id=1, source_target_pairs={{0,8},{8,0},{16,24},{24,16},{1,9},{9,1},{17,25},{25,17},{2,10},{10... | collective-permute-start | bytes 589832 | tf_op jit(solution)/shard_map/ppermute | solution.py:421
  18.0 7.4 %collective-permute-done.13 = f32[2,1,12,16,128]{4,3,2,1,0:T(8,128)S(1)} collective-permute-done((f32[2,1,12,16,128]{4,3,2,1,0:T(8,128)S(1)}, f32[2,1,12,16,128]{4,3,2,1,0:T(8,128)S(1)}, u32[]{:S(2)}, u32[]{:S(2)}) %collective-permute-start.13) | collective-permute-done | bytes 196640 | tf_op jit(solution)/shard_map/ppermute | solution.py:421
  25.3 1.9 %collective-permute-start.22 = (f32[2,8,4096]{2,1,0:T(8,128)S(1)}, f32[2,8,4096]{2,1,0:T(8,128)S(1)}, u32[]{:S(2)}, u32[]{:S(2)}) collective-permute-start(f32[2,8,4096]{2,1,0:T(8,128)S(1)} %get-tuple-element.48), channel_id=1, source_target_pairs={{0,8},{8,0},{16,24},{24,16},{1,9},{9,1},{17,25},{25,17},{2,10},{10... | collective-permute-start | bytes 786440 | tf_op jit(solution)/shard_map/ppermute | solution.py:421
  27.3 0.0 collective-permute-done.16
  27.3 1.6 %collective-permute-start.23 = (f32[2,8,4096]{2,1,0:T(8,128)S(1)}, f32[2,8,4096]{2,1,0:T(8,128)S(1)}, u32[]{:S(2)}, u32[]{:S(2)}) collective-permute-start(f32[2,8,4096]{2,1,0:T(8,128)S(1)} %get-tuple-element.49), channel_id=1, source_target_pairs={{0,16},{8,24},{16,0},{24,8},{1,17},{9,25},{17,1},{25,9},{2,18},{10... | collective-permute-start | bytes 786440 | tf_op jit(solution)/shard_map/ppermute | solution.py:421
  28.9 0.0 copy-start.2
  28.9 0.7 collective-permute-done.7
  29.5 1.9 %collective-permute-start.11 = (f32[1,12,16,128]{3,2,1,0:T(8,128)S(1)}, f32[1,12,16,128]{3,2,1,0:T(8,128)S(1)}, u32[]{:S(2)}, u32[]{:S(2)}) collective-permute-start(f32[1,12,16,128]{3,2,1,0:T(8,128)S(1)} %fusion.14), channel_id=1, source_target_pairs={{0,8},{8,0},{16,24},{24,16},{1,9},{9,1},{17,25},{25,17},{2,10},{10... | collective-permute-start | bytes 294920 | tf_op jit(solution)/shard_map/ppermute | solution.py:421
  31.5 4.4 %collective-permute-done.11 = f32[1,12,16,128]{3,2,1,0:T(8,128)S(1)} collective-permute-done((f32[1,12,16,128]{3,2,1,0:T(8,128)S(1)}, f32[1,12,16,128]{3,2,1,0:T(8,128)S(1)}, u32[]{:S(2)}, u32[]{:S(2)}) %collective-permute-start.11) | collective-permute-done | bytes 98336 | tf_op jit(solution)/shard_map/ppermute | solution.py:421
  35.9 1.7 %collective-permute-start.14 = (f32[1,12,16,128]{3,2,1,0:T(8,128)S(1)}, f32[1,12,16,128]{3,2,1,0:T(8,128)S(1)}, u32[]{:S(2)}, u32[]{:S(2)}) collective-permute-start(f32[1,12,16,128]{3,2,1,0:T(8,128)S(1)} %fusion.10), channel_id=1, source_target_pairs={{0,16},{8,24},{16,0},{24,8},{1,17},{9,25},{17,1},{25,9},{2,18},{10... | collective-permute-start | bytes 294920 | tf_op jit(solution)/shard_map/ppermute | solution.py:421
  37.5 2.9 %collective-permute-done.14 = f32[1,12,16,128]{3,2,1,0:T(8,128)S(1)} collective-permute-done((f32[1,12,16,128]{3,2,1,0:T(8,128)S(1)}, f32[1,12,16,128]{3,2,1,0:T(8,128)S(1)}, u32[]{:S(2)}, u32[]{:S(2)}) %collective-permute-start.14) | collective-permute-done | bytes 98336 | tf_op jit(solution)/shard_map/ppermute | solution.py:421
  40.5 1.6 %collective-permute-start.17 = (f32[1,12,16,128]{3,2,1,0:T(8,128)S(1)}, f32[1,12,16,128]{3,2,1,0:T(8,128)S(1)}, u32[]{:S(2)}, u32[]{:S(2)}) collective-permute-start(f32[1,12,16,128]{3,2,1,0:T(8,128)S(1)} %fusion.6), channel_id=1, source_target_pairs={{0,8},{8,0},{16,24},{24,16},{1,9},{9,1},{17,25},{25,17},{2,10},{10... | collective-permute-start | bytes 294920 | tf_op jit(solution)/shard_map/ppermute | solution.py:421
  42.1 3.0 %collective-permute-done.17 = f32[1,12,16,128]{3,2,1,0:T(8,128)S(1)} collective-permute-done((f32[1,12,16,128]{3,2,1,0:T(8,128)S(1)}, f32[1,12,16,128]{3,2,1,0:T(8,128)S(1)}, u32[]{:S(2)}, u32[]{:S(2)}) %collective-permute-start.17) | collective-permute-done | bytes 98336 | tf_op jit(solution)/shard_map/ppermute | solution.py:421
  45.1 1.7 %collective-permute-start.8 = (f32[1,12,16,128]{3,2,1,0:T(8,128)S(1)}, f32[1,12,16,128]{3,2,1,0:T(8,128)S(1)}, u32[]{:S(2)}, u32[]{:S(2)}) collective-permute-start(f32[1,12,16,128]{3,2,1,0:T(8,128)S(1)} %fusion.18), channel_id=1, source_target_pairs={{0,16},{8,24},{16,0},{24,8},{1,17},{9,25},{17,1},{25,9},{2,18},{10... | collective-permute-start | bytes 294920 | tf_op jit(solution)/shard_map/ppermute | solution.py:421
  46.8 2.9 %collective-permute-done.8 = f32[1,12,16,128]{3,2,1,0:T(8,128)S(1)} collective-permute-done((f32[1,12,16,128]{3,2,1,0:T(8,128)S(1)}, f32[1,12,16,128]{3,2,1,0:T(8,128)S(1)}, u32[]{:S(2)}, u32[]{:S(2)}) %collective-permute-start.8) | collective-permute-done | bytes 98336 | tf_op jit(solution)/shard_map/ppermute | solution.py:421
  49.7 0.0 collective-permute-start.12
  49.7 0.0 collective-permute-done.2
  49.7 3.8 %collective-permute-start.15 = (f32[12,16,128]{2,1,0:T(8,128)S(1)}, f32[12,16,128]{2,1,0:T(8,128)S(1)}, u32[]{:S(2)}, u32[]{:S(2)}) collective-permute-start(f32[12,16,128]{2,1,0:T(8,128)S(1)} %fusion.13), channel_id=1, source_target_pairs={{0,6},{1,7},{2,4},{3,5},{4,2},{5,3},{6,0},{7,1},{8,14},{9,15},{10,... | collective-permute-start | bytes 294920 | tf_op jit(solution)/shard_map/ppermute | solution.py:421
  53.6 0.0 collective-permute-done
  53.6 1.6 %collective-permute-start.3 = (f32[2,12,16,128]{3,2,1,0:T(8,128)S(1)}, f32[2,12,16,128]{3,2,1,0:T(8,128)S(1)}, u32[]{:S(2)}, u32[]{:S(2)}) collective-permute-start(f32[2,12,16,128]{3,2,1,0:T(8,128)S(1)} %fusion), channel_id=1, source_target_pairs={{0,8},{8,0},{16,24},{24,16},{1,9},{9,1},{17,25},{25,17},{2,10},{10... | collective-permute-start | bytes 589832 | tf_op jit(solution)/shard_map/ppermute | solution.py:421
  55.2 5.5 %collective-permute-done.3 = f32[2,12,16,128]{3,2,1,0:T(8,128)S(1)} collective-permute-done((f32[2,12,16,128]{3,2,1,0:T(8,128)S(1)}, f32[2,12,16,128]{3,2,1,0:T(8,128)S(1)}, u32[]{:S(2)}, u32[]{:S(2)}) %collective-permute-start.3) | collective-permute-done | bytes 196640 | tf_op jit(solution)/shard_map/ppermute | solution.py:421
  60.6 1.5 %collective-permute-start.1 = (f32[2,12,16,128]{3,2,1,0:T(8,128)S(1)}, f32[2,12,16,128]{3,2,1,0:T(8,128)S(1)}, u32[]{:S(2)}, u32[]{:S(2)}) collective-permute-start(f32[2,12,16,128]{3,2,1,0:T(8,128)S(1)} %fusion.3), channel_id=1, source_target_pairs={{0,16},{8,24},{16,0},{24,8},{1,17},{9,25},{17,1},{25,9},{2,18},{10... | collective-permute-start | bytes 589832 | tf_op jit(solution)/shard_map/ppermute | solution.py:421
  62.2 4.5 %collective-permute-done.1 = f32[2,12,16,128]{3,2,1,0:T(8,128)S(1)} collective-permute-done((f32[2,12,16,128]{3,2,1,0:T(8,128)S(1)}, f32[2,12,16,128]{3,2,1,0:T(8,128)S(1)}, u32[]{:S(2)}, u32[]{:S(2)}) %collective-permute-start.1) | collective-permute-done | bytes 196640 | tf_op jit(solution)/shard_map/ppermute | solution.py:421
  66.7 0.4 collective-permute-start.18
  67.2 0.0 collective-permute-done.12.refs_5_
  67.2 2.8 %collective-permute-start.24 = (f32[2,8,4096]{2,1,0:T(8,128)S(1)}, f32[2,8,4096]{2,1,0:T(8,128)S(1)}, u32[]{:S(2)}, u32[]{:S(2)}) collective-permute-start(f32[2,8,4096]{2,1,0:T(8,128)S(1)} %get-tuple-element.50), channel_id=1, source_target_pairs={{0,24},{8,16},{16,8},{24,0},{1,25},{9,17},{17,9},{25,1},{2,26},{10... | collective-permute-start | bytes 786440 | tf_op jit(solution)/shard_map/ppermute | solution.py:421
  70.0 0.0 collective-permute-done.15.refs_6_
  70.0 1.0 collective-permute-start.9
  71.0 1.6 %collective-permute-done.18.refs_7_ = f32[12,16,128]{2,1,0:T(8,128)S(1)} collective-permute-done((f32[12,16,128]{2,1,0:T(8,128)S(1)}, f32[12,16,128]{2,1,0:T(8,128)S(1)}, u32[]{:S(2)}, u32[]{:S(2)}) %collective-permute-start.18) | collective-permute-done | bytes 98336 | tf_op jit(solution)/shard_map/ppermute | solution.py:421
  72.6 0.0 collective-permute-start.4
  72.6 5.5 %collective-permute-done.9.refs_4_ = f32[12,16,128]{2,1,0:T(8,128)S(1)} collective-permute-done((f32[12,16,128]{2,1,0:T(8,128)S(1)}, f32[12,16,128]{2,1,0:T(8,128)S(1)}, u32[]{:S(2)}, u32[]{:S(2)}) %collective-permute-start.9) | collective-permute-done | bytes 98336 | tf_op jit(solution)/shard_map/ppermute | solution.py:421
  78.2 0.0 collective-permute-start.6
  78.2 0.0 collective-permute-done.4.refs_1_
  78.2 1.7 %collective-permute-start.5 = (f32[12,16,128]{2,1,0:T(8,128)S(1)}, f32[12,16,128]{2,1,0:T(8,128)S(1)}, u32[]{:S(2)}, u32[]{:S(2)}) collective-permute-start(f32[12,16,128]{2,1,0:T(8,128)S(1)} %get-tuple-element.59), channel_id=1, source_target_pairs={{0,2},{1,3},{2,0},{3,1},{4,6},{5,7},{6,4},{7,5},{8,10},{9,11},{10,... | collective-permute-start | bytes 294920 | tf_op jit(solution)/shard_map/ppermute | solution.py:421
  79.9 3.0 %collective-permute-done.6.refs_3_ = f32[12,16,128]{2,1,0:T(8,128)S(1)} collective-permute-done((f32[12,16,128]{2,1,0:T(8,128)S(1)}, f32[12,16,128]{2,1,0:T(8,128)S(1)}, u32[]{:S(2)}, u32[]{:S(2)}) %collective-permute-start.6) | collective-permute-done | bytes 98336 | tf_op jit(solution)/shard_map/ppermute | solution.py:421
  83.0 2.4 %collective-permute-done.5.refs_2_ = f32[12,16,128]{2,1,0:T(8,128)S(1)} collective-permute-done((f32[12,16,128]{2,1,0:T(8,128)S(1)}, f32[12,16,128]{2,1,0:T(8,128)S(1)}, u32[]{:S(2)}, u32[]{:S(2)}) %collective-permute-start.5) | collective-permute-done | bytes 98336 | tf_op jit(solution)/shard_map/ppermute | solution.py:421
  85.4 0.1 coadd.1
  85.4 1.5 %collective-permute-start.19 = (f32[6,32,128]{2,1,0:T(8,128)S(1)}, f32[6,32,128]{2,1,0:T(8,128)S(1)}, u32[]{:S(2)}, u32[]{:S(2)}) collective-permute-start(f32[6,32,128]{2,1,0:T(8,128)S(1)} %get-tuple-element.43.refs_1_), channel_id=1, source_target_pairs={{0,8},{8,0},{16,24},{24,16},{1,9},{9,1},{17,25},{25,17},{2,10},{10... | collective-permute-start | bytes 294920 | tf_op jit(solution)/shard_map/ppermute | solution.py:421
  86.9 0.1 broadcast_in_dim.7
  87.0 0.0 collective-permute-done.22.refs_5_
  87.0 0.1 broadcast_in_dim.8.refs_8_
  87.1 4.0 %deblend.1 = (f32[8,4224]{1,0:T(8,128)S(1)}, f32[8,4224]{1,0:T(8,128)S(1)}, f32[8,4224]{1,0:T(8,128)S(1)}, f32[8,4224]{1,0:T(8,128)S(1)}) custom-call(s32[4]{0:T(128)S(1)} %copy-done.2, f32[6,128,128]{2,1,0:T(8,128)S(1)} %get-tuple-element.46.cov_ref, f32[6,32,128]{2,1,0:T(8,128)S(1)} %get-tuple-element.42.refs_0_, ...), custom_call_target="tpu_custom_call" | custom-call | flops 12582912 | bytes 1966080 | tf_op jit(solution)/shard_map/deblend/pallas_call | solution.py:343
  91.1 0.7 collective-permute-start.25
  91.8 1.4 %collective-permute-start.26 = (f32[8,4224]{1,0:T(8,128)S(1)}, f32[8,4224]{1,0:T(8,128)S(1)}, u32[]{:S(2)}, u32[]{:S(2)}) collective-permute-start(f32[8,4224]{1,0:T(8,128)S(1)} %get-tuple-element.53), channel_id=1, source_target_pairs={{0,16},{8,24},{16,0},{24,8},{1,17},{9,25},{17,1},{25,9},{2,18},{10... | collective-permute-start | bytes 405512 | tf_op jit(solution)/shard_map/ppermute | solution.py:421
  93.2 1.4 %collective-permute-start.27 = (f32[8,4224]{1,0:T(8,128)S(1)}, f32[8,4224]{1,0:T(8,128)S(1)}, u32[]{:S(2)}, u32[]{:S(2)}) collective-permute-start(f32[8,4224]{1,0:T(8,128)S(1)} %get-tuple-element.54), channel_id=1, source_target_pairs={{0,24},{8,16},{16,8},{24,0},{1,25},{9,17},{17,9},{25,1},{2,26},{10... | collective-permute-start | bytes 405512 | tf_op jit(solution)/shard_map/ppermute | solution.py:421
  94.7 1.5 %collective-permute-start.20 = (f32[6,32,128]{2,1,0:T(8,128)S(1)}, f32[6,32,128]{2,1,0:T(8,128)S(1)}, u32[]{:S(2)}, u32[]{:S(2)}) collective-permute-start(f32[6,32,128]{2,1,0:T(8,128)S(1)} %get-tuple-element.44.refs_2_), channel_id=1, source_target_pairs={{0,16},{8,24},{16,0},{24,8},{1,17},{9,25},{17,1},{25,9},{2,18},{10... | collective-permute-start | bytes 294920 | tf_op jit(solution)/shard_map/ppermute | solution.py:421
  96.2 0.0 collective-permute-done.19.refs_1_
  96.2 0.6 collective-permute-start.21
  96.8 7.2 %collective-permute-done.20.refs_2_ = f32[6,32,128]{2,1,0:T(8,128)S(1)} collective-permute-done((f32[6,32,128]{2,1,0:T(8,128)S(1)}, f32[6,32,128]{2,1,0:T(8,128)S(1)}, u32[]{:S(2)}, u32[]{:S(2)}) %collective-permute-start.20) | collective-permute-done | bytes 98336 | tf_op jit(solution)/shard_map/ppermute | solution.py:421
  103.9 0.0 collective-permute-done.21.refs_3_
  103.9 1.1 place_coadd.1
  105.0 0.8 place_morph.1
  (24 shorter events, 0.3 us)
Async XLA Ops:
  0.6 86.3 %copy-start = (f32[4,8,6]{1,0,2:T(4,128)S(1)}, f32[4,8,6]{1,0,2:T(4,128)}, u32[]{:S(2)}) copy-start(f32[4,8,6]{1,0,2:T(4,128)} %param.12) | copy-start | bytes 2308
  0.6 0.7 copy-start.1
  3.2 13.2 %collective-permute-start.10 = (f32[2,1,12,16,128]{4,3,2,1,0:T(8,128)S(1)}, f32[2,1,12,16,128]{4,3,2,1,0:T(8,128)S(1)}, u32[]{:S(2)}, u32[]{:S(2)}) collective-permute-start(f32[2,1,12,16,128]{4,3,2,1,0:T(8,128)S(1)} %get-tuple-element.37), channel_id=1, source_target_pairs={{0,16},{8,24},{16,0},{24,8},{1,17},{9,25},{17,1},{25,9},{2,18},{10... | collective-permute-start | bytes 589832 | tf_op jit(solution)/shard_map/ppermute | solution.py:421
  9.0 40.8 %collective-permute-start.2 = (f32[2,2,12,16,128]{4,3,2,1,0:T(8,128)S(1)}, f32[2,2,12,16,128]{4,3,2,1,0:T(8,128)S(1)}, u32[]{:S(2)}, u32[]{:S(2)}) collective-permute-start(f32[2,2,12,16,128]{4,3,2,1,0:T(8,128)S(1)} %get-tuple-element.33), channel_id=1, source_target_pairs={{0,16},{8,24},{16,0},{24,8},{1,17},{9,25},{17,1},{25,9},{2,18},{10... | collective-permute-start | bytes 1179656 | tf_op jit(solution)/shard_map/ppermute | solution.py:421
  9.1 44.5 %collective-permute-start = (f32[2,2,12,16,128]{4,3,2,1,0:T(8,128)S(1)}, f32[2,2,12,16,128]{4,3,2,1,0:T(8,128)S(1)}, u32[]{:S(2)}, u32[]{:S(2)}) collective-permute-start(f32[2,2,12,16,128]{4,3,2,1,0:T(8,128)S(1)} %get-tuple-element.31), channel_id=1, source_target_pairs={{0,8},{8,0},{16,24},{24,16},{1,9},{9,1},{17,25},{25,17},{2,10},{10... | collective-permute-start | bytes 1179656 | tf_op jit(solution)/shard_map/ppermute | solution.py:421
  12.9 12.4 %collective-permute-start.13 = (f32[2,1,12,16,128]{4,3,2,1,0:T(8,128)S(1)}, f32[2,1,12,16,128]{4,3,2,1,0:T(8,128)S(1)}, u32[]{:S(2)}, u32[]{:S(2)}) collective-permute-start(f32[2,1,12,16,128]{4,3,2,1,0:T(8,128)S(1)} %get-tuple-element.39), channel_id=1, source_target_pairs={{0,8},{8,0},{16,24},{24,16},{1,9},{9,1},{17,25},{25,17},{2,10},{10... | collective-permute-start | bytes 589832 | tf_op jit(solution)/shard_map/ppermute | solution.py:421
  13.1 14.2 %collective-permute-start.16 = (f32[2,1,12,16,128]{4,3,2,1,0:T(8,128)S(1)}, f32[2,1,12,16,128]{4,3,2,1,0:T(8,128)S(1)}, u32[]{:S(2)}, u32[]{:S(2)}) collective-permute-start(f32[2,1,12,16,128]{4,3,2,1,0:T(8,128)S(1)} %get-tuple-element.41), channel_id=1, source_target_pairs={{0,16},{8,24},{16,0},{24,8},{1,17},{9,25},{17,1},{25,9},{2,18},{10... | collective-permute-start | bytes 589832 | tf_op jit(solution)/shard_map/ppermute | solution.py:421
  16.4 13.1 %collective-permute-start.7 = (f32[2,1,12,16,128]{4,3,2,1,0:T(8,128)S(1)}, f32[2,1,12,16,128]{4,3,2,1,0:T(8,128)S(1)}, u32[]{:S(2)}, u32[]{:S(2)}) collective-permute-start(f32[2,1,12,16,128]{4,3,2,1,0:T(8,128)S(1)} %get-tuple-element.35), channel_id=1, source_target_pairs={{0,8},{8,0},{16,24},{24,16},{1,9},{9,1},{17,25},{25,17},{2,10},{10... | collective-permute-start | bytes 589832 | tf_op jit(solution)/shard_map/ppermute | solution.py:421
  25.3 61.7 %collective-permute-start.22 = (f32[2,8,4096]{2,1,0:T(8,128)S(1)}, f32[2,8,4096]{2,1,0:T(8,128)S(1)}, u32[]{:S(2)}, u32[]{:S(2)}) collective-permute-start(f32[2,8,4096]{2,1,0:T(8,128)S(1)} %get-tuple-element.48), channel_id=1, source_target_pairs={{0,8},{8,0},{16,24},{24,16},{1,9},{9,1},{17,25},{25,17},{2,10},{10... | collective-permute-start | bytes 786440 | tf_op jit(solution)/shard_map/ppermute | solution.py:421
  27.3 59.8 %collective-permute-start.23 = (f32[2,8,4096]{2,1,0:T(8,128)S(1)}, f32[2,8,4096]{2,1,0:T(8,128)S(1)}, u32[]{:S(2)}, u32[]{:S(2)}) collective-permute-start(f32[2,8,4096]{2,1,0:T(8,128)S(1)} %get-tuple-element.49), channel_id=1, source_target_pairs={{0,16},{8,24},{16,0},{24,8},{1,17},{9,25},{17,1},{25,9},{2,18},{10... | collective-permute-start | bytes 786440 | tf_op jit(solution)/shard_map/ppermute | solution.py:421
  28.9 58.2 %copy-start.2 = (s32[4]{0:T(128)S(1)}, s32[4]{0:T(128)}, u32[]{:S(2)}) copy-start(s32[4]{0:T(128)} %count_ref.1) | copy-start | bytes 52
  29.5 6.3 %collective-permute-start.11 = (f32[1,12,16,128]{3,2,1,0:T(8,128)S(1)}, f32[1,12,16,128]{3,2,1,0:T(8,128)S(1)}, u32[]{:S(2)}, u32[]{:S(2)}) collective-permute-start(f32[1,12,16,128]{3,2,1,0:T(8,128)S(1)} %fusion.14), channel_id=1, source_target_pairs={{0,8},{8,0},{16,24},{24,16},{1,9},{9,1},{17,25},{25,17},{2,10},{10... | collective-permute-start | bytes 294920 | tf_op jit(solution)/shard_map/ppermute | solution.py:421
  35.9 4.6 %collective-permute-start.14 = (f32[1,12,16,128]{3,2,1,0:T(8,128)S(1)}, f32[1,12,16,128]{3,2,1,0:T(8,128)S(1)}, u32[]{:S(2)}, u32[]{:S(2)}) collective-permute-start(f32[1,12,16,128]{3,2,1,0:T(8,128)S(1)} %fusion.10), channel_id=1, source_target_pairs={{0,16},{8,24},{16,0},{24,8},{1,17},{9,25},{17,1},{25,9},{2,18},{10... | collective-permute-start | bytes 294920 | tf_op jit(solution)/shard_map/ppermute | solution.py:421
  40.5 4.6 %collective-permute-start.17 = (f32[1,12,16,128]{3,2,1,0:T(8,128)S(1)}, f32[1,12,16,128]{3,2,1,0:T(8,128)S(1)}, u32[]{:S(2)}, u32[]{:S(2)}) collective-permute-start(f32[1,12,16,128]{3,2,1,0:T(8,128)S(1)} %fusion.6), channel_id=1, source_target_pairs={{0,8},{8,0},{16,24},{24,16},{1,9},{9,1},{17,25},{25,17},{2,10},{10... | collective-permute-start | bytes 294920 | tf_op jit(solution)/shard_map/ppermute | solution.py:421
  45.1 4.6 %collective-permute-start.8 = (f32[1,12,16,128]{3,2,1,0:T(8,128)S(1)}, f32[1,12,16,128]{3,2,1,0:T(8,128)S(1)}, u32[]{:S(2)}, u32[]{:S(2)}) collective-permute-start(f32[1,12,16,128]{3,2,1,0:T(8,128)S(1)} %fusion.18), channel_id=1, source_target_pairs={{0,16},{8,24},{16,0},{24,8},{1,17},{9,25},{17,1},{25,9},{2,18},{10... | collective-permute-start | bytes 294920 | tf_op jit(solution)/shard_map/ppermute | solution.py:421
  49.7 17.5 %collective-permute-start.12 = (f32[12,16,128]{2,1,0:T(8,128)S(1)}, f32[12,16,128]{2,1,0:T(8,128)S(1)}, u32[]{:S(2)}, u32[]{:S(2)}) collective-permute-start(f32[12,16,128]{2,1,0:T(8,128)S(1)} %fusion.17), channel_id=1, source_target_pairs={{0,5},{1,4},{2,7},{3,6},{4,1},{5,0},{6,3},{7,2},{8,13},{9,12},{10,... | collective-permute-start | bytes 294920 | tf_op jit(solution)/shard_map/ppermute | solution.py:421
  49.7 20.3 %collective-permute-start.15 = (f32[12,16,128]{2,1,0:T(8,128)S(1)}, f32[12,16,128]{2,1,0:T(8,128)S(1)}, u32[]{:S(2)}, u32[]{:S(2)}) collective-permute-start(f32[12,16,128]{2,1,0:T(8,128)S(1)} %fusion.13), channel_id=1, source_target_pairs={{0,6},{1,7},{2,4},{3,5},{4,2},{5,3},{6,0},{7,1},{8,14},{9,15},{10,... | collective-permute-start | bytes 294920 | tf_op jit(solution)/shard_map/ppermute | solution.py:421
  53.6 7.0 %collective-permute-start.3 = (f32[2,12,16,128]{3,2,1,0:T(8,128)S(1)}, f32[2,12,16,128]{3,2,1,0:T(8,128)S(1)}, u32[]{:S(2)}, u32[]{:S(2)}) collective-permute-start(f32[2,12,16,128]{3,2,1,0:T(8,128)S(1)} %fusion), channel_id=1, source_target_pairs={{0,8},{8,0},{16,24},{24,16},{1,9},{9,1},{17,25},{25,17},{2,10},{10... | collective-permute-start | bytes 589832 | tf_op jit(solution)/shard_map/ppermute | solution.py:421
  60.6 6.1 %collective-permute-start.1 = (f32[2,12,16,128]{3,2,1,0:T(8,128)S(1)}, f32[2,12,16,128]{3,2,1,0:T(8,128)S(1)}, u32[]{:S(2)}, u32[]{:S(2)}) collective-permute-start(f32[2,12,16,128]{3,2,1,0:T(8,128)S(1)} %fusion.3), channel_id=1, source_target_pairs={{0,16},{8,24},{16,0},{24,8},{1,17},{9,25},{17,1},{25,9},{2,18},{10... | collective-permute-start | bytes 589832 | tf_op jit(solution)/shard_map/ppermute | solution.py:421
  66.7 5.8 %collective-permute-start.18 = (f32[12,16,128]{2,1,0:T(8,128)S(1)}, f32[12,16,128]{2,1,0:T(8,128)S(1)}, u32[]{:S(2)}, u32[]{:S(2)}) collective-permute-start(f32[12,16,128]{2,1,0:T(8,128)S(1)} %fusion.9), channel_id=1, source_target_pairs={{0,7},{1,6},{2,5},{3,4},{4,3},{5,2},{6,1},{7,0},{8,15},{9,14},{10,... | collective-permute-start | bytes 294920 | tf_op jit(solution)/shard_map/ppermute | solution.py:421
  67.2 19.8 %collective-permute-start.24 = (f32[2,8,4096]{2,1,0:T(8,128)S(1)}, f32[2,8,4096]{2,1,0:T(8,128)S(1)}, u32[]{:S(2)}, u32[]{:S(2)}) collective-permute-start(f32[2,8,4096]{2,1,0:T(8,128)S(1)} %get-tuple-element.50), channel_id=1, source_target_pairs={{0,24},{8,16},{16,8},{24,0},{1,25},{9,17},{17,9},{25,1},{2,26},{10... | collective-permute-start | bytes 786440 | tf_op jit(solution)/shard_map/ppermute | solution.py:421
  70.0 8.2 %collective-permute-start.9 = (f32[12,16,128]{2,1,0:T(8,128)S(1)}, f32[12,16,128]{2,1,0:T(8,128)S(1)}, u32[]{:S(2)}, u32[]{:S(2)}) collective-permute-start(f32[12,16,128]{2,1,0:T(8,128)S(1)} %fusion.21), channel_id=1, source_target_pairs={{0,4},{1,5},{2,6},{3,7},{4,0},{5,1},{6,2},{7,3},{8,12},{9,13},{10,... | collective-permute-start | bytes 294920 | tf_op jit(solution)/shard_map/ppermute | solution.py:421
  72.6 5.6 %collective-permute-start.4 = (f32[12,16,128]{2,1,0:T(8,128)S(1)}, f32[12,16,128]{2,1,0:T(8,128)S(1)}, u32[]{:S(2)}, u32[]{:S(2)}) collective-permute-start(f32[12,16,128]{2,1,0:T(8,128)S(1)} %get-tuple-element.58), channel_id=1, source_target_pairs={{0,1},{1,0},{2,3},{3,2},{4,5},{5,4},{6,7},{7,6},{8,9},{9,8},{10,11... | collective-permute-start | bytes 294920 | tf_op jit(solution)/shard_map/ppermute | solution.py:421
  78.2 4.8 %collective-permute-start.6 = (f32[12,16,128]{2,1,0:T(8,128)S(1)}, f32[12,16,128]{2,1,0:T(8,128)S(1)}, u32[]{:S(2)}, u32[]{:S(2)}) collective-permute-start(f32[12,16,128]{2,1,0:T(8,128)S(1)} %get-tuple-element.57), channel_id=1, source_target_pairs={{0,3},{1,2},{2,1},{3,0},{4,7},{5,6},{6,5},{7,4},{8,11},{9,10},{10,... | collective-permute-start | bytes 294920 | tf_op jit(solution)/shard_map/ppermute | solution.py:421
  78.2 7.2 %collective-permute-start.5 = (f32[12,16,128]{2,1,0:T(8,128)S(1)}, f32[12,16,128]{2,1,0:T(8,128)S(1)}, u32[]{:S(2)}, u32[]{:S(2)}) collective-permute-start(f32[12,16,128]{2,1,0:T(8,128)S(1)} %get-tuple-element.59), channel_id=1, source_target_pairs={{0,2},{1,3},{2,0},{3,1},{4,6},{5,7},{6,4},{7,5},{8,10},{9,11},{10,... | collective-permute-start | bytes 294920 | tf_op jit(solution)/shard_map/ppermute | solution.py:421
  85.4 10.7 %collective-permute-start.19 = (f32[6,32,128]{2,1,0:T(8,128)S(1)}, f32[6,32,128]{2,1,0:T(8,128)S(1)}, u32[]{:S(2)}, u32[]{:S(2)}) collective-permute-start(f32[6,32,128]{2,1,0:T(8,128)S(1)} %get-tuple-element.43.refs_1_), channel_id=1, source_target_pairs={{0,8},{8,0},{16,24},{24,16},{1,9},{9,1},{17,25},{25,17},{2,10},{10... | collective-permute-start | bytes 294920 | tf_op jit(solution)/shard_map/ppermute | solution.py:421
  91.1 13.9 %collective-permute-start.25 = (f32[8,4224]{1,0:T(8,128)S(1)}, f32[8,4224]{1,0:T(8,128)S(1)}, u32[]{:S(2)}, u32[]{:S(2)}) collective-permute-start(f32[8,4224]{1,0:T(8,128)S(1)} %get-tuple-element.52), channel_id=1, source_target_pairs={{0,8},{8,0},{16,24},{24,16},{1,9},{9,1},{17,25},{25,17},{2,10},{10... | collective-permute-start | bytes 405512 | tf_op jit(solution)/shard_map/ppermute | solution.py:421
  91.8 13.2 %collective-permute-start.26 = (f32[8,4224]{1,0:T(8,128)S(1)}, f32[8,4224]{1,0:T(8,128)S(1)}, u32[]{:S(2)}, u32[]{:S(2)}) collective-permute-start(f32[8,4224]{1,0:T(8,128)S(1)} %get-tuple-element.53), channel_id=1, source_target_pairs={{0,16},{8,24},{16,0},{24,8},{1,17},{9,25},{17,1},{25,9},{2,18},{10... | collective-permute-start | bytes 405512 | tf_op jit(solution)/shard_map/ppermute | solution.py:421
  93.2 11.8 %collective-permute-start.27 = (f32[8,4224]{1,0:T(8,128)S(1)}, f32[8,4224]{1,0:T(8,128)S(1)}, u32[]{:S(2)}, u32[]{:S(2)}) collective-permute-start(f32[8,4224]{1,0:T(8,128)S(1)} %get-tuple-element.54), channel_id=1, source_target_pairs={{0,24},{8,16},{16,8},{24,0},{1,25},{9,17},{17,9},{25,1},{2,26},{10... | collective-permute-start | bytes 405512 | tf_op jit(solution)/shard_map/ppermute | solution.py:421
  94.7 9.3 %collective-permute-start.20 = (f32[6,32,128]{2,1,0:T(8,128)S(1)}, f32[6,32,128]{2,1,0:T(8,128)S(1)}, u32[]{:S(2)}, u32[]{:S(2)}) collective-permute-start(f32[6,32,128]{2,1,0:T(8,128)S(1)} %get-tuple-element.44.refs_2_), channel_id=1, source_target_pairs={{0,16},{8,24},{16,0},{24,8},{1,17},{9,25},{17,1},{25,9},{2,18},{10... | collective-permute-start | bytes 294920 | tf_op jit(solution)/shard_map/ppermute | solution.py:421
  96.2 7.7 %collective-permute-start.21 = (f32[6,32,128]{2,1,0:T(8,128)S(1)}, f32[6,32,128]{2,1,0:T(8,128)S(1)}, u32[]{:S(2)}, u32[]{:S(2)}) collective-permute-start(f32[6,32,128]{2,1,0:T(8,128)S(1)} %get-tuple-element.45.refs_3_), channel_id=1, source_target_pairs={{0,24},{8,16},{16,8},{24,0},{1,25},{9,17},{17,9},{25,1},{2,26},{10... | collective-permute-start | bytes 294920 | tf_op jit(solution)/shard_map/ppermute | solution.py:421
where the time goes:
time: 106 us
  waiting for transfers between devices  51 us (48%)
  starting transfers between devices  39.1 us (37%)
  Pallas kernels  13.8 us (13%)
    ppermute x28, waiting for transfers between devices, xor_permute(): return lax.ppermute(x, axis, [(i, i ^ mask) for i in range(size)])  51 us
    ppermute x28, starting transfers between devices, xor_permute(): return lax.ppermute(x, axis, [(i, i ^ mask) for i in range(size)])  39.1 us
    pallas_call x3, Pallas kernels, visit_sums(): pl.pallas_call(kernel, in_specs=[whole(), in_place(), in_place()], out_sp...  6.4 us
    pallas_call x1, Pallas kernels, deblend_kernel(): pl.pallas_call(kernel, in_specs=[pl.BlockSpec(memory_space=pltpu.SMEM)] +...  4.02 us
  transfers between devices with their start and end apart: 28, of which 13 were waited for; matrix products, arithmetic and copies ran while one was open for 0% of the time, Pallas kernels for 10%

commit v1 on v0

--- a/solution.py
+++ b/solution.py
@@ -68,13 +68,18 @@
     return (coadd_flux, spectra, morphology)
 
 
-VMEM_LIMIT = 8 * 1024 * 1024
+VMEM_LIMIT = 6 * 1024 * 1024
+SMALL_LIMIT = 1024 * 1024
 
 
 def hbm(x):
     return pltpu.with_memory_space_constraint(x, pltpu.HBM)
 
 
+def vmem(x):
+    return pltpu.with_memory_space_constraint(x, pltpu.VMEM)
+
+
 def whole():
     return pl.BlockSpec(memory_space=pltpu.VMEM)
 
@@ -91,7 +96,7 @@
     return pltpu.CompilerParams(vmem_limit_bytes=limit)
 
 
-def visit_sums(flux, prec, live, ks, owned, n_e, cores):
+def visit_sums(flux, prec, live, ks, owned, n_e, cores, fetched):
     epochs, bands, blends, pix = flux.shape
     group = cores * owned
     rows = pix // LANES
@@ -100,21 +105,41 @@
     n_k = len(ks)
     order = {0: ((1, 3), (0, 2)), 1: ((2, 3), (0, 1))}
 
-    def kernel(live_ref, flux_ref, prec_ref, s0, k0, s1, k1, scr, fbuf, pbuf, sems):
+    def kernel(live_in, flux_in, prec_in, s0, k0, s1, k1, scr, *own):
         e, b = lax.axis_index("epoch"), lax.axis_index("blend")
         chip, c = b // cores, b % cores
 
-        def copies(i, band):
-            at = pl.ds(pl.multiple_of((chip ^ ks[i]) * group, 8), group)
-            return [
-                pltpu.make_async_copy(ref.at[:, band, at, :], buf.at[i, band], sems.at[i, band, n])
-                for n, (ref, buf) in enumerate(((flux_ref, fbuf), (prec_ref, pbuf)))
-            ]
-
-        for i in range(n_k):
-            for band in range(bands):
-                for copy in copies(i, band):
-                    copy.start()
+        def at_rows(i):
+            return pl.ds(pl.multiple_of((chip ^ ks[i]) * group, 8), group)
+
+        if fetched:
+            live_ref = live_in
+
+            def load(ref, i, band, ep, at):
+                return ref[ep, band, at_rows(i), at].astype(jnp.float32)
+
+            refs = (flux_in, prec_in)
+        else:
+            fbuf, pbuf, live_ref, sems, live_sem = own
+
+            def copies(i, band):
+                return [
+                    pltpu.make_async_copy(ref.at[:, band, at_rows(i), :], buf.at[i, band], sems.at[i, band, n])
+                    for n, (ref, buf) in enumerate(((flux_in, fbuf), (prec_in, pbuf)))
+                ]
+
+            live_copy = pltpu.make_async_copy(live_in, live_ref, live_sem)
+            live_copy.start()
+            for i in range(n_k):
+                for band in range(bands):
+                    for copy in copies(i, band):
+                        copy.start()
+            live_copy.wait()
+
+            def load(ref, i, band, ep, at):
+                return ref[i, band, ep, :, at].astype(jnp.float32)
+
+            refs = (fbuf, pbuf)
         sub = lax.broadcasted_iota(jnp.int32, (group, blends), 0)
         lane = lax.broadcasted_iota(jnp.int32, (group, blends), 1)
         for i in range(n_k):
@@ -125,42 +150,83 @@
                 col = jnp.where(pick, jnp.broadcast_to(row, pick.shape), 0.0)
                 lives.append(jnp.broadcast_to(jnp.sum(col, axis=1, keepdims=True), (group, LANES)))
             for band in range(bands):
-                for copy in copies(i, band):
-                    copy.wait()
+                if not fetched:
+                    for copy in copies(i, band):
+                        copy.wait()
                 for j in range(rows):
                     at = pl.ds(j * LANES, LANES)
                     num = wsum = None
                     for ep in range(epochs):
-                        w = pbuf[i, band, ep, :, at].astype(jnp.float32) * lives[ep]
-                        n = w * fbuf[i, band, ep, :, at].astype(jnp.float32)
+                        w = load(refs[1], i, band, ep, at) * lives[ep]
+                        n = w * load(refs[0], i, band, ep, at)
                         num = n if num is None else num + n
                         wsum = w if wsum is None else wsum + w
                     scr[pl.ds(band * rows + j, group, stride=block_rows), :] = num
                     scr[pl.ds((bands + band) * rows + j, group, stride=block_rows), :] = wsum
-            for d, refs in ((0, (s0, k0)), (1, (s1, k1))):
-                for ref, slots in zip(refs, order[d]):
+            for d, outs in ((0, (s0, k0)), (1, (s1, k1))):
+                for ref, slots in zip(outs, order[d]):
                     for slot, p in enumerate(slots):
                         r = jnp.bitwise_xor(c, d) * n_e + jnp.bitwise_xor(e, p)
                         start = pl.multiple_of(r * block_rows, 8)
                         ref[slot, i] = scr[pl.ds(start, block_rows), :].reshape(2 * bands, rows, LANES)
 
+    scratch = [pltpu.VMEM((group * block_rows, LANES), jnp.float32)]
+    if not fetched:
+        scratch += [
+            pltpu.VMEM((n_k, bands, epochs, group, pix), flux.dtype),
+            pltpu.VMEM((n_k, bands, epochs, group, pix), prec.dtype),
+            pltpu.VMEM(live.shape, live.dtype),
+            pltpu.SemaphoreType.DMA((n_k, bands, 2)),
+            pltpu.SemaphoreType.DMA,
+        ]
     out = pltpu.VMEM((half, n_k, 2 * bands, rows, LANES), jnp.float32)
     n_in = n_k * epochs * bands * group * pix
-    return pl.pallas_call(
-        kernel,
-        in_specs=[whole(), in_place(), in_place()],
+    put = vmem if fetched else hbm
+    return pl.pallas_call(
+        kernel,
+        in_specs=[whole() if fetched else in_place()] * 3,
         out_specs=[whole()] * 4,
         out_shape=[out] * 4,
-        scratch_shapes=[
-            pltpu.VMEM((group * block_rows, LANES), jnp.float32),
-            pltpu.VMEM((n_k, bands, epochs, group, pix), flux.dtype),
-            pltpu.VMEM((n_k, bands, epochs, group, pix), prec.dtype),
-            pltpu.SemaphoreType.DMA((n_k, bands, 2)),
-        ],
+        scratch_shapes=scratch,
         compiler_params=params(),
         cost_estimate=cost(n_in * 6, n_in * 4 + n_in * 2),
         name="visit_sums",
-    )(live, flux, prec)
+    )(put(live), put(flux), put(prec))
+
+
+def halve_kernel(keep, got):
+    def kernel(keep_ref, got_ref, part, onward):
+        part[...] = keep_ref[0] + got_ref[0]
+        onward[...] = keep_ref[1] + got_ref[1]
+
+    out = pltpu.VMEM(keep.shape[1:], keep.dtype)
+    return pl.pallas_call(
+        kernel,
+        in_specs=[whole()] * 2,
+        out_specs=[whole()] * 2,
+        out_shape=[out] * 2,
+        compiler_params=params(SMALL_LIMIT),
+        cost_estimate=cost(keep.size, keep.size * 12),
+        name="halve",
+    )(keep, vmem(got))
+
+
+def finish_kernel(part, got):
+    n_k = part.shape[0]
+
+    def kernel(part_ref, got_ref, *outs):
+        for i in range(n_k):
+            outs[i][...] = part_ref[i] + got_ref[i]
+
+    return pl.pallas_call(
+        kernel,
+        in_specs=[whole()] * 2,
+        out_specs=[whole()] * n_k,
+        out_shape=[pltpu.VMEM(part.shape[1:], part.dtype)] * n_k,
+        compiler_params=params(SMALL_LIMIT),
+        cost_estimate=cost(part.size, part.size * 12),
+        name="finish",
+    )(part, vmem(got))
 
 
 def pack_kernel(morph, footprint, n_e):
@@ -262,7 +328,13 @@
                 mask = pk_in[p][1, :, at] * live
                 ma[pl.ds(start + j, slots, stride=total), :] = mask
                 mo[pl.ds(start + j, slots, stride=total), :] = pk_in[p][0, :, at] * mask
-        spec[...] = spec_ref[...]
+        lane = lax.broadcasted_iota(jnp.int32, (slots, LANES), 1)
+        small = (slots, spec_ref.shape[2])
+        diag = lax.broadcasted_iota(jnp.int32, small, 0) == lax.broadcasted_iota(jnp.int32, small, 1)
+        for c in range(bands):
+            row = jnp.broadcast_to(spec_ref[c, pl.ds(e, 1), :], small)
+            col = jnp.sum(jnp.where(diag, row, 0.0), axis=1, keepdims=True)
+            spec[pl.ds(c * slots, slots), :] = jnp.broadcast_to(col, (slots, LANES))
 
         def bcast(ref, row):
             return jnp.broadcast_to(ref[pl.ds(row, 1), :], (8, LANES))
@@ -302,7 +374,7 @@
                     res[c, pl.ds(at, 8), :] = cv[c] * (cd[c] - model)
                 return carry
 
-            lax.fori_loop(0, groups, group, 0)
+            lax.fori_loop(0, groups, group, 0, unroll=2)
             for k in range(slots):
                 sums = [None] * (bands + 1)
                 for g in range(groups):
@@ -327,7 +399,6 @@
                 s = spec[pl.ds(c * slots, slots), :]
                 spec[pl.ds(c * slots, slots), :] = jnp.maximum(0.0, s + reduced(c) / den)
 
-        lane = lax.broadcasted_iota(jnp.int32, (slots, LANES), 1)
         tile = jnp.zeros((slots, LANES), jnp.float32)
         for c in range(bands):
             on_diag = jnp.where(lane == k_iota, spec[pl.ds(c * slots, slots), :], 0.0)
@@ -424,12 +495,12 @@
 def on_device_blend(
     n_e, n_b, visit_flux, visit_precision, visit_live, footprint, source_count, spectra_init, morphology_init
 ):
-    owned, slots, _ = morphology_init.shape
+    owned, _, _ = morphology_init.shape
     bands = visit_flux.shape[2]
     cores = 2
-    e = lax.axis_index("epoch")
-    flux = hbm(jnp.transpose(visit_flux, (0, 2, 1, 3)))
-    prec = hbm(jnp.transpose(visit_precision, (0, 2, 1, 3)))
+    flux = jnp.transpose(visit_flux, (0, 2, 1, 3))
+    prec = jnp.transpose(visit_precision, (0, 2, 1, 3))
+
 
     def swap(xs):
         out = [xs[0]]
@@ -437,19 +508,18 @@
             out.append(xor_permute(xs[p], "epoch", n_e, p))
         return out
 
-    spectra = lax.dynamic_index_in_dim(spectra_init, e, 0, keepdims=False)
-    spectra = jnp.transpose(spectra).reshape(bands * slots, 1)
-    spectra = jnp.broadcast_to(spectra, (bands * slots, LANES))
+    spectra = jnp.transpose(spectra_init, (2, 0, 1))
 
     chips = n_b // cores
     chunks = [[k] for k in range(chips - 1, 1, -1)] + [[1, 0] if chips > 1 else [0]]
     pieces = [None] * n_b
-    for ks in chunks:
-        s0, k0, s1, k1 = visit_sums(flux, prec, visit_live, ks, owned, n_e, cores)
+    for n, ks in enumerate(chunks):
+        s0, k0, s1, k1 = visit_sums(flux, prec, visit_live, ks, owned, n_e, cores, n > 0)
         for d, (send, keep, first, second) in enumerate(((s0, k0, 1, 2), (s1, k1, 2, 1))):
             got = xor_permute(send, "epoch", n_e, first)
-            onward = xor_permute(keep[1] + got[1], "epoch", n_e, second)
-            full = keep[0] + got[0] + onward
+            part, onward = halve_kernel(keep, got)
+            got = xor_permute(onward, "epoch", n_e, second)
+            full = finish_kernel(part, got)
             for i, k in enumerate(ks):
                 m = k * cores + d
                 pieces[m] = xor_permute(full[i], "blend", n_b, m) if m else full[i]

time: 106 us -> 85.9 us (0.81)
  waiting for transfers between devices: 51 us -> 30.5 us
  local copies, waits for them, and re-layouts: 0.88 us -> 4.47 us
  Pallas kernels: 13.8 us -> 11.9 us
  starting transfers between devices: 39.1 us -> 37.9 us
    ppermute x28, waiting for transfers between devices: 51 us -> 30.5 us  [xor_permute(): return lax.ppermute(x, axis, [(i, i ^ mask) for i in range(size)])]
    unnamed x6 -> x10, local copies, waits for them, and re-layouts: 0.7 us -> 4.47 us
    pallas_call x3 -> x15, Pallas kernels: 6.4 us -> 4.78 us  [the longest x3 4.5 us: visit_sums(): pl.pallas_call(kernel, in_specs=[whole() if fetched else in_place()] * 3,...]
    ppermute x28, starting transfers between devices: 39.1 us -> 37.9 us  [xor_permute(): return lax.ppermute(x, axis, [(i, i ^ mask) for i in range(size)])]
  transfers between devices with their start and end apart: 28 -> 28, of which waited for: 13 -> 8; matrix products, arithmetic and copies ran while one was open for 0% -> 0% of each run, Pallas kernels for 10% -> 11%
where the time goes in v1:
time: 85.9 us; the launch traced here: 85.6 us
  starting transfers between devices  37.9 us (44%)
  waiting for transfers between devices  30.5 us (36%)
  Pallas kernels  11.9 us (14%)
  local copies, waits for them, and re-layouts  4.47 us (5%)
    ppermute x28, starting transfers between devices, xor_permute(): return lax.ppermute(x, axis, [(i, i ^ mask) for i in range(size)])  37.9 us
    ppermute x28, waiting for transfers between devices, xor_permute(): return lax.ppermute(x, axis, [(i, i ^ mask) for i in range(size)])  30.5 us
    pallas_call x3, Pallas kernels, visit_sums(): pl.pallas_call(kernel, in_specs=[whole() if fetched else in_place()] * 3,...  4.5 us
    unnamed x10, local copies, waits for them, and re-layouts  4.47 us
    pallas_call x1, Pallas kernels, deblend_kernel(): pl.pallas_call(kernel, in_specs=[pl.BlockSpec(memory_space=pltpu.SMEM)] +...  3.76 us
  transfers between devices with their start and end apart: 28, of which 8 were waited for; matrix products, arithmetic and copies ran while one was open for 0% of the time, Pallas kernels for 11%

profile of v1, /device:TPU:0, one launch (start us, length us, event | category | flops | bytes accessed | tf_op | source)
XLA Modules:
  0.0 85.6 jit_solution(3641906558017186630)
XLA Ops:
  0.6 0.0 copy-start
  0.6 1.9 %copy-done = bf16[4,32,6,2048]{3,1,2,0:T(8,128)(2,1)S(1)} copy-done((bf16[4,32,6,2048]{3,1,2,0:T(8,128)(2,1)S(1)}, bf16[4,32,6,2048]{3,1,2,0:T(8,128)(2,1)}, u32[]{:S(2)}) %copy-start) | copy-done | bytes 3145752
  2.5 1.9 %copy-done.1 = bf16[4,32,6,2048]{3,1,2,0:T(8,128)(2,1)S(1)} copy-done((bf16[4,32,6,2048]{3,1,2,0:T(8,128)(2,1)S(1)}, bf16[4,32,6,2048]{3,1,2,0:T(8,128)(2,1)}, u32[]{:S(2)}) %copy-start.1) | copy-done | bytes 3145752
  4.4 0.7 copy-done.2
  5.1 1.5 %visit_sums.3 = (f32[2,2,12,16,128]{4,3,2,1,0:T(8,128)S(1)}, f32[2,2,12,16,128]{4,3,2,1,0:T(8,128)S(1)}, f32[2,2,12,16,128]{4,3,2,1,0:T(8,128)S(1)}, f32[2,2,12,16,128]{4,3,2,1,0:T(8,128)S(1)}) custom-call(s32[4,32]{1,0:T(4,128)S(1)} %copy-done.2, bf16[4,6,32,2048]{3,2,1,0:T(8,128)(2,1)S(1)} %bitcast.6, bf16[4,6,32,2048]{3,2,1,0:T(8,128)(2,1)S(1)} %bitcast.9), custom_call_target="tpu_custom_call" | custom-call | flops 4718592 | bytes 4718592 | tf_op jit(solution)/shard_map/visit_sums/pallas_call | solution.py:185
  6.6 3.1 %collective-permute-start.2 = (f32[2,2,12,16,128]{4,3,2,1,0:T(8,128)S(1)}, f32[2,2,12,16,128]{4,3,2,1,0:T(8,128)S(1)}, u32[]{:S(2)}, u32[]{:S(2)}) collective-permute-start(f32[2,2,12,16,128]{4,3,2,1,0:T(8,128)S(1)} %get-tuple-element.52), channel_id=1, source_target_pairs={{0,16},{8,24},{16,0},{24,8},{1,17},{9,25},{17,1},{25,9},{2,18},{10... | collective-permute-start | bytes 1179656 | tf_op jit(solution)/shard_map/ppermute | solution.py:492
  9.7 0.8 visit_sums.4
  10.5 0.1 collective-permute-start.10
  10.6 2.0 %collective-permute-start = (f32[2,2,12,16,128]{4,3,2,1,0:T(8,128)S(1)}, f32[2,2,12,16,128]{4,3,2,1,0:T(8,128)S(1)}, u32[]{:S(2)}, u32[]{:S(2)}) collective-permute-start(f32[2,2,12,16,128]{4,3,2,1,0:T(8,128)S(1)} %get-tuple-element.47), channel_id=1, source_target_pairs={{0,8},{8,0},{16,24},{24,16},{1,9},{9,1},{17,25},{25,17},{2,10},{10... | collective-permute-start | bytes 1179656 | tf_op jit(solution)/shard_map/ppermute | solution.py:492
  12.6 2.2 %visit_sums.5 = (f32[2,1,12,16,128]{4,3,2,1,0:T(8,128)S(1)}, f32[2,1,12,16,128]{4,3,2,1,0:T(8,128)S(1)}, f32[2,1,12,16,128]{4,3,2,1,0:T(8,128)S(1)}, f32[2,1,12,16,128]{4,3,2,1,0:T(8,128)S(1)}) custom-call(s32[4,32]{1,0:T(4,128)} %live_in.5, bf16[4,6,32,2048]{3,2,1,0:T(8,128)(2,1)} %bitcast.5, bf16[4,6,32,2048]{3,2,1,0:T(8,128)(2,1)} %bitcast.8), custom_call_target="tpu_custom_call" | custom-call | flops 2359296 | bytes 2359296 | tf_op jit(solution)/shard_map/visit_sums/pallas_call | solution.py:185
  14.7 0.2 collective-permute-start.13
  14.9 1.9 %collective-permute-start.16 = (f32[2,1,12,16,128]{4,3,2,1,0:T(8,128)S(1)}, f32[2,1,12,16,128]{4,3,2,1,0:T(8,128)S(1)}, u32[]{:S(2)}, u32[]{:S(2)}) collective-permute-start(f32[2,1,12,16,128]{4,3,2,1,0:T(8,128)S(1)} %get-tuple-element.71), channel_id=1, source_target_pairs={{0,16},{8,24},{16,0},{24,8},{1,17},{9,25},{17,1},{25,9},{2,18},{10... | collective-permute-start | bytes 589832 | tf_op jit(solution)/shard_map/ppermute | solution.py:492
  16.9 7.0 %collective-permute-done.10.got_ref = f32[2,1,12,16,128]{4,3,2,1,0:T(8,128)S(1)} collective-permute-done((f32[2,1,12,16,128]{4,3,2,1,0:T(8,128)S(1)}, f32[2,1,12,16,128]{4,3,2,1,0:T(8,128)S(1)}, u32[]{:S(2)}, u32[]{:S(2)}) %collective-permute-start.10) | collective-permute-done | bytes 196640 | tf_op jit(solution)/shard_map/ppermute | solution.py:492
  23.9 2.0 %collective-permute-start.7 = (f32[2,1,12,16,128]{4,3,2,1,0:T(8,128)S(1)}, f32[2,1,12,16,128]{4,3,2,1,0:T(8,128)S(1)}, u32[]{:S(2)}, u32[]{:S(2)}) collective-permute-start(f32[2,1,12,16,128]{4,3,2,1,0:T(8,128)S(1)} %get-tuple-element.59), channel_id=1, source_target_pairs={{0,8},{8,0},{16,24},{24,16},{1,9},{9,1},{17,25},{25,17},{2,10},{10... | collective-permute-start | bytes 589832 | tf_op jit(solution)/shard_map/ppermute | solution.py:492
  25.9 0.1 collective-permute-done.13.got_ref
  26.0 1.8 %collective-permute-start.11 = (f32[1,12,16,128]{3,2,1,0:T(8,128)S(1)}, f32[1,12,16,128]{3,2,1,0:T(8,128)S(1)}, u32[]{:S(2)}, u32[]{:S(2)}) collective-permute-start(f32[1,12,16,128]{3,2,1,0:T(8,128)S(1)} %get-tuple-element.65), channel_id=1, source_target_pairs={{0,8},{8,0},{16,24},{24,16},{1,9},{9,1},{17,25},{25,17},{2,10},{10... | collective-permute-start | bytes 294920 | tf_op jit(solution)/shard_map/ppermute | solution.py:492
  27.9 0.0 copy-start.3
  27.9 0.0 copy-start.4
  27.9 0.0 collective-permute-done.16.got_ref
  27.9 1.6 %collective-permute-start.14 = (f32[1,12,16,128]{3,2,1,0:T(8,128)S(1)}, f32[1,12,16,128]{3,2,1,0:T(8,128)S(1)}, u32[]{:S(2)}, u32[]{:S(2)}) collective-permute-start(f32[1,12,16,128]{3,2,1,0:T(8,128)S(1)} %get-tuple-element.69), channel_id=1, source_target_pairs={{0,16},{8,24},{16,0},{24,8},{1,17},{9,25},{17,1},{25,9},{2,18},{10... | collective-permute-start | bytes 294920 | tf_op jit(solution)/shard_map/ppermute | solution.py:492
  29.5 0.0 collective-permute-done.2.got_ref
  29.5 1.0 %collective-permute-start.17 = (f32[1,12,16,128]{3,2,1,0:T(8,128)S(1)}, f32[1,12,16,128]{3,2,1,0:T(8,128)S(1)}, u32[]{:S(2)}, u32[]{:S(2)}) collective-permute-start(f32[1,12,16,128]{3,2,1,0:T(8,128)S(1)} %get-tuple-element.73), channel_id=1, source_target_pairs={{0,8},{8,0},{16,24},{24,16},{1,9},{9,1},{17,25},{25,17},{2,10},{10... | collective-permute-start | bytes 294920 | tf_op jit(solution)/shard_map/ppermute | solution.py:492
  30.6 0.4 collective-permute-done.7.got_ref
  31.1 1.8 %collective-permute-start.3 = (f32[2,12,16,128]{3,2,1,0:T(8,128)S(1)}, f32[2,12,16,128]{3,2,1,0:T(8,128)S(1)}, u32[]{:S(2)}, u32[]{:S(2)}) collective-permute-start(f32[2,12,16,128]{3,2,1,0:T(8,128)S(1)} %get-tuple-element.54), channel_id=1, source_target_pairs={{0,8},{8,0},{16,24},{24,16},{1,9},{9,1},{17,25},{25,17},{2,10},{10... | collective-permute-start | bytes 589832 | tf_op jit(solution)/shard_map/ppermute | solution.py:492
  32.9 0.0 collective-permute-done.got_ref
  32.9 2.4 %collective-permute-start.8 = (f32[1,12,16,128]{3,2,1,0:T(8,128)S(1)}, f32[1,12,16,128]{3,2,1,0:T(8,128)S(1)}, u32[]{:S(2)}, u32[]{:S(2)}) collective-permute-start(f32[1,12,16,128]{3,2,1,0:T(8,128)S(1)} %get-tuple-element.61), channel_id=1, source_target_pairs={{0,16},{8,24},{16,0},{24,8},{1,17},{9,25},{17,1},{25,9},{2,18},{10... | collective-permute-start | bytes 294920 | tf_op jit(solution)/shard_map/ppermute | solution.py:492
  35.3 0.0 collective-permute-done.11.got_ref
  35.3 0.5 collective-permute-start.1
  35.8 0.0 collective-permute-done.14.got_ref
  35.8 0.1 collective-permute-start.12
  35.9 0.0 collective-permute-done.17.got_ref
  35.9 3.7 %collective-permute-start.15 = (f32[12,16,128]{2,1,0:T(8,128)S(1)}, f32[12,16,128]{2,1,0:T(8,128)S(1)}, u32[]{:S(2)}, u32[]{:S(2)}) collective-permute-start(f32[12,16,128]{2,1,0:T(8,128)S(1)} %finish.10), channel_id=1, source_target_pairs={{0,6},{1,7},{2,4},{3,5},{4,2},{5,3},{6,0},{7,1},{8,14},{9,15},{10,... | collective-permute-start | bytes 294920 | tf_op jit(solution)/shard_map/ppermute | solution.py:492
  39.6 2.3 %collective-permute-start.18 = (f32[12,16,128]{2,1,0:T(8,128)S(1)}, f32[12,16,128]{2,1,0:T(8,128)S(1)}, u32[]{:S(2)}, u32[]{:S(2)}) collective-permute-start(f32[12,16,128]{2,1,0:T(8,128)S(1)} %finish.11), channel_id=1, source_target_pairs={{0,7},{1,6},{2,5},{3,4},{4,3},{5,2},{6,1},{7,0},{8,15},{9,14},{10,... | collective-permute-start | bytes 294920 | tf_op jit(solution)/shard_map/ppermute | solution.py:492
  41.9 1.4 %pack.1 = (f32[2,8,4096]{2,1,0:T(8,128)S(1)}, f32[2,8,4096]{2,1,0:T(8,128)S(1)}, f32[2,8,4096]{2,1,0:T(8,128)S(1)}, f32[2,8,4096]{2,1,0:T(8,128)S(1)}) custom-call(f32[4,8,4096]{2,1,0:T(8,128)} %morph_ref.1, s32[4,8,4096]{2,1,0:T(8,128)} %foot_ref.1), custom_call_target="tpu_custom_call" | custom-call | flops 262144 | bytes 2097152 | tf_op jit(solution)/shard_map/pack/pallas_call | solution.py:256
  43.3 4.7 %collective-permute-done.12.refs_5_ = f32[12,16,128]{2,1,0:T(8,128)S(1)} collective-permute-done((f32[12,16,128]{2,1,0:T(8,128)S(1)}, f32[12,16,128]{2,1,0:T(8,128)S(1)}, u32[]{:S(2)}, u32[]{:S(2)}) %collective-permute-start.12) | collective-permute-done | bytes 98336 | tf_op jit(solution)/shard_map/ppermute | solution.py:492
  47.9 1.5 %collective-permute-start.22 = (f32[2,8,4096]{2,1,0:T(8,128)S(1)}, f32[2,8,4096]{2,1,0:T(8,128)S(1)}, u32[]{:S(2)}, u32[]{:S(2)}) collective-permute-start(f32[2,8,4096]{2,1,0:T(8,128)S(1)} %get-tuple-element.80), channel_id=1, source_target_pairs={{0,8},{8,0},{16,24},{24,16},{1,9},{9,1},{17,25},{25,17},{2,10},{10... | collective-permute-start | bytes 786440 | tf_op jit(solution)/shard_map/ppermute | solution.py:492
  49.4 0.0 collective-permute-done.15.refs_6_
  49.4 0.7 collective-permute-start.23
  50.1 0.0 collective-permute-done.3.got_ref
  50.1 1.3 %collective-permute-start.24 = (f32[2,8,4096]{2,1,0:T(8,128)S(1)}, f32[2,8,4096]{2,1,0:T(8,128)S(1)}, u32[]{:S(2)}, u32[]{:S(2)}) collective-permute-start(f32[2,8,4096]{2,1,0:T(8,128)S(1)} %get-tuple-element.82), channel_id=1, source_target_pairs={{0,24},{8,16},{16,8},{24,0},{1,25},{9,17},{17,9},{25,1},{2,26},{10... | collective-permute-start | bytes 786440 | tf_op jit(solution)/shard_map/ppermute | solution.py:492
  51.5 1.7 %collective-permute-start.9 = (f32[12,16,128]{2,1,0:T(8,128)S(1)}, f32[12,16,128]{2,1,0:T(8,128)S(1)}, u32[]{:S(2)}, u32[]{:S(2)}) collective-permute-start(f32[12,16,128]{2,1,0:T(8,128)S(1)} %finish.8), channel_id=1, source_target_pairs={{0,4},{1,5},{2,6},{3,7},{4,0},{5,1},{6,2},{7,3},{8,12},{9,13},{10,... | collective-permute-start | bytes 294920 | tf_op jit(solution)/shard_map/ppermute | solution.py:492
  53.2 0.0 collective-permute-done.1.got_ref
  53.2 1.1 %collective-permute-start.4 = (f32[12,16,128]{2,1,0:T(8,128)S(1)}, f32[12,16,128]{2,1,0:T(8,128)S(1)}, u32[]{:S(2)}, u32[]{:S(2)}) collective-permute-start(f32[12,16,128]{2,1,0:T(8,128)S(1)} %get-tuple-element.55), channel_id=1, source_target_pairs={{0,1},{1,0},{2,3},{3,2},{4,5},{5,4},{6,7},{7,6},{8,9},{9,8},{10,11... | collective-permute-start | bytes 294920 | tf_op jit(solution)/shard_map/ppermute | solution.py:492
  54.3 5.3 %collective-permute-done.9.refs_4_ = f32[12,16,128]{2,1,0:T(8,128)S(1)} collective-permute-done((f32[12,16,128]{2,1,0:T(8,128)S(1)}, f32[12,16,128]{2,1,0:T(8,128)S(1)}, u32[]{:S(2)}, u32[]{:S(2)}) %collective-permute-start.9) | collective-permute-done | bytes 98336 | tf_op jit(solution)/shard_map/ppermute | solution.py:492
  59.6 0.0 collective-permute-start.6
  59.6 0.2 collective-permute-start.5
  59.8 4.3 %collective-permute-done.6.refs_3_ = f32[12,16,128]{2,1,0:T(8,128)S(1)} collective-permute-done((f32[12,16,128]{2,1,0:T(8,128)S(1)}, f32[12,16,128]{2,1,0:T(8,128)S(1)}, u32[]{:S(2)}, u32[]{:S(2)}) %collective-permute-start.6) | collective-permute-done | bytes 98336 | tf_op jit(solution)/shard_map/ppermute | solution.py:492
  64.1 1.2 %collective-permute-done.5.refs_2_ = f32[12,16,128]{2,1,0:T(8,128)S(1)} collective-permute-done((f32[12,16,128]{2,1,0:T(8,128)S(1)}, f32[12,16,128]{2,1,0:T(8,128)S(1)}, u32[]{:S(2)}, u32[]{:S(2)}) %collective-permute-start.5) | collective-permute-done | bytes 98336 | tf_op jit(solution)/shard_map/ppermute | solution.py:492
  65.3 0.1 coadd.1
  65.4 0.8 collective-permute-start.19
  66.3 0.0 collective-permute-done.22.refs_5_
  66.3 0.0 collective-permute-done.23.refs_6_
  66.3 3.8 %deblend.1 = (f32[8,4224]{1,0:T(8,128)S(1)}, f32[8,4224]{1,0:T(8,128)S(1)}, f32[8,4224]{1,0:T(8,128)S(1)}, f32[8,4224]{1,0:T(8,128)S(1)}) custom-call(s32[4]{0:T(128)S(1)} %copy-done.4, f32[6,128,128]{2,1,0:T(8,128)S(1)} %get-tuple-element.78.cov_ref, f32[6,32,128]{2,1,0:T(8,128)S(1)} %get-tuple-element.74.refs_0_, ...), custom_call_target="tpu_custom_call" | custom-call | flops 12582912 | bytes 1966080 | tf_op jit(solution)/shard_map/deblend/pallas_call | solution.py:414
  70.0 1.3 %collective-permute-start.25 = (f32[8,4224]{1,0:T(8,128)S(1)}, f32[8,4224]{1,0:T(8,128)S(1)}, u32[]{:S(2)}, u32[]{:S(2)}) collective-permute-start(f32[8,4224]{1,0:T(8,128)S(1)} %get-tuple-element.84), channel_id=1, source_target_pairs={{0,8},{8,0},{16,24},{24,16},{1,9},{9,1},{17,25},{25,17},{2,10},{10... | collective-permute-start | bytes 405512 | tf_op jit(solution)/shard_map/ppermute | solution.py:492
  71.4 0.9 %collective-permute-start.26 = (f32[8,4224]{1,0:T(8,128)S(1)}, f32[8,4224]{1,0:T(8,128)S(1)}, u32[]{:S(2)}, u32[]{:S(2)}) collective-permute-start(f32[8,4224]{1,0:T(8,128)S(1)} %get-tuple-element.85), channel_id=1, source_target_pairs={{0,16},{8,24},{16,0},{24,8},{1,17},{9,25},{17,1},{25,9},{2,18},{10... | collective-permute-start | bytes 405512 | tf_op jit(solution)/shard_map/ppermute | solution.py:492
  72.3 1.3 %collective-permute-start.27 = (f32[8,4224]{1,0:T(8,128)S(1)}, f32[8,4224]{1,0:T(8,128)S(1)}, u32[]{:S(2)}, u32[]{:S(2)}) collective-permute-start(f32[8,4224]{1,0:T(8,128)S(1)} %get-tuple-element.86), channel_id=1, source_target_pairs={{0,24},{8,16},{16,8},{24,0},{1,25},{9,17},{17,9},{25,1},{2,26},{10... | collective-permute-start | bytes 405512 | tf_op jit(solution)/shard_map/ppermute | solution.py:492
  73.6 1.4 %collective-permute-start.20 = (f32[6,32,128]{2,1,0:T(8,128)S(1)}, f32[6,32,128]{2,1,0:T(8,128)S(1)}, u32[]{:S(2)}, u32[]{:S(2)}) collective-permute-start(f32[6,32,128]{2,1,0:T(8,128)S(1)} %get-tuple-element.76.refs_2_), channel_id=1, source_target_pairs={{0,16},{8,24},{16,0},{24,8},{1,17},{9,25},{17,1},{25,9},{2,18},{10... | collective-permute-start | bytes 294920 | tf_op jit(solution)/shard_map/ppermute | solution.py:492
  75.0 1.3 %collective-permute-start.21 = (f32[6,32,128]{2,1,0:T(8,128)S(1)}, f32[6,32,128]{2,1,0:T(8,128)S(1)}, u32[]{:S(2)}, u32[]{:S(2)}) collective-permute-start(f32[6,32,128]{2,1,0:T(8,128)S(1)} %get-tuple-element.77.refs_3_), channel_id=1, source_target_pairs={{0,24},{8,16},{16,8},{24,0},{1,25},{9,17},{17,9},{25,1},{2,26},{10... | collective-permute-start | bytes 294920 | tf_op jit(solution)/shard_map/ppermute | solution.py:492
  76.3 7.4 %collective-permute-done.20.refs_2_ = f32[6,32,128]{2,1,0:T(8,128)S(1)} collective-permute-done((f32[6,32,128]{2,1,0:T(8,128)S(1)}, f32[6,32,128]{2,1,0:T(8,128)S(1)}, u32[]{:S(2)}, u32[]{:S(2)}) %collective-permute-start.20) | collective-permute-done | bytes 98336 | tf_op jit(solution)/shard_map/ppermute | solution.py:492
  83.7 0.0 collective-permute-done.21.refs_3_
  83.7 1.1 %place_coadd.1 = f32[6,4,4096]{2,1,0:T(4,128)} custom-call(f32[6,32,128]{2,1,0:T(8,128)S(1)} %get-tuple-element.74.refs_0_, f32[6,32,128]{2,1,0:T(8,128)S(1)} %collective-permute-done.19.refs_1_, f32[6,32,128]{2,1,0:T(8,128)S(1)} %collective-permute-done.20.refs_2_, f32[6,32,128]{2,1,0:T(8,128)S(1)} %collective-permute-done.21.refs_3_), custom_call_target="tpu_custom_call" | custom-call | flops 98304 | bytes 786432 | tf_op jit(solution)/shard_map/place_coadd/pallas_call | solution.py:448
  84.8 0.0 collective-permute-done.26.refs_2_
  84.8 0.0 collective-permute-done.27.refs_3_
  84.8 0.8 place_morph.1
  (22 shorter events, 0.3 us)
Async XLA Ops:
  0.6 1.9 %copy-start = (bf16[4,32,6,2048]{3,1,2,0:T(8,128)(2,1)S(1)}, bf16[4,32,6,2048]{3,1,2,0:T(8,128)(2,1)}, u32[]{:S(2)}) copy-start(bf16[4,32,6,2048]{3,1,2,0:T(8,128)(2,1)} %param.7) | copy-start | bytes 9437188
  2.5 1.9 %copy-start.1 = (bf16[4,32,6,2048]{3,1,2,0:T(8,128)(2,1)S(1)}, bf16[4,32,6,2048]{3,1,2,0:T(8,128)(2,1)}, u32[]{:S(2)}) copy-start(bf16[4,32,6,2048]{3,1,2,0:T(8,128)(2,1)} %param.8) | copy-start | bytes 9437188
  4.4 0.7 copy-start.2
  6.6 22.9 %collective-permute-start.2 = (f32[2,2,12,16,128]{4,3,2,1,0:T(8,128)S(1)}, f32[2,2,12,16,128]{4,3,2,1,0:T(8,128)S(1)}, u32[]{:S(2)}, u32[]{:S(2)}) collective-permute-start(f32[2,2,12,16,128]{4,3,2,1,0:T(8,128)S(1)} %get-tuple-element.52), channel_id=1, source_target_pairs={{0,16},{8,24},{16,0},{24,8},{1,17},{9,25},{17,1},{25,9},{2,18},{10... | collective-permute-start | bytes 1179656 | tf_op jit(solution)/shard_map/ppermute | solution.py:492
  10.5 13.4 %collective-permute-start.10 = (f32[2,1,12,16,128]{4,3,2,1,0:T(8,128)S(1)}, f32[2,1,12,16,128]{4,3,2,1,0:T(8,128)S(1)}, u32[]{:S(2)}, u32[]{:S(2)}) collective-permute-start(f32[2,1,12,16,128]{4,3,2,1,0:T(8,128)S(1)} %get-tuple-element.63), channel_id=1, source_target_pairs={{0,16},{8,24},{16,0},{24,8},{1,17},{9,25},{17,1},{25,9},{2,18},{10... | collective-permute-start | bytes 589832 | tf_op jit(solution)/shard_map/ppermute | solution.py:492
  10.6 22.3 %collective-permute-start = (f32[2,2,12,16,128]{4,3,2,1,0:T(8,128)S(1)}, f32[2,2,12,16,128]{4,3,2,1,0:T(8,128)S(1)}, u32[]{:S(2)}, u32[]{:S(2)}) collective-permute-start(f32[2,2,12,16,128]{4,3,2,1,0:T(8,128)S(1)} %get-tuple-element.47), channel_id=1, source_target_pairs={{0,8},{8,0},{16,24},{24,16},{1,9},{9,1},{17,25},{25,17},{2,10},{10... | collective-permute-start | bytes 1179656 | tf_op jit(solution)/shard_map/ppermute | solution.py:492
  14.7 11.3 %collective-permute-start.13 = (f32[2,1,12,16,128]{4,3,2,1,0:T(8,128)S(1)}, f32[2,1,12,16,128]{4,3,2,1,0:T(8,128)S(1)}, u32[]{:S(2)}, u32[]{:S(2)}) collective-permute-start(f32[2,1,12,16,128]{4,3,2,1,0:T(8,128)S(1)} %get-tuple-element.67), channel_id=1, source_target_pairs={{0,8},{8,0},{16,24},{24,16},{1,9},{9,1},{17,25},{25,17},{2,10},{10... | collective-permute-start | bytes 589832 | tf_op jit(solution)/shard_map/ppermute | solution.py:492
  14.9 13.0 %collective-permute-start.16 = (f32[2,1,12,16,128]{4,3,2,1,0:T(8,128)S(1)}, f32[2,1,12,16,128]{4,3,2,1,0:T(8,128)S(1)}, u32[]{:S(2)}, u32[]{:S(2)}) collective-permute-start(f32[2,1,12,16,128]{4,3,2,1,0:T(8,128)S(1)} %get-tuple-element.71), channel_id=1, source_target_pairs={{0,16},{8,24},{16,0},{24,8},{1,17},{9,25},{17,1},{25,9},{2,18},{10... | collective-permute-start | bytes 589832 | tf_op jit(solution)/shard_map/ppermute | solution.py:492
  23.9 7.2 %collective-permute-start.7 = (f32[2,1,12,16,128]{4,3,2,1,0:T(8,128)S(1)}, f32[2,1,12,16,128]{4,3,2,1,0:T(8,128)S(1)}, u32[]{:S(2)}, u32[]{:S(2)}) collective-permute-start(f32[2,1,12,16,128]{4,3,2,1,0:T(8,128)S(1)} %get-tuple-element.59), channel_id=1, source_target_pairs={{0,8},{8,0},{16,24},{24,16},{1,9},{9,1},{17,25},{25,17},{2,10},{10... | collective-permute-start | bytes 589832 | tf_op jit(solution)/shard_map/ppermute | solution.py:492
  26.0 9.3 %collective-permute-start.11 = (f32[1,12,16,128]{3,2,1,0:T(8,128)S(1)}, f32[1,12,16,128]{3,2,1,0:T(8,128)S(1)}, u32[]{:S(2)}, u32[]{:S(2)}) collective-permute-start(f32[1,12,16,128]{3,2,1,0:T(8,128)S(1)} %get-tuple-element.65), channel_id=1, source_target_pairs={{0,8},{8,0},{16,24},{24,16},{1,9},{9,1},{17,25},{25,17},{2,10},{10... | collective-permute-start | bytes 294920 | tf_op jit(solution)/shard_map/ppermute | solution.py:492
  27.9 38.4 %copy-start.3 = (f32[4,8,6]{1,0,2:T(4,128)S(1)}, f32[4,8,6]{1,0,2:T(4,128)}, u32[]{:S(2)}) copy-start(f32[4,8,6]{1,0,2:T(4,128)} %param.12) | copy-start | bytes 2308
  27.9 38.4 %copy-start.4 = (s32[4]{0:T(128)S(1)}, s32[4]{0:T(128)}, u32[]{:S(2)}) copy-start(s32[4]{0:T(128)} %count_ref.1) | copy-start | bytes 52
  27.9 7.9 %collective-permute-start.14 = (f32[1,12,16,128]{3,2,1,0:T(8,128)S(1)}, f32[1,12,16,128]{3,2,1,0:T(8,128)S(1)}, u32[]{:S(2)}, u32[]{:S(2)}) collective-permute-start(f32[1,12,16,128]{3,2,1,0:T(8,128)S(1)} %get-tuple-element.69), channel_id=1, source_target_pairs={{0,16},{8,24},{16,0},{24,8},{1,17},{9,25},{17,1},{25,9},{2,18},{10... | collective-permute-start | bytes 294920 | tf_op jit(solution)/shard_map/ppermute | solution.py:492
  29.5 6.4 %collective-permute-start.17 = (f32[1,12,16,128]{3,2,1,0:T(8,128)S(1)}, f32[1,12,16,128]{3,2,1,0:T(8,128)S(1)}, u32[]{:S(2)}, u32[]{:S(2)}) collective-permute-start(f32[1,12,16,128]{3,2,1,0:T(8,128)S(1)} %get-tuple-element.73), channel_id=1, source_target_pairs={{0,8},{8,0},{16,24},{24,16},{1,9},{9,1},{17,25},{25,17},{2,10},{10... | collective-permute-start | bytes 294920 | tf_op jit(solution)/shard_map/ppermute | solution.py:492
  31.1 19.1 %collective-permute-start.3 = (f32[2,12,16,128]{3,2,1,0:T(8,128)S(1)}, f32[2,12,16,128]{3,2,1,0:T(8,128)S(1)}, u32[]{:S(2)}, u32[]{:S(2)}) collective-permute-start(f32[2,12,16,128]{3,2,1,0:T(8,128)S(1)} %get-tuple-element.54), channel_id=1, source_target_pairs={{0,8},{8,0},{16,24},{24,16},{1,9},{9,1},{17,25},{25,17},{2,10},{10... | collective-permute-start | bytes 589832 | tf_op jit(solution)/shard_map/ppermute | solution.py:492
  32.9 6.7 %collective-permute-start.8 = (f32[1,12,16,128]{3,2,1,0:T(8,128)S(1)}, f32[1,12,16,128]{3,2,1,0:T(8,128)S(1)}, u32[]{:S(2)}, u32[]{:S(2)}) collective-permute-start(f32[1,12,16,128]{3,2,1,0:T(8,128)S(1)} %get-tuple-element.61), channel_id=1, source_target_pairs={{0,16},{8,24},{16,0},{24,8},{1,17},{9,25},{17,1},{25,9},{2,18},{10... | collective-permute-start | bytes 294920 | tf_op jit(solution)/shard_map/ppermute | solution.py:492
  35.3 17.8 %collective-permute-start.1 = (f32[2,12,16,128]{3,2,1,0:T(8,128)S(1)}, f32[2,12,16,128]{3,2,1,0:T(8,128)S(1)}, u32[]{:S(2)}, u32[]{:S(2)}) collective-permute-start(f32[2,12,16,128]{3,2,1,0:T(8,128)S(1)} %get-tuple-element.49), channel_id=1, source_target_pairs={{0,16},{8,24},{16,0},{24,8},{1,17},{9,25},{17,1},{25,9},{2,18},{10... | collective-permute-start | bytes 589832 | tf_op jit(solution)/shard_map/ppermute | solution.py:492
  35.8 12.1 %collective-permute-start.12 = (f32[12,16,128]{2,1,0:T(8,128)S(1)}, f32[12,16,128]{2,1,0:T(8,128)S(1)}, u32[]{:S(2)}, u32[]{:S(2)}) collective-permute-start(f32[12,16,128]{2,1,0:T(8,128)S(1)} %finish.9), channel_id=1, source_target_pairs={{0,5},{1,4},{2,7},{3,6},{4,1},{5,0},{6,3},{7,2},{8,13},{9,12},{10,... | collective-permute-start | bytes 294920 | tf_op jit(solution)/shard_map/ppermute | solution.py:492
  35.9 13.5 %collective-permute-start.15 = (f32[12,16,128]{2,1,0:T(8,128)S(1)}, f32[12,16,128]{2,1,0:T(8,128)S(1)}, u32[]{:S(2)}, u32[]{:S(2)}) collective-permute-start(f32[12,16,128]{2,1,0:T(8,128)S(1)} %finish.10), channel_id=1, source_target_pairs={{0,6},{1,7},{2,4},{3,5},{4,2},{5,3},{6,0},{7,1},{8,14},{9,15},{10,... | collective-permute-start | bytes 294920 | tf_op jit(solution)/shard_map/ppermute | solution.py:492
  39.6 11.9 %collective-permute-start.18 = (f32[12,16,128]{2,1,0:T(8,128)S(1)}, f32[12,16,128]{2,1,0:T(8,128)S(1)}, u32[]{:S(2)}, u32[]{:S(2)}) collective-permute-start(f32[12,16,128]{2,1,0:T(8,128)S(1)} %finish.11), channel_id=1, source_target_pairs={{0,7},{1,6},{2,5},{3,4},{4,3},{5,2},{6,1},{7,0},{8,15},{9,14},{10,... | collective-permute-start | bytes 294920 | tf_op jit(solution)/shard_map/ppermute | solution.py:492
  47.9 18.3 %collective-permute-start.22 = (f32[2,8,4096]{2,1,0:T(8,128)S(1)}, f32[2,8,4096]{2,1,0:T(8,128)S(1)}, u32[]{:S(2)}, u32[]{:S(2)}) collective-permute-start(f32[2,8,4096]{2,1,0:T(8,128)S(1)} %get-tuple-element.80), channel_id=1, source_target_pairs={{0,8},{8,0},{16,24},{24,16},{1,9},{9,1},{17,25},{25,17},{2,10},{10... | collective-permute-start | bytes 786440 | tf_op jit(solution)/shard_map/ppermute | solution.py:492
  49.4 16.8 %collective-permute-start.23 = (f32[2,8,4096]{2,1,0:T(8,128)S(1)}, f32[2,8,4096]{2,1,0:T(8,128)S(1)}, u32[]{:S(2)}, u32[]{:S(2)}) collective-permute-start(f32[2,8,4096]{2,1,0:T(8,128)S(1)} %get-tuple-element.81), channel_id=1, source_target_pairs={{0,16},{8,24},{16,0},{24,8},{1,17},{9,25},{17,1},{25,9},{2,18},{10... | collective-permute-start | bytes 786440 | tf_op jit(solution)/shard_map/ppermute | solution.py:492
  50.1 16.1 %collective-permute-start.24 = (f32[2,8,4096]{2,1,0:T(8,128)S(1)}, f32[2,8,4096]{2,1,0:T(8,128)S(1)}, u32[]{:S(2)}, u32[]{:S(2)}) collective-permute-start(f32[2,8,4096]{2,1,0:T(8,128)S(1)} %get-tuple-element.82), channel_id=1, source_target_pairs={{0,24},{8,16},{16,8},{24,0},{1,25},{9,17},{17,9},{25,1},{2,26},{10... | collective-permute-start | bytes 786440 | tf_op jit(solution)/shard_map/ppermute | solution.py:492
  51.5 8.1 %collective-permute-start.9 = (f32[12,16,128]{2,1,0:T(8,128)S(1)}, f32[12,16,128]{2,1,0:T(8,128)S(1)}, u32[]{:S(2)}, u32[]{:S(2)}) collective-permute-start(f32[12,16,128]{2,1,0:T(8,128)S(1)} %finish.8), channel_id=1, source_target_pairs={{0,4},{1,5},{2,6},{3,7},{4,0},{5,1},{6,2},{7,3},{8,12},{9,13},{10,... | collective-permute-start | bytes 294920 | tf_op jit(solution)/shard_map/ppermute | solution.py:492
  53.2 6.5 %collective-permute-start.4 = (f32[12,16,128]{2,1,0:T(8,128)S(1)}, f32[12,16,128]{2,1,0:T(8,128)S(1)}, u32[]{:S(2)}, u32[]{:S(2)}) collective-permute-start(f32[12,16,128]{2,1,0:T(8,128)S(1)} %get-tuple-element.55), channel_id=1, source_target_pairs={{0,1},{1,0},{2,3},{3,2},{4,5},{5,4},{6,7},{7,6},{8,9},{9,8},{10,11... | collective-permute-start | bytes 294920 | tf_op jit(solution)/shard_map/ppermute | solution.py:492
  59.6 4.5 %collective-permute-start.6 = (f32[12,16,128]{2,1,0:T(8,128)S(1)}, f32[12,16,128]{2,1,0:T(8,128)S(1)}, u32[]{:S(2)}, u32[]{:S(2)}) collective-permute-start(f32[12,16,128]{2,1,0:T(8,128)S(1)} %get-tuple-element.57), channel_id=1, source_target_pairs={{0,3},{1,2},{2,1},{3,0},{4,7},{5,6},{6,5},{7,4},{8,11},{9,10},{10,... | collective-permute-start | bytes 294920 | tf_op jit(solution)/shard_map/ppermute | solution.py:492
  59.6 5.7 %collective-permute-start.5 = (f32[12,16,128]{2,1,0:T(8,128)S(1)}, f32[12,16,128]{2,1,0:T(8,128)S(1)}, u32[]{:S(2)}, u32[]{:S(2)}) collective-permute-start(f32[12,16,128]{2,1,0:T(8,128)S(1)} %get-tuple-element.56), channel_id=1, source_target_pairs={{0,2},{1,3},{2,0},{3,1},{4,6},{5,7},{6,4},{7,5},{8,10},{9,11},{10,... | collective-permute-start | bytes 294920 | tf_op jit(solution)/shard_map/ppermute | solution.py:492
  65.4 9.6 %collective-permute-start.19 = (f32[6,32,128]{2,1,0:T(8,128)S(1)}, f32[6,32,128]{2,1,0:T(8,128)S(1)}, u32[]{:S(2)}, u32[]{:S(2)}) collective-permute-start(f32[6,32,128]{2,1,0:T(8,128)S(1)} %get-tuple-element.75.refs_1_), channel_id=1, source_target_pairs={{0,8},{8,0},{16,24},{24,16},{1,9},{9,1},{17,25},{25,17},{2,10},{10... | collective-permute-start | bytes 294920 | tf_op jit(solution)/shard_map/ppermute | solution.py:492
  70.0 14.7 %collective-permute-start.25 = (f32[8,4224]{1,0:T(8,128)S(1)}, f32[8,4224]{1,0:T(8,128)S(1)}, u32[]{:S(2)}, u32[]{:S(2)}) collective-permute-start(f32[8,4224]{1,0:T(8,128)S(1)} %get-tuple-element.84), channel_id=1, source_target_pairs={{0,8},{8,0},{16,24},{24,16},{1,9},{9,1},{17,25},{25,17},{2,10},{10... | collective-permute-start | bytes 405512 | tf_op jit(solution)/shard_map/ppermute | solution.py:492
  71.4 13.4 %collective-permute-start.26 = (f32[8,4224]{1,0:T(8,128)S(1)}, f32[8,4224]{1,0:T(8,128)S(1)}, u32[]{:S(2)}, u32[]{:S(2)}) collective-permute-start(f32[8,4224]{1,0:T(8,128)S(1)} %get-tuple-element.85), channel_id=1, source_target_pairs={{0,16},{8,24},{16,0},{24,8},{1,17},{9,25},{17,1},{25,9},{2,18},{10... | collective-permute-start | bytes 405512 | tf_op jit(solution)/shard_map/ppermute | solution.py:492
  72.3 12.5 %collective-permute-start.27 = (f32[8,4224]{1,0:T(8,128)S(1)}, f32[8,4224]{1,0:T(8,128)S(1)}, u32[]{:S(2)}, u32[]{:S(2)}) collective-permute-start(f32[8,4224]{1,0:T(8,128)S(1)} %get-tuple-element.86), channel_id=1, source_target_pairs={{0,24},{8,16},{16,8},{24,0},{1,25},{9,17},{17,9},{25,1},{2,26},{10... | collective-permute-start | bytes 405512 | tf_op jit(solution)/shard_map/ppermute | solution.py:492
  73.6 10.1 %collective-permute-start.20 = (f32[6,32,128]{2,1,0:T(8,128)S(1)}, f32[6,32,128]{2,1,0:T(8,128)S(1)}, u32[]{:S(2)}, u32[]{:S(2)}) collective-permute-start(f32[6,32,128]{2,1,0:T(8,128)S(1)} %get-tuple-element.76.refs_2_), channel_id=1, source_target_pairs={{0,16},{8,24},{16,0},{24,8},{1,17},{9,25},{17,1},{25,9},{2,18},{10... | collective-permute-start | bytes 294920 | tf_op jit(solution)/shard_map/ppermute | solution.py:492
  75.0 8.7 %collective-permute-start.21 = (f32[6,32,128]{2,1,0:T(8,128)S(1)}, f32[6,32,128]{2,1,0:T(8,128)S(1)}, u32[]{:S(2)}, u32[]{:S(2)}) collective-permute-start(f32[6,32,128]{2,1,0:T(8,128)S(1)} %get-tuple-element.77.refs_3_), channel_id=1, source_target_pairs={{0,24},{8,16},{16,8},{24,0},{1,25},{9,17},{17,9},{25,1},{2,26},{10... | collective-permute-start | bytes 294920 | tf_op jit(solution)/shard_map/ppermute | solution.py:492

commit v2 on v1

--- a/solution.py
+++ b/solution.py
@@ -229,43 +229,51 @@
     )(part, vmem(got))
 
 
-def pack_kernel(morph, footprint, n_e):
+def pack_kernel(counts, morph, footprint, n_e):
     _, slots, lanes = morph.shape
-
-    def kernel(morph_ref, foot_ref, *refs):
-        outs, buf, sems = refs[:n_e], refs[n_e], refs[n_e + 1]
+    rows = lanes // LANES
+
+    def kernel(count_ref, morph_ref, foot_ref, *refs):
+        outs, mbuf, fbuf, sems = refs[:n_e], refs[n_e], refs[n_e + 1], refs[n_e + 2]
         e = lax.axis_index("epoch")
         copies = []
         for p in range(n_e):
             q = jnp.bitwise_xor(e, p)
             copies.append(
                 (
-                    pltpu.make_async_copy(morph_ref.at[q], outs[p].at[0], sems.at[p, 0]),
-                    pltpu.make_async_copy(foot_ref.at[q], buf.at[p], sems.at[p, 1]),
+                    pltpu.make_async_copy(morph_ref.at[q], mbuf.at[p], sems.at[p, 0]),
+                    pltpu.make_async_copy(foot_ref.at[q], fbuf.at[p], sems.at[p, 1]),
                 )
             )
         for pair in copies:
             for copy in pair:
                 copy.start()
+        k_iota = lax.broadcasted_iota(jnp.int32, (slots, LANES), 0)
         for p, pair in enumerate(copies):
+            live = (k_iota < count_ref[jnp.bitwise_xor(e, p)]).astype(jnp.float32)
             for copy in pair:
                 copy.wait()
-            outs[p][1] = buf[p].astype(jnp.float32)
+            for j in range(rows):
+                at = pl.ds(j * LANES, LANES)
+                mask = fbuf[p, :, at].astype(jnp.float32) * live
+                outs[p][0, pl.ds(j, slots, stride=rows), :] = mbuf[p, :, at] * mask
+                outs[p][1, pl.ds(j, slots, stride=rows), :] = mask
 
     n = n_e * slots * lanes
     return pl.pallas_call(
         kernel,
-        in_specs=[in_place()] * 2,
+        in_specs=[pl.BlockSpec(memory_space=pltpu.SMEM)] + [in_place()] * 2,
         out_specs=[whole()] * n_e,
-        out_shape=[pltpu.VMEM((2, slots, lanes), jnp.float32)] * n_e,
+        out_shape=[pltpu.VMEM((2, slots * rows, LANES), jnp.float32)] * n_e,
         scratch_shapes=[
+            pltpu.VMEM((n_e, slots, lanes), morph.dtype),
             pltpu.VMEM((n_e, slots, lanes), footprint.dtype),
             pltpu.SemaphoreType.DMA((n_e, 2)),
         ],
         compiler_params=params(),
         cost_estimate=cost(n * 2, n * 16),
         name="pack",
-    )(morph, footprint)
+    )(counts, morph, footprint)
 
 
 def coadd_kernel(pieces, bands, n_e):
@@ -277,17 +285,19 @@
     def kernel(*refs):
         ins, cov, outs, scr = refs[:n_b], refs[n_b], refs[n_b + 1 : n_b + 1 + n_e], refs[-1]
         e, b = lax.axis_index("epoch"), lax.axis_index("blend")
+        parts = per_e // rows
         for m in range(n_b):
-            start = pl.multiple_of(jnp.bitwise_xor(b, m) * rows, 8)
+            at = jnp.bitwise_xor(b, m)
+            block = jnp.bitwise_xor(at // parts, e)
+            start = pl.multiple_of(block * per_e + (at % parts) * rows, 8)
             for band in range(bands):
                 num, wsum = ins[m][band], ins[m][bands + band]
                 inv = 1.0 / (1.0 + wsum)
                 cov[band, pl.ds(start, rows), :] = wsum * inv
                 scr[band, pl.ds(start, rows), :] = num * inv
         for p in range(n_e):
-            start = pl.multiple_of(jnp.bitwise_xor(e, p) * per_e, 8)
             for band in range(bands):
-                outs[p][band] = scr[band, pl.ds(start, per_e), :]
+                outs[p][band] = scr[band, pl.ds(p * per_e, per_e), :]
 
     return pl.pallas_call(
         kernel,
@@ -305,8 +315,9 @@
 def deblend_kernel(counts, cov, coadds, packed, spectra):
     n_e = len(coadds)
     bands, total, _ = cov.shape
-    _, slots, lanes = packed[0].shape
-    per_e = lanes // LANES
+    per_e = total // n_e
+    lanes = per_e * LANES
+    slots = packed[0].shape[1] // per_e
     groups = total // 8
 
     def kernel(count_ref, cov_ref, *refs):
@@ -315,19 +326,15 @@
         outs = refs[2 * n_e + 1 : 3 * n_e + 1]
         co, mo, ma, res, acc, spec, step = refs[3 * n_e + 1 :]
         e = lax.axis_index("epoch")
-        count = count_ref[e]
-        n_live = count.astype(jnp.float32)
+        n_live = count_ref[e].astype(jnp.float32)
         k_iota = lax.broadcasted_iota(jnp.int32, (slots, LANES), 0)
-        live = (k_iota < count).astype(jnp.float32)
         for p in range(n_e):
-            start = jnp.bitwise_xor(e, p) * per_e
             for band in range(bands):
-                co[band, pl.ds(pl.multiple_of(start, 8), per_e), :] = co_in[p][band]
-            for j in range(per_e):
-                at = pl.ds(j * LANES, LANES)
-                mask = pk_in[p][1, :, at] * live
-                ma[pl.ds(start + j, slots, stride=total), :] = mask
-                mo[pl.ds(start + j, slots, stride=total), :] = pk_in[p][0, :, at] * mask
+                co[band, pl.ds(p * per_e, per_e), :] = co_in[p][band]
+            for k in range(slots):
+                at = pl.ds(k * total + p * per_e, per_e)
+                mo[at, :] = pk_in[p][0, pl.ds(k * per_e, per_e), :]
+                ma[at, :] = pk_in[p][1, pl.ds(k * per_e, per_e), :]
         lane = lax.broadcasted_iota(jnp.int32, (slots, LANES), 1)
         small = (slots, spec_ref.shape[2])
         diag = lax.broadcasted_iota(jnp.int32, small, 0) == lax.broadcasted_iota(jnp.int32, small, 1)
@@ -405,9 +412,9 @@
             row = jnp.broadcast_to(jnp.sum(on_diag, axis=0, keepdims=True), (slots, LANES))
             tile = jnp.where(k_iota == c, row, tile)
         for p in range(n_e):
-            start = jnp.bitwise_xor(e, p) * per_e
             for j in range(per_e):
-                outs[p][:, pl.ds(j * LANES, LANES)] = mo[pl.ds(start + j, slots, stride=total), :]
+                at = pl.ds(p * per_e + j, slots, stride=total)
+                outs[p][:, pl.ds(j * LANES, LANES)] = mo[at, :]
             outs[p][:, pl.ds(lanes, LANES)] = tile
 
     f32 = jnp.float32
@@ -523,7 +530,7 @@
             for i, k in enumerate(ks):
                 m = k * cores + d
                 pieces[m] = xor_permute(full[i], "blend", n_b, m) if m else full[i]
-    packed = pack_kernel(hbm(morphology_init), hbm(footprint), n_e)
+    packed = pack_kernel(source_count, hbm(morphology_init), hbm(footprint), n_e)
     packed = swap(packed)
     cov, *coadds = coadd_kernel(pieces, bands, n_e)
     blocks = deblend_kernel(source_count, cov, coadds, packed, spectra)

time: 85.9 us -> 85.3 us (level)
  waiting for transfers between devices: 30.5 us -> 29.6 us
    ppermute x28, waiting for transfers between devices: 30.5 us -> 29.6 us  [xor_permute(): return lax.ppermute(x, axis, [(i, i ^ mask) for i in range(size)])]
  transfers between devices with their start and end apart: 28 -> 28, of which waited for: 8 -> 8; matrix products, arithmetic and copies ran while one was open for 0% -> 0% of each run, Pallas kernels for 11% -> 12%
where the time goes in v2:
time: 85.3 us; the launch traced here: 85.1 us
  starting transfers between devices  38 us (45%)
  waiting for transfers between devices  29.6 us (35%)
  Pallas kernels  12.2 us (14%)
  local copies, waits for them, and re-layouts  4.47 us (5%)
    ppermute x28, starting transfers between devices, xor_permute(): return lax.ppermute(x, axis, [(i, i ^ mask) for i in range(size)])  38 us
    ppermute x28, waiting for transfers between devices, xor_permute(): return lax.ppermute(x, axis, [(i, i ^ mask) for i in range(size)])  29.6 us
    pallas_call x3, Pallas kernels, visit_sums(): pl.pallas_call(kernel, in_specs=[whole() if fetched else in_place()] * 3,...  4.5 us
    unnamed x10, local copies, waits for them, and re-layouts  4.47 us
    pallas_call x1, Pallas kernels, deblend_kernel(): pl.pallas_call(kernel, in_specs=[pl.BlockSpec(memory_space=pltpu.SMEM)] +...  3.22 us
    pallas_call x1, Pallas kernels, pack_kernel(): pl.pallas_call(kernel, in_specs=[pl.BlockSpec(memory_space=pltpu.SMEM)] +...  2.22 us
  transfers between devices with their start and end apart: 28, of which 8 were waited for; matrix products, arithmetic and copies ran while one was open for 0% of the time, Pallas kernels for 12%

profile of v2, /device:TPU:0, one launch (start us, length us, event | category | flops | bytes accessed | tf_op | source)
XLA Modules:
  0.0 85.1 jit_solution(4692059700811665232)
XLA Ops:
  0.6 0.0 copy-start
  0.6 1.9 %copy-done = bf16[4,32,6,2048]{3,1,2,0:T(8,128)(2,1)S(1)} copy-done((bf16[4,32,6,2048]{3,1,2,0:T(8,128)(2,1)S(1)}, bf16[4,32,6,2048]{3,1,2,0:T(8,128)(2,1)}, u32[]{:S(2)}) %copy-start) | copy-done | bytes 3145752
  2.5 1.9 %copy-done.1 = bf16[4,32,6,2048]{3,1,2,0:T(8,128)(2,1)S(1)} copy-done((bf16[4,32,6,2048]{3,1,2,0:T(8,128)(2,1)S(1)}, bf16[4,32,6,2048]{3,1,2,0:T(8,128)(2,1)}, u32[]{:S(2)}) %copy-start.1) | copy-done | bytes 3145752
  4.4 0.7 copy-done.2
  5.1 1.5 %visit_sums.3 = (f32[2,2,12,16,128]{4,3,2,1,0:T(8,128)S(1)}, f32[2,2,12,16,128]{4,3,2,1,0:T(8,128)S(1)}, f32[2,2,12,16,128]{4,3,2,1,0:T(8,128)S(1)}, f32[2,2,12,16,128]{4,3,2,1,0:T(8,128)S(1)}) custom-call(s32[4,32]{1,0:T(4,128)S(1)} %copy-done.2, bf16[4,6,32,2048]{3,2,1,0:T(8,128)(2,1)S(1)} %bitcast.6, bf16[4,6,32,2048]{3,2,1,0:T(8,128)(2,1)S(1)} %bitcast.9), custom_call_target="tpu_custom_call" | custom-call | flops 4718592 | bytes 4718592 | tf_op jit(solution)/shard_map/visit_sums/pallas_call | solution.py:185
  6.6 3.1 %collective-permute-start.2 = (f32[2,2,12,16,128]{4,3,2,1,0:T(8,128)S(1)}, f32[2,2,12,16,128]{4,3,2,1,0:T(8,128)S(1)}, u32[]{:S(2)}, u32[]{:S(2)}) collective-permute-start(f32[2,2,12,16,128]{4,3,2,1,0:T(8,128)S(1)} %get-tuple-element.52), channel_id=1, source_target_pairs={{0,16},{8,24},{16,0},{24,8},{1,17},{9,25},{17,1},{25,9},{2,18},{10... | collective-permute-start | bytes 1179656 | tf_op jit(solution)/shard_map/ppermute | solution.py:499
  9.7 0.8 visit_sums.4
  10.5 0.1 collective-permute-start.10
  10.6 2.0 %collective-permute-start = (f32[2,2,12,16,128]{4,3,2,1,0:T(8,128)S(1)}, f32[2,2,12,16,128]{4,3,2,1,0:T(8,128)S(1)}, u32[]{:S(2)}, u32[]{:S(2)}) collective-permute-start(f32[2,2,12,16,128]{4,3,2,1,0:T(8,128)S(1)} %get-tuple-element.47), channel_id=1, source_target_pairs={{0,8},{8,0},{16,24},{24,16},{1,9},{9,1},{17,25},{25,17},{2,10},{10... | collective-permute-start | bytes 1179656 | tf_op jit(solution)/shard_map/ppermute | solution.py:499
  12.6 2.2 %visit_sums.5 = (f32[2,1,12,16,128]{4,3,2,1,0:T(8,128)S(1)}, f32[2,1,12,16,128]{4,3,2,1,0:T(8,128)S(1)}, f32[2,1,12,16,128]{4,3,2,1,0:T(8,128)S(1)}, f32[2,1,12,16,128]{4,3,2,1,0:T(8,128)S(1)}) custom-call(s32[4,32]{1,0:T(4,128)} %live_in.5, bf16[4,6,32,2048]{3,2,1,0:T(8,128)(2,1)} %bitcast.5, bf16[4,6,32,2048]{3,2,1,0:T(8,128)(2,1)} %bitcast.8), custom_call_target="tpu_custom_call" | custom-call | flops 2359296 | bytes 2359296 | tf_op jit(solution)/shard_map/visit_sums/pallas_call | solution.py:185
  14.7 0.0 copy-start.4
  14.8 0.2 collective-permute-start.13
  14.9 1.9 %collective-permute-start.16 = (f32[2,1,12,16,128]{4,3,2,1,0:T(8,128)S(1)}, f32[2,1,12,16,128]{4,3,2,1,0:T(8,128)S(1)}, u32[]{:S(2)}, u32[]{:S(2)}) collective-permute-start(f32[2,1,12,16,128]{4,3,2,1,0:T(8,128)S(1)} %get-tuple-element.71), channel_id=1, source_target_pairs={{0,16},{8,24},{16,0},{24,8},{1,17},{9,25},{17,1},{25,9},{2,18},{10... | collective-permute-start | bytes 589832 | tf_op jit(solution)/shard_map/ppermute | solution.py:499
  16.9 7.0 %collective-permute-done.10.got_ref = f32[2,1,12,16,128]{4,3,2,1,0:T(8,128)S(1)} collective-permute-done((f32[2,1,12,16,128]{4,3,2,1,0:T(8,128)S(1)}, f32[2,1,12,16,128]{4,3,2,1,0:T(8,128)S(1)}, u32[]{:S(2)}, u32[]{:S(2)}) %collective-permute-start.10) | collective-permute-done | bytes 196640 | tf_op jit(solution)/shard_map/ppermute | solution.py:499
  23.9 2.0 %collective-permute-start.7 = (f32[2,1,12,16,128]{4,3,2,1,0:T(8,128)S(1)}, f32[2,1,12,16,128]{4,3,2,1,0:T(8,128)S(1)}, u32[]{:S(2)}, u32[]{:S(2)}) collective-permute-start(f32[2,1,12,16,128]{4,3,2,1,0:T(8,128)S(1)} %get-tuple-element.59), channel_id=1, source_target_pairs={{0,8},{8,0},{16,24},{24,16},{1,9},{9,1},{17,25},{25,17},{2,10},{10... | collective-permute-start | bytes 589832 | tf_op jit(solution)/shard_map/ppermute | solution.py:499
  25.9 0.1 collective-permute-done.13.got_ref
  26.0 1.8 %collective-permute-start.11 = (f32[1,12,16,128]{3,2,1,0:T(8,128)S(1)}, f32[1,12,16,128]{3,2,1,0:T(8,128)S(1)}, u32[]{:S(2)}, u32[]{:S(2)}) collective-permute-start(f32[1,12,16,128]{3,2,1,0:T(8,128)S(1)} %get-tuple-element.65), channel_id=1, source_target_pairs={{0,8},{8,0},{16,24},{24,16},{1,9},{9,1},{17,25},{25,17},{2,10},{10... | collective-permute-start | bytes 294920 | tf_op jit(solution)/shard_map/ppermute | solution.py:499
  27.9 0.0 copy-start.3
  27.9 0.0 collective-permute-done.16.got_ref
  27.9 1.6 %collective-permute-start.14 = (f32[1,12,16,128]{3,2,1,0:T(8,128)S(1)}, f32[1,12,16,128]{3,2,1,0:T(8,128)S(1)}, u32[]{:S(2)}, u32[]{:S(2)}) collective-permute-start(f32[1,12,16,128]{3,2,1,0:T(8,128)S(1)} %get-tuple-element.69), channel_id=1, source_target_pairs={{0,16},{8,24},{16,0},{24,8},{1,17},{9,25},{17,1},{25,9},{2,18},{10... | collective-permute-start | bytes 294920 | tf_op jit(solution)/shard_map/ppermute | solution.py:499
  29.5 0.0 collective-permute-done.2.got_ref
  29.5 1.1 %collective-permute-start.17 = (f32[1,12,16,128]{3,2,1,0:T(8,128)S(1)}, f32[1,12,16,128]{3,2,1,0:T(8,128)S(1)}, u32[]{:S(2)}, u32[]{:S(2)}) collective-permute-start(f32[1,12,16,128]{3,2,1,0:T(8,128)S(1)} %get-tuple-element.73), channel_id=1, source_target_pairs={{0,8},{8,0},{16,24},{24,16},{1,9},{9,1},{17,25},{25,17},{2,10},{10... | collective-permute-start | bytes 294920 | tf_op jit(solution)/shard_map/ppermute | solution.py:499
  30.6 0.4 collective-permute-done.7.got_ref
  31.1 1.8 %collective-permute-start.3 = (f32[2,12,16,128]{3,2,1,0:T(8,128)S(1)}, f32[2,12,16,128]{3,2,1,0:T(8,128)S(1)}, u32[]{:S(2)}, u32[]{:S(2)}) collective-permute-start(f32[2,12,16,128]{3,2,1,0:T(8,128)S(1)} %get-tuple-element.54), channel_id=1, source_target_pairs={{0,8},{8,0},{16,24},{24,16},{1,9},{9,1},{17,25},{25,17},{2,10},{10... | collective-permute-start | bytes 589832 | tf_op jit(solution)/shard_map/ppermute | solution.py:499
  32.9 0.0 collective-permute-done.got_ref
  32.9 2.4 %collective-permute-start.8 = (f32[1,12,16,128]{3,2,1,0:T(8,128)S(1)}, f32[1,12,16,128]{3,2,1,0:T(8,128)S(1)}, u32[]{:S(2)}, u32[]{:S(2)}) collective-permute-start(f32[1,12,16,128]{3,2,1,0:T(8,128)S(1)} %get-tuple-element.61), channel_id=1, source_target_pairs={{0,16},{8,24},{16,0},{24,8},{1,17},{9,25},{17,1},{25,9},{2,18},{10... | collective-permute-start | bytes 294920 | tf_op jit(solution)/shard_map/ppermute | solution.py:499
  35.3 0.0 collective-permute-done.11.got_ref
  35.3 0.5 collective-permute-start.1
  35.8 0.0 collective-permute-done.14.got_ref
  35.8 0.1 collective-permute-start.12
  35.9 0.0 collective-permute-done.17.got_ref
  35.9 3.7 %collective-permute-start.15 = (f32[12,16,128]{2,1,0:T(8,128)S(1)}, f32[12,16,128]{2,1,0:T(8,128)S(1)}, u32[]{:S(2)}, u32[]{:S(2)}) collective-permute-start(f32[12,16,128]{2,1,0:T(8,128)S(1)} %finish.10), channel_id=1, source_target_pairs={{0,6},{1,7},{2,4},{3,5},{4,2},{5,3},{6,0},{7,1},{8,14},{9,15},{10,... | collective-permute-start | bytes 294920 | tf_op jit(solution)/shard_map/ppermute | solution.py:499
  39.6 0.0 collective-permute-done.8.got_ref
  39.6 2.3 %collective-permute-start.18 = (f32[12,16,128]{2,1,0:T(8,128)S(1)}, f32[12,16,128]{2,1,0:T(8,128)S(1)}, u32[]{:S(2)}, u32[]{:S(2)}) collective-permute-start(f32[12,16,128]{2,1,0:T(8,128)S(1)} %finish.11), channel_id=1, source_target_pairs={{0,7},{1,6},{2,5},{3,4},{4,3},{5,2},{6,1},{7,0},{8,15},{9,14},{10,... | collective-permute-start | bytes 294920 | tf_op jit(solution)/shard_map/ppermute | solution.py:499
  41.9 2.2 %pack.1 = (f32[2,256,128]{2,1,0:T(8,128)S(1)}, f32[2,256,128]{2,1,0:T(8,128)S(1)}, f32[2,256,128]{2,1,0:T(8,128)S(1)}, f32[2,256,128]{2,1,0:T(8,128)S(1)}) custom-call(s32[4]{0:T(128)S(1)} %copy-done.4, f32[4,8,4096]{2,1,0:T(8,128)} %morph_ref.1, s32[4,8,4096]{2,1,0:T(8,128)} %foot_ref.1), custom_call_target="tpu_custom_call" | custom-call | flops 262144 | bytes 2097152 | tf_op jit(solution)/shard_map/pack/pallas_call | solution.py:263
  44.1 3.8 %collective-permute-done.12.refs_5_ = f32[12,16,128]{2,1,0:T(8,128)S(1)} collective-permute-done((f32[12,16,128]{2,1,0:T(8,128)S(1)}, f32[12,16,128]{2,1,0:T(8,128)S(1)}, u32[]{:S(2)}, u32[]{:S(2)}) %collective-permute-start.12) | collective-permute-done | bytes 98336 | tf_op jit(solution)/shard_map/ppermute | solution.py:499
  47.9 1.5 %collective-permute-start.22 = (f32[2,256,128]{2,1,0:T(8,128)S(1)}, f32[2,256,128]{2,1,0:T(8,128)S(1)}, u32[]{:S(2)}, u32[]{:S(2)}) collective-permute-start(f32[2,256,128]{2,1,0:T(8,128)S(1)} %get-tuple-element.80), channel_id=1, source_target_pairs={{0,8},{8,0},{16,24},{24,16},{1,9},{9,1},{17,25},{25,17},{2,10},{10... | collective-permute-start | bytes 786440 | tf_op jit(solution)/shard_map/ppermute | solution.py:499
  49.4 0.0 collective-permute-done.15.refs_6_
  49.4 0.7 collective-permute-start.23
  50.1 0.0 collective-permute-done.3.got_ref
  50.1 1.3 %collective-permute-start.24 = (f32[2,256,128]{2,1,0:T(8,128)S(1)}, f32[2,256,128]{2,1,0:T(8,128)S(1)}, u32[]{:S(2)}, u32[]{:S(2)}) collective-permute-start(f32[2,256,128]{2,1,0:T(8,128)S(1)} %get-tuple-element.82), channel_id=1, source_target_pairs={{0,24},{8,16},{16,8},{24,0},{1,25},{9,17},{17,9},{25,1},{2,26},{10... | collective-permute-start | bytes 786440 | tf_op jit(solution)/shard_map/ppermute | solution.py:499
  51.5 0.0 collective-permute-done.18.refs_7_
  51.5 1.7 %collective-permute-start.9 = (f32[12,16,128]{2,1,0:T(8,128)S(1)}, f32[12,16,128]{2,1,0:T(8,128)S(1)}, u32[]{:S(2)}, u32[]{:S(2)}) collective-permute-start(f32[12,16,128]{2,1,0:T(8,128)S(1)} %finish.8), channel_id=1, source_target_pairs={{0,4},{1,5},{2,6},{3,7},{4,0},{5,1},{6,2},{7,3},{8,12},{9,13},{10,... | collective-permute-start | bytes 294920 | tf_op jit(solution)/shard_map/ppermute | solution.py:499
  53.2 0.0 collective-permute-done.1.got_ref
  53.2 1.1 %collective-permute-start.4 = (f32[12,16,128]{2,1,0:T(8,128)S(1)}, f32[12,16,128]{2,1,0:T(8,128)S(1)}, u32[]{:S(2)}, u32[]{:S(2)}) collective-permute-start(f32[12,16,128]{2,1,0:T(8,128)S(1)} %get-tuple-element.55), channel_id=1, source_target_pairs={{0,1},{1,0},{2,3},{3,2},{4,5},{5,4},{6,7},{7,6},{8,9},{9,8},{10,11... | collective-permute-start | bytes 294920 | tf_op jit(solution)/shard_map/ppermute | solution.py:499
  54.3 5.3 %collective-permute-done.9.refs_4_ = f32[12,16,128]{2,1,0:T(8,128)S(1)} collective-permute-done((f32[12,16,128]{2,1,0:T(8,128)S(1)}, f32[12,16,128]{2,1,0:T(8,128)S(1)}, u32[]{:S(2)}, u32[]{:S(2)}) %collective-permute-start.9) | collective-permute-done | bytes 98336 | tf_op jit(solution)/shard_map/ppermute | solution.py:499
  59.6 0.0 collective-permute-start.6
  59.6 0.0 collective-permute-done.4.refs_1_
  59.6 0.2 collective-permute-start.5
  59.8 4.3 %collective-permute-done.6.refs_3_ = f32[12,16,128]{2,1,0:T(8,128)S(1)} collective-permute-done((f32[12,16,128]{2,1,0:T(8,128)S(1)}, f32[12,16,128]{2,1,0:T(8,128)S(1)}, u32[]{:S(2)}, u32[]{:S(2)}) %collective-permute-start.6) | collective-permute-done | bytes 98336 | tf_op jit(solution)/shard_map/ppermute | solution.py:499
  64.1 1.2 %collective-permute-done.5.refs_2_ = f32[12,16,128]{2,1,0:T(8,128)S(1)} collective-permute-done((f32[12,16,128]{2,1,0:T(8,128)S(1)}, f32[12,16,128]{2,1,0:T(8,128)S(1)}, u32[]{:S(2)}, u32[]{:S(2)}) %collective-permute-start.5) | collective-permute-done | bytes 98336 | tf_op jit(solution)/shard_map/ppermute | solution.py:499
  65.3 0.1 coadd.1
  65.4 0.8 collective-permute-start.19
  66.3 3.2 %deblend.1 = (f32[8,4224]{1,0:T(8,128)S(1)}, f32[8,4224]{1,0:T(8,128)S(1)}, f32[8,4224]{1,0:T(8,128)S(1)}, f32[8,4224]{1,0:T(8,128)S(1)}) custom-call(s32[4]{0:T(128)S(1)} %copy-done.4, f32[6,128,128]{2,1,0:T(8,128)S(1)} %get-tuple-element.78.cov_ref, f32[6,32,128]{2,1,0:T(8,128)S(1)} %get-tuple-element.74.refs_0_, ...), custom_call_target="tpu_custom_call" | custom-call | flops 12582912 | bytes 1966080 | tf_op jit(solution)/shard_map/deblend/pallas_call | solution.py:421
  69.5 1.3 %collective-permute-start.25 = (f32[8,4224]{1,0:T(8,128)S(1)}, f32[8,4224]{1,0:T(8,128)S(1)}, u32[]{:S(2)}, u32[]{:S(2)}) collective-permute-start(f32[8,4224]{1,0:T(8,128)S(1)} %get-tuple-element.84), channel_id=1, source_target_pairs={{0,8},{8,0},{16,24},{24,16},{1,9},{9,1},{17,25},{25,17},{2,10},{10... | collective-permute-start | bytes 405512 | tf_op jit(solution)/shard_map/ppermute | solution.py:499
  70.8 0.9 %collective-permute-start.26 = (f32[8,4224]{1,0:T(8,128)S(1)}, f32[8,4224]{1,0:T(8,128)S(1)}, u32[]{:S(2)}, u32[]{:S(2)}) collective-permute-start(f32[8,4224]{1,0:T(8,128)S(1)} %get-tuple-element.85), channel_id=1, source_target_pairs={{0,16},{8,24},{16,0},{24,8},{1,17},{9,25},{17,1},{25,9},{2,18},{10... | collective-permute-start | bytes 405512 | tf_op jit(solution)/shard_map/ppermute | solution.py:499
  71.8 1.3 %collective-permute-start.27 = (f32[8,4224]{1,0:T(8,128)S(1)}, f32[8,4224]{1,0:T(8,128)S(1)}, u32[]{:S(2)}, u32[]{:S(2)}) collective-permute-start(f32[8,4224]{1,0:T(8,128)S(1)} %get-tuple-element.86), channel_id=1, source_target_pairs={{0,24},{8,16},{16,8},{24,0},{1,25},{9,17},{17,9},{25,1},{2,26},{10... | collective-permute-start | bytes 405512 | tf_op jit(solution)/shard_map/ppermute | solution.py:499
  73.1 1.4 %collective-permute-start.20 = (f32[6,32,128]{2,1,0:T(8,128)S(1)}, f32[6,32,128]{2,1,0:T(8,128)S(1)}, u32[]{:S(2)}, u32[]{:S(2)}) collective-permute-start(f32[6,32,128]{2,1,0:T(8,128)S(1)} %get-tuple-element.76.refs_2_), channel_id=1, source_target_pairs={{0,16},{8,24},{16,0},{24,8},{1,17},{9,25},{17,1},{25,9},{2,18},{10... | collective-permute-start | bytes 294920 | tf_op jit(solution)/shard_map/ppermute | solution.py:499
  74.5 0.0 collective-permute-done.19.refs_1_
  74.5 1.3 %collective-permute-start.21 = (f32[6,32,128]{2,1,0:T(8,128)S(1)}, f32[6,32,128]{2,1,0:T(8,128)S(1)}, u32[]{:S(2)}, u32[]{:S(2)}) collective-permute-start(f32[6,32,128]{2,1,0:T(8,128)S(1)} %get-tuple-element.77.refs_3_), channel_id=1, source_target_pairs={{0,24},{8,16},{16,8},{24,0},{1,25},{9,17},{17,9},{25,1},{2,26},{10... | collective-permute-start | bytes 294920 | tf_op jit(solution)/shard_map/ppermute | solution.py:499
  75.8 7.4 %collective-permute-done.20.refs_2_ = f32[6,32,128]{2,1,0:T(8,128)S(1)} collective-permute-done((f32[6,32,128]{2,1,0:T(8,128)S(1)}, f32[6,32,128]{2,1,0:T(8,128)S(1)}, u32[]{:S(2)}, u32[]{:S(2)}) %collective-permute-start.20) | collective-permute-done | bytes 98336 | tf_op jit(solution)/shard_map/ppermute | solution.py:499
  83.2 0.0 collective-permute-done.21.refs_3_
  83.2 1.1 %place_coadd.1 = f32[6,4,4096]{2,1,0:T(4,128)} custom-call(f32[6,32,128]{2,1,0:T(8,128)S(1)} %get-tuple-element.74.refs_0_, f32[6,32,128]{2,1,0:T(8,128)S(1)} %collective-permute-done.19.refs_1_, f32[6,32,128]{2,1,0:T(8,128)S(1)} %collective-permute-done.20.refs_2_, f32[6,32,128]{2,1,0:T(8,128)S(1)} %collective-permute-done.21.refs_3_), custom_call_target="tpu_custom_call" | custom-call | flops 98304 | bytes 786432 | tf_op jit(solution)/shard_map/place_coadd/pallas_call | solution.py:455
  84.2 0.8 place_morph.1
  (22 shorter events, 0.3 us)
Async XLA Ops:
  0.6 1.9 %copy-start = (bf16[4,32,6,2048]{3,1,2,0:T(8,128)(2,1)S(1)}, bf16[4,32,6,2048]{3,1,2,0:T(8,128)(2,1)}, u32[]{:S(2)}) copy-start(bf16[4,32,6,2048]{3,1,2,0:T(8,128)(2,1)} %param.7) | copy-start | bytes 9437188
  2.5 1.9 %copy-start.1 = (bf16[4,32,6,2048]{3,1,2,0:T(8,128)(2,1)S(1)}, bf16[4,32,6,2048]{3,1,2,0:T(8,128)(2,1)}, u32[]{:S(2)}) copy-start(bf16[4,32,6,2048]{3,1,2,0:T(8,128)(2,1)} %param.8) | copy-start | bytes 9437188
  4.4 0.7 copy-start.2
  6.6 22.9 %collective-permute-start.2 = (f32[2,2,12,16,128]{4,3,2,1,0:T(8,128)S(1)}, f32[2,2,12,16,128]{4,3,2,1,0:T(8,128)S(1)}, u32[]{:S(2)}, u32[]{:S(2)}) collective-permute-start(f32[2,2,12,16,128]{4,3,2,1,0:T(8,128)S(1)} %get-tuple-element.52), channel_id=1, source_target_pairs={{0,16},{8,24},{16,0},{24,8},{1,17},{9,25},{17,1},{25,9},{2,18},{10... | collective-permute-start | bytes 1179656 | tf_op jit(solution)/shard_map/ppermute | solution.py:499
  10.5 13.4 %collective-permute-start.10 = (f32[2,1,12,16,128]{4,3,2,1,0:T(8,128)S(1)}, f32[2,1,12,16,128]{4,3,2,1,0:T(8,128)S(1)}, u32[]{:S(2)}, u32[]{:S(2)}) collective-permute-start(f32[2,1,12,16,128]{4,3,2,1,0:T(8,128)S(1)} %get-tuple-element.63), channel_id=1, source_target_pairs={{0,16},{8,24},{16,0},{24,8},{1,17},{9,25},{17,1},{25,9},{2,18},{10... | collective-permute-start | bytes 589832 | tf_op jit(solution)/shard_map/ppermute | solution.py:499
  10.6 22.3 %collective-permute-start = (f32[2,2,12,16,128]{4,3,2,1,0:T(8,128)S(1)}, f32[2,2,12,16,128]{4,3,2,1,0:T(8,128)S(1)}, u32[]{:S(2)}, u32[]{:S(2)}) collective-permute-start(f32[2,2,12,16,128]{4,3,2,1,0:T(8,128)S(1)} %get-tuple-element.47), channel_id=1, source_target_pairs={{0,8},{8,0},{16,24},{24,16},{1,9},{9,1},{17,25},{25,17},{2,10},{10... | collective-permute-start | bytes 1179656 | tf_op jit(solution)/shard_map/ppermute | solution.py:499
  14.7 27.2 %copy-start.4 = (s32[4]{0:T(128)S(1)}, s32[4]{0:T(128)}, u32[]{:S(2)}) copy-start(s32[4]{0:T(128)} %count_ref.3) | copy-start | bytes 52
  14.8 11.3 %collective-permute-start.13 = (f32[2,1,12,16,128]{4,3,2,1,0:T(8,128)S(1)}, f32[2,1,12,16,128]{4,3,2,1,0:T(8,128)S(1)}, u32[]{:S(2)}, u32[]{:S(2)}) collective-permute-start(f32[2,1,12,16,128]{4,3,2,1,0:T(8,128)S(1)} %get-tuple-element.67), channel_id=1, source_target_pairs={{0,8},{8,0},{16,24},{24,16},{1,9},{9,1},{17,25},{25,17},{2,10},{10... | collective-permute-start | bytes 589832 | tf_op jit(solution)/shard_map/ppermute | solution.py:499
  14.9 13.0 %collective-permute-start.16 = (f32[2,1,12,16,128]{4,3,2,1,0:T(8,128)S(1)}, f32[2,1,12,16,128]{4,3,2,1,0:T(8,128)S(1)}, u32[]{:S(2)}, u32[]{:S(2)}) collective-permute-start(f32[2,1,12,16,128]{4,3,2,1,0:T(8,128)S(1)} %get-tuple-element.71), channel_id=1, source_target_pairs={{0,16},{8,24},{16,0},{24,8},{1,17},{9,25},{17,1},{25,9},{2,18},{10... | collective-permute-start | bytes 589832 | tf_op jit(solution)/shard_map/ppermute | solution.py:499
  23.9 7.2 %collective-permute-start.7 = (f32[2,1,12,16,128]{4,3,2,1,0:T(8,128)S(1)}, f32[2,1,12,16,128]{4,3,2,1,0:T(8,128)S(1)}, u32[]{:S(2)}, u32[]{:S(2)}) collective-permute-start(f32[2,1,12,16,128]{4,3,2,1,0:T(8,128)S(1)} %get-tuple-element.59), channel_id=1, source_target_pairs={{0,8},{8,0},{16,24},{24,16},{1,9},{9,1},{17,25},{25,17},{2,10},{10... | collective-permute-start | bytes 589832 | tf_op jit(solution)/shard_map/ppermute | solution.py:499
  26.0 9.3 %collective-permute-start.11 = (f32[1,12,16,128]{3,2,1,0:T(8,128)S(1)}, f32[1,12,16,128]{3,2,1,0:T(8,128)S(1)}, u32[]{:S(2)}, u32[]{:S(2)}) collective-permute-start(f32[1,12,16,128]{3,2,1,0:T(8,128)S(1)} %get-tuple-element.65), channel_id=1, source_target_pairs={{0,8},{8,0},{16,24},{24,16},{1,9},{9,1},{17,25},{25,17},{2,10},{10... | collective-permute-start | bytes 294920 | tf_op jit(solution)/shard_map/ppermute | solution.py:499
  27.9 38.4 %copy-start.3 = (f32[4,8,6]{1,0,2:T(4,128)S(1)}, f32[4,8,6]{1,0,2:T(4,128)}, u32[]{:S(2)}) copy-start(f32[4,8,6]{1,0,2:T(4,128)} %param.12) | copy-start | bytes 2308
  27.9 7.9 %collective-permute-start.14 = (f32[1,12,16,128]{3,2,1,0:T(8,128)S(1)}, f32[1,12,16,128]{3,2,1,0:T(8,128)S(1)}, u32[]{:S(2)}, u32[]{:S(2)}) collective-permute-start(f32[1,12,16,128]{3,2,1,0:T(8,128)S(1)} %get-tuple-element.69), channel_id=1, source_target_pairs={{0,16},{8,24},{16,0},{24,8},{1,17},{9,25},{17,1},{25,9},{2,18},{10... | collective-permute-start | bytes 294920 | tf_op jit(solution)/shard_map/ppermute | solution.py:499
  29.5 6.4 %collective-permute-start.17 = (f32[1,12,16,128]{3,2,1,0:T(8,128)S(1)}, f32[1,12,16,128]{3,2,1,0:T(8,128)S(1)}, u32[]{:S(2)}, u32[]{:S(2)}) collective-permute-start(f32[1,12,16,128]{3,2,1,0:T(8,128)S(1)} %get-tuple-element.73), channel_id=1, source_target_pairs={{0,8},{8,0},{16,24},{24,16},{1,9},{9,1},{17,25},{25,17},{2,10},{10... | collective-permute-start | bytes 294920 | tf_op jit(solution)/shard_map/ppermute | solution.py:499
  31.1 19.1 %collective-permute-start.3 = (f32[2,12,16,128]{3,2,1,0:T(8,128)S(1)}, f32[2,12,16,128]{3,2,1,0:T(8,128)S(1)}, u32[]{:S(2)}, u32[]{:S(2)}) collective-permute-start(f32[2,12,16,128]{3,2,1,0:T(8,128)S(1)} %get-tuple-element.54), channel_id=1, source_target_pairs={{0,8},{8,0},{16,24},{24,16},{1,9},{9,1},{17,25},{25,17},{2,10},{10... | collective-permute-start | bytes 589832 | tf_op jit(solution)/shard_map/ppermute | solution.py:499
  32.9 6.7 %collective-permute-start.8 = (f32[1,12,16,128]{3,2,1,0:T(8,128)S(1)}, f32[1,12,16,128]{3,2,1,0:T(8,128)S(1)}, u32[]{:S(2)}, u32[]{:S(2)}) collective-permute-start(f32[1,12,16,128]{3,2,1,0:T(8,128)S(1)} %get-tuple-element.61), channel_id=1, source_target_pairs={{0,16},{8,24},{16,0},{24,8},{1,17},{9,25},{17,1},{25,9},{2,18},{10... | collective-permute-start | bytes 294920 | tf_op jit(solution)/shard_map/ppermute | solution.py:499
  35.3 17.8 %collective-permute-start.1 = (f32[2,12,16,128]{3,2,1,0:T(8,128)S(1)}, f32[2,12,16,128]{3,2,1,0:T(8,128)S(1)}, u32[]{:S(2)}, u32[]{:S(2)}) collective-permute-start(f32[2,12,16,128]{3,2,1,0:T(8,128)S(1)} %get-tuple-element.49), channel_id=1, source_target_pairs={{0,16},{8,24},{16,0},{24,8},{1,17},{9,25},{17,1},{25,9},{2,18},{10... | collective-permute-start | bytes 589832 | tf_op jit(solution)/shard_map/ppermute | solution.py:499
  35.8 12.1 %collective-permute-start.12 = (f32[12,16,128]{2,1,0:T(8,128)S(1)}, f32[12,16,128]{2,1,0:T(8,128)S(1)}, u32[]{:S(2)}, u32[]{:S(2)}) collective-permute-start(f32[12,16,128]{2,1,0:T(8,128)S(1)} %finish.9), channel_id=1, source_target_pairs={{0,5},{1,4},{2,7},{3,6},{4,1},{5,0},{6,3},{7,2},{8,13},{9,12},{10,... | collective-permute-start | bytes 294920 | tf_op jit(solution)/shard_map/ppermute | solution.py:499
  35.9 13.5 %collective-permute-start.15 = (f32[12,16,128]{2,1,0:T(8,128)S(1)}, f32[12,16,128]{2,1,0:T(8,128)S(1)}, u32[]{:S(2)}, u32[]{:S(2)}) collective-permute-start(f32[12,16,128]{2,1,0:T(8,128)S(1)} %finish.10), channel_id=1, source_target_pairs={{0,6},{1,7},{2,4},{3,5},{4,2},{5,3},{6,0},{7,1},{8,14},{9,15},{10,... | collective-permute-start | bytes 294920 | tf_op jit(solution)/shard_map/ppermute | solution.py:499
  39.6 11.9 %collective-permute-start.18 = (f32[12,16,128]{2,1,0:T(8,128)S(1)}, f32[12,16,128]{2,1,0:T(8,128)S(1)}, u32[]{:S(2)}, u32[]{:S(2)}) collective-permute-start(f32[12,16,128]{2,1,0:T(8,128)S(1)} %finish.11), channel_id=1, source_target_pairs={{0,7},{1,6},{2,5},{3,4},{4,3},{5,2},{6,1},{7,0},{8,15},{9,14},{10,... | collective-permute-start | bytes 294920 | tf_op jit(solution)/shard_map/ppermute | solution.py:499
  47.9 18.3 %collective-permute-start.22 = (f32[2,256,128]{2,1,0:T(8,128)S(1)}, f32[2,256,128]{2,1,0:T(8,128)S(1)}, u32[]{:S(2)}, u32[]{:S(2)}) collective-permute-start(f32[2,256,128]{2,1,0:T(8,128)S(1)} %get-tuple-element.80), channel_id=1, source_target_pairs={{0,8},{8,0},{16,24},{24,16},{1,9},{9,1},{17,25},{25,17},{2,10},{10... | collective-permute-start | bytes 786440 | tf_op jit(solution)/shard_map/ppermute | solution.py:499
  49.4 16.8 %collective-permute-start.23 = (f32[2,256,128]{2,1,0:T(8,128)S(1)}, f32[2,256,128]{2,1,0:T(8,128)S(1)}, u32[]{:S(2)}, u32[]{:S(2)}) collective-permute-start(f32[2,256,128]{2,1,0:T(8,128)S(1)} %get-tuple-element.81), channel_id=1, source_target_pairs={{0,16},{8,24},{16,0},{24,8},{1,17},{9,25},{17,1},{25,9},{2,18},{10... | collective-permute-start | bytes 786440 | tf_op jit(solution)/shard_map/ppermute | solution.py:499
  50.1 16.2 %collective-permute-start.24 = (f32[2,256,128]{2,1,0:T(8,128)S(1)}, f32[2,256,128]{2,1,0:T(8,128)S(1)}, u32[]{:S(2)}, u32[]{:S(2)}) collective-permute-start(f32[2,256,128]{2,1,0:T(8,128)S(1)} %get-tuple-element.82), channel_id=1, source_target_pairs={{0,24},{8,16},{16,8},{24,0},{1,25},{9,17},{17,9},{25,1},{2,26},{10... | collective-permute-start | bytes 786440 | tf_op jit(solution)/shard_map/ppermute | solution.py:499
  51.5 8.1 %collective-permute-start.9 = (f32[12,16,128]{2,1,0:T(8,128)S(1)}, f32[12,16,128]{2,1,0:T(8,128)S(1)}, u32[]{:S(2)}, u32[]{:S(2)}) collective-permute-start(f32[12,16,128]{2,1,0:T(8,128)S(1)} %finish.8), channel_id=1, source_target_pairs={{0,4},{1,5},{2,6},{3,7},{4,0},{5,1},{6,2},{7,3},{8,12},{9,13},{10,... | collective-permute-start | bytes 294920 | tf_op jit(solution)/shard_map/ppermute | solution.py:499
  53.2 6.5 %collective-permute-start.4 = (f32[12,16,128]{2,1,0:T(8,128)S(1)}, f32[12,16,128]{2,1,0:T(8,128)S(1)}, u32[]{:S(2)}, u32[]{:S(2)}) collective-permute-start(f32[12,16,128]{2,1,0:T(8,128)S(1)} %get-tuple-element.55), channel_id=1, source_target_pairs={{0,1},{1,0},{2,3},{3,2},{4,5},{5,4},{6,7},{7,6},{8,9},{9,8},{10,11... | collective-permute-start | bytes 294920 | tf_op jit(solution)/shard_map/ppermute | solution.py:499
  59.6 4.5 %collective-permute-start.6 = (f32[12,16,128]{2,1,0:T(8,128)S(1)}, f32[12,16,128]{2,1,0:T(8,128)S(1)}, u32[]{:S(2)}, u32[]{:S(2)}) collective-permute-start(f32[12,16,128]{2,1,0:T(8,128)S(1)} %get-tuple-element.57), channel_id=1, source_target_pairs={{0,3},{1,2},{2,1},{3,0},{4,7},{5,6},{6,5},{7,4},{8,11},{9,10},{10,... | collective-permute-start | bytes 294920 | tf_op jit(solution)/shard_map/ppermute | solution.py:499
  59.6 5.7 %collective-permute-start.5 = (f32[12,16,128]{2,1,0:T(8,128)S(1)}, f32[12,16,128]{2,1,0:T(8,128)S(1)}, u32[]{:S(2)}, u32[]{:S(2)}) collective-permute-start(f32[12,16,128]{2,1,0:T(8,128)S(1)} %get-tuple-element.56), channel_id=1, source_target_pairs={{0,2},{1,3},{2,0},{3,1},{4,6},{5,7},{6,4},{7,5},{8,10},{9,11},{10,... | collective-permute-start | bytes 294920 | tf_op jit(solution)/shard_map/ppermute | solution.py:499
  65.4 9.0 %collective-permute-start.19 = (f32[6,32,128]{2,1,0:T(8,128)S(1)}, f32[6,32,128]{2,1,0:T(8,128)S(1)}, u32[]{:S(2)}, u32[]{:S(2)}) collective-permute-start(f32[6,32,128]{2,1,0:T(8,128)S(1)} %get-tuple-element.75.refs_1_), channel_id=1, source_target_pairs={{0,8},{8,0},{16,24},{24,16},{1,9},{9,1},{17,25},{25,17},{2,10},{10... | collective-permute-start | bytes 294920 | tf_op jit(solution)/shard_map/ppermute | solution.py:499
  69.5 14.7 %collective-permute-start.25 = (f32[8,4224]{1,0:T(8,128)S(1)}, f32[8,4224]{1,0:T(8,128)S(1)}, u32[]{:S(2)}, u32[]{:S(2)}) collective-permute-start(f32[8,4224]{1,0:T(8,128)S(1)} %get-tuple-element.84), channel_id=1, source_target_pairs={{0,8},{8,0},{16,24},{24,16},{1,9},{9,1},{17,25},{25,17},{2,10},{10... | collective-permute-start | bytes 405512 | tf_op jit(solution)/shard_map/ppermute | solution.py:499
  70.8 13.4 %collective-permute-start.26 = (f32[8,4224]{1,0:T(8,128)S(1)}, f32[8,4224]{1,0:T(8,128)S(1)}, u32[]{:S(2)}, u32[]{:S(2)}) collective-permute-start(f32[8,4224]{1,0:T(8,128)S(1)} %get-tuple-element.85), channel_id=1, source_target_pairs={{0,16},{8,24},{16,0},{24,8},{1,17},{9,25},{17,1},{25,9},{2,18},{10... | collective-permute-start | bytes 405512 | tf_op jit(solution)/shard_map/ppermute | solution.py:499
  71.8 12.5 %collective-permute-start.27 = (f32[8,4224]{1,0:T(8,128)S(1)}, f32[8,4224]{1,0:T(8,128)S(1)}, u32[]{:S(2)}, u32[]{:S(2)}) collective-permute-start(f32[8,4224]{1,0:T(8,128)S(1)} %get-tuple-element.86), channel_id=1, source_target_pairs={{0,24},{8,16},{16,8},{24,0},{1,25},{9,17},{17,9},{25,1},{2,26},{10... | collective-permute-start | bytes 405512 | tf_op jit(solution)/shard_map/ppermute | solution.py:499
  73.1 10.1 %collective-permute-start.20 = (f32[6,32,128]{2,1,0:T(8,128)S(1)}, f32[6,32,128]{2,1,0:T(8,128)S(1)}, u32[]{:S(2)}, u32[]{:S(2)}) collective-permute-start(f32[6,32,128]{2,1,0:T(8,128)S(1)} %get-tuple-element.76.refs_2_), channel_id=1, source_target_pairs={{0,16},{8,24},{16,0},{24,8},{1,17},{9,25},{17,1},{25,9},{2,18},{10... | collective-permute-start | bytes 294920 | tf_op jit(solution)/shard_map/ppermute | solution.py:499
  74.5 8.7 %collective-permute-start.21 = (f32[6,32,128]{2,1,0:T(8,128)S(1)}, f32[6,32,128]{2,1,0:T(8,128)S(1)}, u32[]{:S(2)}, u32[]{:S(2)}) collective-permute-start(f32[6,32,128]{2,1,0:T(8,128)S(1)} %get-tuple-element.77.refs_3_), channel_id=1, source_target_pairs={{0,24},{8,16},{16,8},{24,0},{1,25},{9,17},{17,9},{25,1},{2,26},{10... | collective-permute-start | bytes 294920 | tf_op jit(solution)/shard_map/ppermute | solution.py:499

commit v3 on v2

--- a/solution.py
+++ b/solution.py
@@ -129,11 +129,11 @@
                 ]
 
             live_copy = pltpu.make_async_copy(live_in, live_ref, live_sem)
-            live_copy.start()
+            live_copy.start(priority=1)
             for i in range(n_k):
                 for band in range(bands):
-                    for copy in copies(i, band):
-                        copy.start()
+                    for n, copy in enumerate(copies(i, band)):
+                        copy.start(priority=n)
             live_copy.wait()
 
             def load(ref, i, band, ep, at):

time: 85.3 us -> 85.3 us (level)
  no operation moved by 1% of the time
where the time goes in v3:
time: 85.3 us; the launch traced here: 85.1 us
  starting transfers between devices  38 us (45%)
  waiting for transfers between devices  29.5 us (35%)
  Pallas kernels  12.3 us (14%)
  local copies, waits for them, and re-layouts  4.47 us (5%)
    ppermute x28, starting transfers between devices, xor_permute(): return lax.ppermute(x, axis, [(i, i ^ mask) for i in range(size)])  38 us
    ppermute x28, waiting for transfers between devices, xor_permute(): return lax.ppermute(x, axis, [(i, i ^ mask) for i in range(size)])  29.5 us
    pallas_call x3, Pallas kernels, visit_sums(): pl.pallas_call(kernel, in_specs=[whole() if fetched else in_place()] * 3,...  4.6 us
    unnamed x10, local copies, waits for them, and re-layouts  4.47 us
    pallas_call x1, Pallas kernels, deblend_kernel(): pl.pallas_call(kernel, in_specs=[pl.BlockSpec(memory_space=pltpu.SMEM)] +...  3.22 us
    pallas_call x1, Pallas kernels, pack_kernel(): pl.pallas_call(kernel, in_specs=[pl.BlockSpec(memory_space=pltpu.SMEM)] +...  2.22 us
  transfers between devices with their start and end apart: 28, of which 8 were waited for; matrix products, arithmetic and copies ran while one was open for 0% of the time, Pallas kernels for 12%

profile of v3, /device:TPU:0, one launch (start us, length us, event | category | flops | bytes accessed | tf_op | source)
XLA Modules:
  0.0 85.1 jit_solution(11145157488533825582)
XLA Ops:
  0.6 0.0 copy-start
  0.6 1.9 %copy-done = bf16[4,32,6,2048]{3,1,2,0:T(8,128)(2,1)S(1)} copy-done((bf16[4,32,6,2048]{3,1,2,0:T(8,128)(2,1)S(1)}, bf16[4,32,6,2048]{3,1,2,0:T(8,128)(2,1)}, u32[]{:S(2)}) %copy-start) | copy-done | bytes 3145752
  2.5 1.9 %copy-done.1 = bf16[4,32,6,2048]{3,1,2,0:T(8,128)(2,1)S(1)} copy-done((bf16[4,32,6,2048]{3,1,2,0:T(8,128)(2,1)S(1)}, bf16[4,32,6,2048]{3,1,2,0:T(8,128)(2,1)}, u32[]{:S(2)}) %copy-start.1) | copy-done | bytes 3145752
  4.4 0.7 copy-done.2
  5.1 1.5 %visit_sums.3 = (f32[2,2,12,16,128]{4,3,2,1,0:T(8,128)S(1)}, f32[2,2,12,16,128]{4,3,2,1,0:T(8,128)S(1)}, f32[2,2,12,16,128]{4,3,2,1,0:T(8,128)S(1)}, f32[2,2,12,16,128]{4,3,2,1,0:T(8,128)S(1)}) custom-call(s32[4,32]{1,0:T(4,128)S(1)} %copy-done.2, bf16[4,6,32,2048]{3,2,1,0:T(8,128)(2,1)S(1)} %bitcast.6, bf16[4,6,32,2048]{3,2,1,0:T(8,128)(2,1)S(1)} %bitcast.9), custom_call_target="tpu_custom_call" | custom-call | flops 4718592 | bytes 4718592 | tf_op jit(solution)/shard_map/visit_sums/pallas_call | solution.py:185
  6.6 3.1 %collective-permute-start.2 = (f32[2,2,12,16,128]{4,3,2,1,0:T(8,128)S(1)}, f32[2,2,12,16,128]{4,3,2,1,0:T(8,128)S(1)}, u32[]{:S(2)}, u32[]{:S(2)}) collective-permute-start(f32[2,2,12,16,128]{4,3,2,1,0:T(8,128)S(1)} %get-tuple-element.52), channel_id=1, source_target_pairs={{0,16},{8,24},{16,0},{24,8},{1,17},{9,25},{17,1},{25,9},{2,18},{10... | collective-permute-start | bytes 1179656 | tf_op jit(solution)/shard_map/ppermute | solution.py:499
  9.7 0.8 visit_sums.4
  10.5 0.1 collective-permute-start.10
  10.6 2.0 %collective-permute-start = (f32[2,2,12,16,128]{4,3,2,1,0:T(8,128)S(1)}, f32[2,2,12,16,128]{4,3,2,1,0:T(8,128)S(1)}, u32[]{:S(2)}, u32[]{:S(2)}) collective-permute-start(f32[2,2,12,16,128]{4,3,2,1,0:T(8,128)S(1)} %get-tuple-element.47), channel_id=1, source_target_pairs={{0,8},{8,0},{16,24},{24,16},{1,9},{9,1},{17,25},{25,17},{2,10},{10... | collective-permute-start | bytes 1179656 | tf_op jit(solution)/shard_map/ppermute | solution.py:499
  12.6 2.3 %visit_sums.5 = (f32[2,1,12,16,128]{4,3,2,1,0:T(8,128)S(1)}, f32[2,1,12,16,128]{4,3,2,1,0:T(8,128)S(1)}, f32[2,1,12,16,128]{4,3,2,1,0:T(8,128)S(1)}, f32[2,1,12,16,128]{4,3,2,1,0:T(8,128)S(1)}) custom-call(s32[4,32]{1,0:T(4,128)} %live_in.5, bf16[4,6,32,2048]{3,2,1,0:T(8,128)(2,1)} %bitcast.5, bf16[4,6,32,2048]{3,2,1,0:T(8,128)(2,1)} %bitcast.8), custom_call_target="tpu_custom_call" | custom-call | flops 2359296 | bytes 2359296 | tf_op jit(solution)/shard_map/visit_sums/pallas_call | solution.py:185
  14.8 0.0 copy-start.4
  14.9 0.2 collective-permute-start.13
  15.0 1.9 %collective-permute-start.16 = (f32[2,1,12,16,128]{4,3,2,1,0:T(8,128)S(1)}, f32[2,1,12,16,128]{4,3,2,1,0:T(8,128)S(1)}, u32[]{:S(2)}, u32[]{:S(2)}) collective-permute-start(f32[2,1,12,16,128]{4,3,2,1,0:T(8,128)S(1)} %get-tuple-element.71), channel_id=1, source_target_pairs={{0,16},{8,24},{16,0},{24,8},{1,17},{9,25},{17,1},{25,9},{2,18},{10... | collective-permute-start | bytes 589832 | tf_op jit(solution)/shard_map/ppermute | solution.py:499
  17.0 6.9 %collective-permute-done.10.got_ref = f32[2,1,12,16,128]{4,3,2,1,0:T(8,128)S(1)} collective-permute-done((f32[2,1,12,16,128]{4,3,2,1,0:T(8,128)S(1)}, f32[2,1,12,16,128]{4,3,2,1,0:T(8,128)S(1)}, u32[]{:S(2)}, u32[]{:S(2)}) %collective-permute-start.10) | collective-permute-done | bytes 196640 | tf_op jit(solution)/shard_map/ppermute | solution.py:499
  23.9 2.0 %collective-permute-start.7 = (f32[2,1,12,16,128]{4,3,2,1,0:T(8,128)S(1)}, f32[2,1,12,16,128]{4,3,2,1,0:T(8,128)S(1)}, u32[]{:S(2)}, u32[]{:S(2)}) collective-permute-start(f32[2,1,12,16,128]{4,3,2,1,0:T(8,128)S(1)} %get-tuple-element.59), channel_id=1, source_target_pairs={{0,8},{8,0},{16,24},{24,16},{1,9},{9,1},{17,25},{25,17},{2,10},{10... | collective-permute-start | bytes 589832 | tf_op jit(solution)/shard_map/ppermute | solution.py:499
  25.9 0.1 collective-permute-done.13.got_ref
  26.0 1.8 %collective-permute-start.11 = (f32[1,12,16,128]{3,2,1,0:T(8,128)S(1)}, f32[1,12,16,128]{3,2,1,0:T(8,128)S(1)}, u32[]{:S(2)}, u32[]{:S(2)}) collective-permute-start(f32[1,12,16,128]{3,2,1,0:T(8,128)S(1)} %get-tuple-element.65), channel_id=1, source_target_pairs={{0,8},{8,0},{16,24},{24,16},{1,9},{9,1},{17,25},{25,17},{2,10},{10... | collective-permute-start | bytes 294920 | tf_op jit(solution)/shard_map/ppermute | solution.py:499
  27.9 0.0 copy-start.3
  27.9 0.0 collective-permute-done.16.got_ref
  27.9 1.6 %collective-permute-start.14 = (f32[1,12,16,128]{3,2,1,0:T(8,128)S(1)}, f32[1,12,16,128]{3,2,1,0:T(8,128)S(1)}, u32[]{:S(2)}, u32[]{:S(2)}) collective-permute-start(f32[1,12,16,128]{3,2,1,0:T(8,128)S(1)} %get-tuple-element.69), channel_id=1, source_target_pairs={{0,16},{8,24},{16,0},{24,8},{1,17},{9,25},{17,1},{25,9},{2,18},{10... | collective-permute-start | bytes 294920 | tf_op jit(solution)/shard_map/ppermute | solution.py:499
  29.5 0.0 collective-permute-done.2.got_ref
  29.5 1.1 %collective-permute-start.17 = (f32[1,12,16,128]{3,2,1,0:T(8,128)S(1)}, f32[1,12,16,128]{3,2,1,0:T(8,128)S(1)}, u32[]{:S(2)}, u32[]{:S(2)}) collective-permute-start(f32[1,12,16,128]{3,2,1,0:T(8,128)S(1)} %get-tuple-element.73), channel_id=1, source_target_pairs={{0,8},{8,0},{16,24},{24,16},{1,9},{9,1},{17,25},{25,17},{2,10},{10... | collective-permute-start | bytes 294920 | tf_op jit(solution)/shard_map/ppermute | solution.py:499
  30.6 0.4 collective-permute-done.7.got_ref
  31.1 1.8 %collective-permute-start.3 = (f32[2,12,16,128]{3,2,1,0:T(8,128)S(1)}, f32[2,12,16,128]{3,2,1,0:T(8,128)S(1)}, u32[]{:S(2)}, u32[]{:S(2)}) collective-permute-start(f32[2,12,16,128]{3,2,1,0:T(8,128)S(1)} %get-tuple-element.54), channel_id=1, source_target_pairs={{0,8},{8,0},{16,24},{24,16},{1,9},{9,1},{17,25},{25,17},{2,10},{10... | collective-permute-start | bytes 589832 | tf_op jit(solution)/shard_map/ppermute | solution.py:499
  32.9 0.0 collective-permute-done.got_ref
  32.9 2.4 %collective-permute-start.8 = (f32[1,12,16,128]{3,2,1,0:T(8,128)S(1)}, f32[1,12,16,128]{3,2,1,0:T(8,128)S(1)}, u32[]{:S(2)}, u32[]{:S(2)}) collective-permute-start(f32[1,12,16,128]{3,2,1,0:T(8,128)S(1)} %get-tuple-element.61), channel_id=1, source_target_pairs={{0,16},{8,24},{16,0},{24,8},{1,17},{9,25},{17,1},{25,9},{2,18},{10... | collective-permute-start | bytes 294920 | tf_op jit(solution)/shard_map/ppermute | solution.py:499
  35.3 0.0 collective-permute-done.11.got_ref
  35.3 0.5 collective-permute-start.1
  35.8 0.0 collective-permute-done.14.got_ref
  35.8 0.1 collective-permute-start.12
  35.9 0.0 collective-permute-done.17.got_ref
  35.9 3.7 %collective-permute-start.15 = (f32[12,16,128]{2,1,0:T(8,128)S(1)}, f32[12,16,128]{2,1,0:T(8,128)S(1)}, u32[]{:S(2)}, u32[]{:S(2)}) collective-permute-start(f32[12,16,128]{2,1,0:T(8,128)S(1)} %finish.10), channel_id=1, source_target_pairs={{0,6},{1,7},{2,4},{3,5},{4,2},{5,3},{6,0},{7,1},{8,14},{9,15},{10,... | collective-permute-start | bytes 294920 | tf_op jit(solution)/shard_map/ppermute | solution.py:499
  39.6 0.0 collective-permute-done.8.got_ref
  39.6 2.3 %collective-permute-start.18 = (f32[12,16,128]{2,1,0:T(8,128)S(1)}, f32[12,16,128]{2,1,0:T(8,128)S(1)}, u32[]{:S(2)}, u32[]{:S(2)}) collective-permute-start(f32[12,16,128]{2,1,0:T(8,128)S(1)} %finish.11), channel_id=1, source_target_pairs={{0,7},{1,6},{2,5},{3,4},{4,3},{5,2},{6,1},{7,0},{8,15},{9,14},{10,... | collective-permute-start | bytes 294920 | tf_op jit(solution)/shard_map/ppermute | solution.py:499
  41.9 2.2 %pack.1 = (f32[2,256,128]{2,1,0:T(8,128)S(1)}, f32[2,256,128]{2,1,0:T(8,128)S(1)}, f32[2,256,128]{2,1,0:T(8,128)S(1)}, f32[2,256,128]{2,1,0:T(8,128)S(1)}) custom-call(s32[4]{0:T(128)S(1)} %copy-done.4, f32[4,8,4096]{2,1,0:T(8,128)} %morph_ref.1, s32[4,8,4096]{2,1,0:T(8,128)} %foot_ref.1), custom_call_target="tpu_custom_call" | custom-call | flops 262144 | bytes 2097152 | tf_op jit(solution)/shard_map/pack/pallas_call | solution.py:263
  44.1 3.8 %collective-permute-done.12.refs_5_ = f32[12,16,128]{2,1,0:T(8,128)S(1)} collective-permute-done((f32[12,16,128]{2,1,0:T(8,128)S(1)}, f32[12,16,128]{2,1,0:T(8,128)S(1)}, u32[]{:S(2)}, u32[]{:S(2)}) %collective-permute-start.12) | collective-permute-done | bytes 98336 | tf_op jit(solution)/shard_map/ppermute | solution.py:499
  47.9 1.5 %collective-permute-start.22 = (f32[2,256,128]{2,1,0:T(8,128)S(1)}, f32[2,256,128]{2,1,0:T(8,128)S(1)}, u32[]{:S(2)}, u32[]{:S(2)}) collective-permute-start(f32[2,256,128]{2,1,0:T(8,128)S(1)} %get-tuple-element.80), channel_id=1, source_target_pairs={{0,8},{8,0},{16,24},{24,16},{1,9},{9,1},{17,25},{25,17},{2,10},{10... | collective-permute-start | bytes 786440 | tf_op jit(solution)/shard_map/ppermute | solution.py:499
  49.4 0.0 collective-permute-done.15.refs_6_
  49.4 0.7 collective-permute-start.23
  50.1 0.0 collective-permute-done.3.got_ref
  50.1 1.3 %collective-permute-start.24 = (f32[2,256,128]{2,1,0:T(8,128)S(1)}, f32[2,256,128]{2,1,0:T(8,128)S(1)}, u32[]{:S(2)}, u32[]{:S(2)}) collective-permute-start(f32[2,256,128]{2,1,0:T(8,128)S(1)} %get-tuple-element.82), channel_id=1, source_target_pairs={{0,24},{8,16},{16,8},{24,0},{1,25},{9,17},{17,9},{25,1},{2,26},{10... | collective-permute-start | bytes 786440 | tf_op jit(solution)/shard_map/ppermute | solution.py:499
  51.5 0.0 collective-permute-done.18.refs_7_
  51.5 1.7 %collective-permute-start.9 = (f32[12,16,128]{2,1,0:T(8,128)S(1)}, f32[12,16,128]{2,1,0:T(8,128)S(1)}, u32[]{:S(2)}, u32[]{:S(2)}) collective-permute-start(f32[12,16,128]{2,1,0:T(8,128)S(1)} %finish.8), channel_id=1, source_target_pairs={{0,4},{1,5},{2,6},{3,7},{4,0},{5,1},{6,2},{7,3},{8,12},{9,13},{10,... | collective-permute-start | bytes 294920 | tf_op jit(solution)/shard_map/ppermute | solution.py:499
  53.2 0.0 collective-permute-done.1.got_ref
  53.2 1.1 %collective-permute-start.4 = (f32[12,16,128]{2,1,0:T(8,128)S(1)}, f32[12,16,128]{2,1,0:T(8,128)S(1)}, u32[]{:S(2)}, u32[]{:S(2)}) collective-permute-start(f32[12,16,128]{2,1,0:T(8,128)S(1)} %get-tuple-element.55), channel_id=1, source_target_pairs={{0,1},{1,0},{2,3},{3,2},{4,5},{5,4},{6,7},{7,6},{8,9},{9,8},{10,11... | collective-permute-start | bytes 294920 | tf_op jit(solution)/shard_map/ppermute | solution.py:499
  54.3 5.3 %collective-permute-done.9.refs_4_ = f32[12,16,128]{2,1,0:T(8,128)S(1)} collective-permute-done((f32[12,16,128]{2,1,0:T(8,128)S(1)}, f32[12,16,128]{2,1,0:T(8,128)S(1)}, u32[]{:S(2)}, u32[]{:S(2)}) %collective-permute-start.9) | collective-permute-done | bytes 98336 | tf_op jit(solution)/shard_map/ppermute | solution.py:499
  59.6 0.0 collective-permute-start.6
  59.6 0.0 collective-permute-done.4.refs_1_
  59.6 0.2 collective-permute-start.5
  59.8 4.3 %collective-permute-done.6.refs_3_ = f32[12,16,128]{2,1,0:T(8,128)S(1)} collective-permute-done((f32[12,16,128]{2,1,0:T(8,128)S(1)}, f32[12,16,128]{2,1,0:T(8,128)S(1)}, u32[]{:S(2)}, u32[]{:S(2)}) %collective-permute-start.6) | collective-permute-done | bytes 98336 | tf_op jit(solution)/shard_map/ppermute | solution.py:499
  64.1 1.2 %collective-permute-done.5.refs_2_ = f32[12,16,128]{2,1,0:T(8,128)S(1)} collective-permute-done((f32[12,16,128]{2,1,0:T(8,128)S(1)}, f32[12,16,128]{2,1,0:T(8,128)S(1)}, u32[]{:S(2)}, u32[]{:S(2)}) %collective-permute-start.5) | collective-permute-done | bytes 98336 | tf_op jit(solution)/shard_map/ppermute | solution.py:499
  65.3 0.1 coadd.1
  65.4 0.8 collective-permute-start.19
  66.3 3.2 %deblend.1 = (f32[8,4224]{1,0:T(8,128)S(1)}, f32[8,4224]{1,0:T(8,128)S(1)}, f32[8,4224]{1,0:T(8,128)S(1)}, f32[8,4224]{1,0:T(8,128)S(1)}) custom-call(s32[4]{0:T(128)S(1)} %copy-done.4, f32[6,128,128]{2,1,0:T(8,128)S(1)} %get-tuple-element.78.cov_ref, f32[6,32,128]{2,1,0:T(8,128)S(1)} %get-tuple-element.74.refs_0_, ...), custom_call_target="tpu_custom_call" | custom-call | flops 12582912 | bytes 1966080 | tf_op jit(solution)/shard_map/deblend/pallas_call | solution.py:421
  69.5 1.3 %collective-permute-start.25 = (f32[8,4224]{1,0:T(8,128)S(1)}, f32[8,4224]{1,0:T(8,128)S(1)}, u32[]{:S(2)}, u32[]{:S(2)}) collective-permute-start(f32[8,4224]{1,0:T(8,128)S(1)} %get-tuple-element.84), channel_id=1, source_target_pairs={{0,8},{8,0},{16,24},{24,16},{1,9},{9,1},{17,25},{25,17},{2,10},{10... | collective-permute-start | bytes 405512 | tf_op jit(solution)/shard_map/ppermute | solution.py:499
  70.8 0.9 %collective-permute-start.26 = (f32[8,4224]{1,0:T(8,128)S(1)}, f32[8,4224]{1,0:T(8,128)S(1)}, u32[]{:S(2)}, u32[]{:S(2)}) collective-permute-start(f32[8,4224]{1,0:T(8,128)S(1)} %get-tuple-element.85), channel_id=1, source_target_pairs={{0,16},{8,24},{16,0},{24,8},{1,17},{9,25},{17,1},{25,9},{2,18},{10... | collective-permute-start | bytes 405512 | tf_op jit(solution)/shard_map/ppermute | solution.py:499
  71.8 1.3 %collective-permute-start.27 = (f32[8,4224]{1,0:T(8,128)S(1)}, f32[8,4224]{1,0:T(8,128)S(1)}, u32[]{:S(2)}, u32[]{:S(2)}) collective-permute-start(f32[8,4224]{1,0:T(8,128)S(1)} %get-tuple-element.86), channel_id=1, source_target_pairs={{0,24},{8,16},{16,8},{24,0},{1,25},{9,17},{17,9},{25,1},{2,26},{10... | collective-permute-start | bytes 405512 | tf_op jit(solution)/shard_map/ppermute | solution.py:499
  73.1 1.4 %collective-permute-start.20 = (f32[6,32,128]{2,1,0:T(8,128)S(1)}, f32[6,32,128]{2,1,0:T(8,128)S(1)}, u32[]{:S(2)}, u32[]{:S(2)}) collective-permute-start(f32[6,32,128]{2,1,0:T(8,128)S(1)} %get-tuple-element.76.refs_2_), channel_id=1, source_target_pairs={{0,16},{8,24},{16,0},{24,8},{1,17},{9,25},{17,1},{25,9},{2,18},{10... | collective-permute-start | bytes 294920 | tf_op jit(solution)/shard_map/ppermute | solution.py:499
  74.5 0.0 collective-permute-done.19.refs_1_
  74.5 1.3 %collective-permute-start.21 = (f32[6,32,128]{2,1,0:T(8,128)S(1)}, f32[6,32,128]{2,1,0:T(8,128)S(1)}, u32[]{:S(2)}, u32[]{:S(2)}) collective-permute-start(f32[6,32,128]{2,1,0:T(8,128)S(1)} %get-tuple-element.77.refs_3_), channel_id=1, source_target_pairs={{0,24},{8,16},{16,8},{24,0},{1,25},{9,17},{17,9},{25,1},{2,26},{10... | collective-permute-start | bytes 294920 | tf_op jit(solution)/shard_map/ppermute | solution.py:499
  75.8 7.4 %collective-permute-done.20.refs_2_ = f32[6,32,128]{2,1,0:T(8,128)S(1)} collective-permute-done((f32[6,32,128]{2,1,0:T(8,128)S(1)}, f32[6,32,128]{2,1,0:T(8,128)S(1)}, u32[]{:S(2)}, u32[]{:S(2)}) %collective-permute-start.20) | collective-permute-done | bytes 98336 | tf_op jit(solution)/shard_map/ppermute | solution.py:499
  83.2 0.0 collective-permute-done.21.refs_3_
  83.2 1.1 %place_coadd.1 = f32[6,4,4096]{2,1,0:T(4,128)} custom-call(f32[6,32,128]{2,1,0:T(8,128)S(1)} %get-tuple-element.74.refs_0_, f32[6,32,128]{2,1,0:T(8,128)S(1)} %collective-permute-done.19.refs_1_, f32[6,32,128]{2,1,0:T(8,128)S(1)} %collective-permute-done.20.refs_2_, f32[6,32,128]{2,1,0:T(8,128)S(1)} %collective-permute-done.21.refs_3_), custom_call_target="tpu_custom_call" | custom-call | flops 98304 | bytes 786432 | tf_op jit(solution)/shard_map/place_coadd/pallas_call | solution.py:455
  84.2 0.8 place_morph.1
  (22 shorter events, 0.3 us)
Async XLA Ops:
  0.6 1.9 %copy-start = (bf16[4,32,6,2048]{3,1,2,0:T(8,128)(2,1)S(1)}, bf16[4,32,6,2048]{3,1,2,0:T(8,128)(2,1)}, u32[]{:S(2)}) copy-start(bf16[4,32,6,2048]{3,1,2,0:T(8,128)(2,1)} %param.7) | copy-start | bytes 9437188
  2.5 1.9 %copy-start.1 = (bf16[4,32,6,2048]{3,1,2,0:T(8,128)(2,1)S(1)}, bf16[4,32,6,2048]{3,1,2,0:T(8,128)(2,1)}, u32[]{:S(2)}) copy-start(bf16[4,32,6,2048]{3,1,2,0:T(8,128)(2,1)} %param.8) | copy-start | bytes 9437188
  4.4 0.7 copy-start.2
  6.6 22.9 %collective-permute-start.2 = (f32[2,2,12,16,128]{4,3,2,1,0:T(8,128)S(1)}, f32[2,2,12,16,128]{4,3,2,1,0:T(8,128)S(1)}, u32[]{:S(2)}, u32[]{:S(2)}) collective-permute-start(f32[2,2,12,16,128]{4,3,2,1,0:T(8,128)S(1)} %get-tuple-element.52), channel_id=1, source_target_pairs={{0,16},{8,24},{16,0},{24,8},{1,17},{9,25},{17,1},{25,9},{2,18},{10... | collective-permute-start | bytes 1179656 | tf_op jit(solution)/shard_map/ppermute | solution.py:499
  10.5 13.4 %collective-permute-start.10 = (f32[2,1,12,16,128]{4,3,2,1,0:T(8,128)S(1)}, f32[2,1,12,16,128]{4,3,2,1,0:T(8,128)S(1)}, u32[]{:S(2)}, u32[]{:S(2)}) collective-permute-start(f32[2,1,12,16,128]{4,3,2,1,0:T(8,128)S(1)} %get-tuple-element.63), channel_id=1, source_target_pairs={{0,16},{8,24},{16,0},{24,8},{1,17},{9,25},{17,1},{25,9},{2,18},{10... | collective-permute-start | bytes 589832 | tf_op jit(solution)/shard_map/ppermute | solution.py:499
  10.6 22.3 %collective-permute-start = (f32[2,2,12,16,128]{4,3,2,1,0:T(8,128)S(1)}, f32[2,2,12,16,128]{4,3,2,1,0:T(8,128)S(1)}, u32[]{:S(2)}, u32[]{:S(2)}) collective-permute-start(f32[2,2,12,16,128]{4,3,2,1,0:T(8,128)S(1)} %get-tuple-element.47), channel_id=1, source_target_pairs={{0,8},{8,0},{16,24},{24,16},{1,9},{9,1},{17,25},{25,17},{2,10},{10... | collective-permute-start | bytes 1179656 | tf_op jit(solution)/shard_map/ppermute | solution.py:499
  14.8 27.1 %copy-start.4 = (s32[4]{0:T(128)S(1)}, s32[4]{0:T(128)}, u32[]{:S(2)}) copy-start(s32[4]{0:T(128)} %count_ref.3) | copy-start | bytes 52
  14.9 11.2 %collective-permute-start.13 = (f32[2,1,12,16,128]{4,3,2,1,0:T(8,128)S(1)}, f32[2,1,12,16,128]{4,3,2,1,0:T(8,128)S(1)}, u32[]{:S(2)}, u32[]{:S(2)}) collective-permute-start(f32[2,1,12,16,128]{4,3,2,1,0:T(8,128)S(1)} %get-tuple-element.67), channel_id=1, source_target_pairs={{0,8},{8,0},{16,24},{24,16},{1,9},{9,1},{17,25},{25,17},{2,10},{10... | collective-permute-start | bytes 589832 | tf_op jit(solution)/shard_map/ppermute | solution.py:499
  15.0 12.9 %collective-permute-start.16 = (f32[2,1,12,16,128]{4,3,2,1,0:T(8,128)S(1)}, f32[2,1,12,16,128]{4,3,2,1,0:T(8,128)S(1)}, u32[]{:S(2)}, u32[]{:S(2)}) collective-permute-start(f32[2,1,12,16,128]{4,3,2,1,0:T(8,128)S(1)} %get-tuple-element.71), channel_id=1, source_target_pairs={{0,16},{8,24},{16,0},{24,8},{1,17},{9,25},{17,1},{25,9},{2,18},{10... | collective-permute-start | bytes 589832 | tf_op jit(solution)/shard_map/ppermute | solution.py:499
  23.9 7.2 %collective-permute-start.7 = (f32[2,1,12,16,128]{4,3,2,1,0:T(8,128)S(1)}, f32[2,1,12,16,128]{4,3,2,1,0:T(8,128)S(1)}, u32[]{:S(2)}, u32[]{:S(2)}) collective-permute-start(f32[2,1,12,16,128]{4,3,2,1,0:T(8,128)S(1)} %get-tuple-element.59), channel_id=1, source_target_pairs={{0,8},{8,0},{16,24},{24,16},{1,9},{9,1},{17,25},{25,17},{2,10},{10... | collective-permute-start | bytes 589832 | tf_op jit(solution)/shard_map/ppermute | solution.py:499
  26.0 9.3 %collective-permute-start.11 = (f32[1,12,16,128]{3,2,1,0:T(8,128)S(1)}, f32[1,12,16,128]{3,2,1,0:T(8,128)S(1)}, u32[]{:S(2)}, u32[]{:S(2)}) collective-permute-start(f32[1,12,16,128]{3,2,1,0:T(8,128)S(1)} %get-tuple-element.65), channel_id=1, source_target_pairs={{0,8},{8,0},{16,24},{24,16},{1,9},{9,1},{17,25},{25,17},{2,10},{10... | collective-permute-start | bytes 294920 | tf_op jit(solution)/shard_map/ppermute | solution.py:499
  27.9 38.4 %copy-start.3 = (f32[4,8,6]{1,0,2:T(4,128)S(1)}, f32[4,8,6]{1,0,2:T(4,128)}, u32[]{:S(2)}) copy-start(f32[4,8,6]{1,0,2:T(4,128)} %param.12) | copy-start | bytes 2308
  27.9 7.9 %collective-permute-start.14 = (f32[1,12,16,128]{3,2,1,0:T(8,128)S(1)}, f32[1,12,16,128]{3,2,1,0:T(8,128)S(1)}, u32[]{:S(2)}, u32[]{:S(2)}) collective-permute-start(f32[1,12,16,128]{3,2,1,0:T(8,128)S(1)} %get-tuple-element.69), channel_id=1, source_target_pairs={{0,16},{8,24},{16,0},{24,8},{1,17},{9,25},{17,1},{25,9},{2,18},{10... | collective-permute-start | bytes 294920 | tf_op jit(solution)/shard_map/ppermute | solution.py:499
  29.5 6.4 %collective-permute-start.17 = (f32[1,12,16,128]{3,2,1,0:T(8,128)S(1)}, f32[1,12,16,128]{3,2,1,0:T(8,128)S(1)}, u32[]{:S(2)}, u32[]{:S(2)}) collective-permute-start(f32[1,12,16,128]{3,2,1,0:T(8,128)S(1)} %get-tuple-element.73), channel_id=1, source_target_pairs={{0,8},{8,0},{16,24},{24,16},{1,9},{9,1},{17,25},{25,17},{2,10},{10... | collective-permute-start | bytes 294920 | tf_op jit(solution)/shard_map/ppermute | solution.py:499
  31.1 19.1 %collective-permute-start.3 = (f32[2,12,16,128]{3,2,1,0:T(8,128)S(1)}, f32[2,12,16,128]{3,2,1,0:T(8,128)S(1)}, u32[]{:S(2)}, u32[]{:S(2)}) collective-permute-start(f32[2,12,16,128]{3,2,1,0:T(8,128)S(1)} %get-tuple-element.54), channel_id=1, source_target_pairs={{0,8},{8,0},{16,24},{24,16},{1,9},{9,1},{17,25},{25,17},{2,10},{10... | collective-permute-start | bytes 589832 | tf_op jit(solution)/shard_map/ppermute | solution.py:499
  32.9 6.7 %collective-permute-start.8 = (f32[1,12,16,128]{3,2,1,0:T(8,128)S(1)}, f32[1,12,16,128]{3,2,1,0:T(8,128)S(1)}, u32[]{:S(2)}, u32[]{:S(2)}) collective-permute-start(f32[1,12,16,128]{3,2,1,0:T(8,128)S(1)} %get-tuple-element.61), channel_id=1, source_target_pairs={{0,16},{8,24},{16,0},{24,8},{1,17},{9,25},{17,1},{25,9},{2,18},{10... | collective-permute-start | bytes 294920 | tf_op jit(solution)/shard_map/ppermute | solution.py:499
  35.3 17.8 %collective-permute-start.1 = (f32[2,12,16,128]{3,2,1,0:T(8,128)S(1)}, f32[2,12,16,128]{3,2,1,0:T(8,128)S(1)}, u32[]{:S(2)}, u32[]{:S(2)}) collective-permute-start(f32[2,12,16,128]{3,2,1,0:T(8,128)S(1)} %get-tuple-element.49), channel_id=1, source_target_pairs={{0,16},{8,24},{16,0},{24,8},{1,17},{9,25},{17,1},{25,9},{2,18},{10... | collective-permute-start | bytes 589832 | tf_op jit(solution)/shard_map/ppermute | solution.py:499
  35.8 12.1 %collective-permute-start.12 = (f32[12,16,128]{2,1,0:T(8,128)S(1)}, f32[12,16,128]{2,1,0:T(8,128)S(1)}, u32[]{:S(2)}, u32[]{:S(2)}) collective-permute-start(f32[12,16,128]{2,1,0:T(8,128)S(1)} %finish.9), channel_id=1, source_target_pairs={{0,5},{1,4},{2,7},{3,6},{4,1},{5,0},{6,3},{7,2},{8,13},{9,12},{10,... | collective-permute-start | bytes 294920 | tf_op jit(solution)/shard_map/ppermute | solution.py:499
  35.9 13.5 %collective-permute-start.15 = (f32[12,16,128]{2,1,0:T(8,128)S(1)}, f32[12,16,128]{2,1,0:T(8,128)S(1)}, u32[]{:S(2)}, u32[]{:S(2)}) collective-permute-start(f32[12,16,128]{2,1,0:T(8,128)S(1)} %finish.10), channel_id=1, source_target_pairs={{0,6},{1,7},{2,4},{3,5},{4,2},{5,3},{6,0},{7,1},{8,14},{9,15},{10,... | collective-permute-start | bytes 294920 | tf_op jit(solution)/shard_map/ppermute | solution.py:499
  39.6 11.9 %collective-permute-start.18 = (f32[12,16,128]{2,1,0:T(8,128)S(1)}, f32[12,16,128]{2,1,0:T(8,128)S(1)}, u32[]{:S(2)}, u32[]{:S(2)}) collective-permute-start(f32[12,16,128]{2,1,0:T(8,128)S(1)} %finish.11), channel_id=1, source_target_pairs={{0,7},{1,6},{2,5},{3,4},{4,3},{5,2},{6,1},{7,0},{8,15},{9,14},{10,... | collective-permute-start | bytes 294920 | tf_op jit(solution)/shard_map/ppermute | solution.py:499
  47.9 18.3 %collective-permute-start.22 = (f32[2,256,128]{2,1,0:T(8,128)S(1)}, f32[2,256,128]{2,1,0:T(8,128)S(1)}, u32[]{:S(2)}, u32[]{:S(2)}) collective-permute-start(f32[2,256,128]{2,1,0:T(8,128)S(1)} %get-tuple-element.80), channel_id=1, source_target_pairs={{0,8},{8,0},{16,24},{24,16},{1,9},{9,1},{17,25},{25,17},{2,10},{10... | collective-permute-start | bytes 786440 | tf_op jit(solution)/shard_map/ppermute | solution.py:499
  49.4 16.8 %collective-permute-start.23 = (f32[2,256,128]{2,1,0:T(8,128)S(1)}, f32[2,256,128]{2,1,0:T(8,128)S(1)}, u32[]{:S(2)}, u32[]{:S(2)}) collective-permute-start(f32[2,256,128]{2,1,0:T(8,128)S(1)} %get-tuple-element.81), channel_id=1, source_target_pairs={{0,16},{8,24},{16,0},{24,8},{1,17},{9,25},{17,1},{25,9},{2,18},{10... | collective-permute-start | bytes 786440 | tf_op jit(solution)/shard_map/ppermute | solution.py:499
  50.1 16.2 %collective-permute-start.24 = (f32[2,256,128]{2,1,0:T(8,128)S(1)}, f32[2,256,128]{2,1,0:T(8,128)S(1)}, u32[]{:S(2)}, u32[]{:S(2)}) collective-permute-start(f32[2,256,128]{2,1,0:T(8,128)S(1)} %get-tuple-element.82), channel_id=1, source_target_pairs={{0,24},{8,16},{16,8},{24,0},{1,25},{9,17},{17,9},{25,1},{2,26},{10... | collective-permute-start | bytes 786440 | tf_op jit(solution)/shard_map/ppermute | solution.py:499
  51.5 8.1 %collective-permute-start.9 = (f32[12,16,128]{2,1,0:T(8,128)S(1)}, f32[12,16,128]{2,1,0:T(8,128)S(1)}, u32[]{:S(2)}, u32[]{:S(2)}) collective-permute-start(f32[12,16,128]{2,1,0:T(8,128)S(1)} %finish.8), channel_id=1, source_target_pairs={{0,4},{1,5},{2,6},{3,7},{4,0},{5,1},{6,2},{7,3},{8,12},{9,13},{10,... | collective-permute-start | bytes 294920 | tf_op jit(solution)/shard_map/ppermute | solution.py:499
  53.2 6.5 %collective-permute-start.4 = (f32[12,16,128]{2,1,0:T(8,128)S(1)}, f32[12,16,128]{2,1,0:T(8,128)S(1)}, u32[]{:S(2)}, u32[]{:S(2)}) collective-permute-start(f32[12,16,128]{2,1,0:T(8,128)S(1)} %get-tuple-element.55), channel_id=1, source_target_pairs={{0,1},{1,0},{2,3},{3,2},{4,5},{5,4},{6,7},{7,6},{8,9},{9,8},{10,11... | collective-permute-start | bytes 294920 | tf_op jit(solution)/shard_map/ppermute | solution.py:499
  59.6 4.5 %collective-permute-start.6 = (f32[12,16,128]{2,1,0:T(8,128)S(1)}, f32[12,16,128]{2,1,0:T(8,128)S(1)}, u32[]{:S(2)}, u32[]{:S(2)}) collective-permute-start(f32[12,16,128]{2,1,0:T(8,128)S(1)} %get-tuple-element.57), channel_id=1, source_target_pairs={{0,3},{1,2},{2,1},{3,0},{4,7},{5,6},{6,5},{7,4},{8,11},{9,10},{10,... | collective-permute-start | bytes 294920 | tf_op jit(solution)/shard_map/ppermute | solution.py:499
  59.6 5.7 %collective-permute-start.5 = (f32[12,16,128]{2,1,0:T(8,128)S(1)}, f32[12,16,128]{2,1,0:T(8,128)S(1)}, u32[]{:S(2)}, u32[]{:S(2)}) collective-permute-start(f32[12,16,128]{2,1,0:T(8,128)S(1)} %get-tuple-element.56), channel_id=1, source_target_pairs={{0,2},{1,3},{2,0},{3,1},{4,6},{5,7},{6,4},{7,5},{8,10},{9,11},{10,... | collective-permute-start | bytes 294920 | tf_op jit(solution)/shard_map/ppermute | solution.py:499
  65.4 9.0 %collective-permute-start.19 = (f32[6,32,128]{2,1,0:T(8,128)S(1)}, f32[6,32,128]{2,1,0:T(8,128)S(1)}, u32[]{:S(2)}, u32[]{:S(2)}) collective-permute-start(f32[6,32,128]{2,1,0:T(8,128)S(1)} %get-tuple-element.75.refs_1_), channel_id=1, source_target_pairs={{0,8},{8,0},{16,24},{24,16},{1,9},{9,1},{17,25},{25,17},{2,10},{10... | collective-permute-start | bytes 294920 | tf_op jit(solution)/shard_map/ppermute | solution.py:499
  69.5 14.7 %collective-permute-start.25 = (f32[8,4224]{1,0:T(8,128)S(1)}, f32[8,4224]{1,0:T(8,128)S(1)}, u32[]{:S(2)}, u32[]{:S(2)}) collective-permute-start(f32[8,4224]{1,0:T(8,128)S(1)} %get-tuple-element.84), channel_id=1, source_target_pairs={{0,8},{8,0},{16,24},{24,16},{1,9},{9,1},{17,25},{25,17},{2,10},{10... | collective-permute-start | bytes 405512 | tf_op jit(solution)/shard_map/ppermute | solution.py:499
  70.8 13.4 %collective-permute-start.26 = (f32[8,4224]{1,0:T(8,128)S(1)}, f32[8,4224]{1,0:T(8,128)S(1)}, u32[]{:S(2)}, u32[]{:S(2)}) collective-permute-start(f32[8,4224]{1,0:T(8,128)S(1)} %get-tuple-element.85), channel_id=1, source_target_pairs={{0,16},{8,24},{16,0},{24,8},{1,17},{9,25},{17,1},{25,9},{2,18},{10... | collective-permute-start | bytes 405512 | tf_op jit(solution)/shard_map/ppermute | solution.py:499
  71.8 12.5 %collective-permute-start.27 = (f32[8,4224]{1,0:T(8,128)S(1)}, f32[8,4224]{1,0:T(8,128)S(1)}, u32[]{:S(2)}, u32[]{:S(2)}) collective-permute-start(f32[8,4224]{1,0:T(8,128)S(1)} %get-tuple-element.86), channel_id=1, source_target_pairs={{0,24},{8,16},{16,8},{24,0},{1,25},{9,17},{17,9},{25,1},{2,26},{10... | collective-permute-start | bytes 405512 | tf_op jit(solution)/shard_map/ppermute | solution.py:499
  73.1 10.1 %collective-permute-start.20 = (f32[6,32,128]{2,1,0:T(8,128)S(1)}, f32[6,32,128]{2,1,0:T(8,128)S(1)}, u32[]{:S(2)}, u32[]{:S(2)}) collective-permute-start(f32[6,32,128]{2,1,0:T(8,128)S(1)} %get-tuple-element.76.refs_2_), channel_id=1, source_target_pairs={{0,16},{8,24},{16,0},{24,8},{1,17},{9,25},{17,1},{25,9},{2,18},{10... | collective-permute-start | bytes 294920 | tf_op jit(solution)/shard_map/ppermute | solution.py:499
  74.5 8.7 %collective-permute-start.21 = (f32[6,32,128]{2,1,0:T(8,128)S(1)}, f32[6,32,128]{2,1,0:T(8,128)S(1)}, u32[]{:S(2)}, u32[]{:S(2)}) collective-permute-start(f32[6,32,128]{2,1,0:T(8,128)S(1)} %get-tuple-element.77.refs_3_), channel_id=1, source_target_pairs={{0,24},{8,16},{16,8},{24,0},{1,25},{9,17},{17,9},{25,1},{2,26},{10... | collective-permute-start | bytes 294920 | tf_op jit(solution)/shard_map/ppermute | solution.py:499
